TPU v7x, 32 devices: a 4x4x1 block of a 4x4x8 slice. The times are simulated.
32 devices in a mesh: batch: 1 (over z), dap: 32 (over y, x, core).
Axes of the slice: x: 4, y: 4, z: 1, core: 2. Of those that a mesh axis runs over, the one named last changes fastest.
The devices are a block of a 4x4x8 slice.
Arguments:
- pair_act: bfloat16 [512, 512, 128], P(('batch', 'dap'))
- pair_mask: int32 [512, 512], P(('batch', 'dap'))
- msa_act: bfloat16 [512, 512, 256], P(None, ('batch', 'dap'))
- opm_norm: bfloat16 [2, 2, 256], replicated
- opm_w_in: bfloat16 [2, 256, 2, 32], replicated
- opm_b_in: bfloat16 [2, 2, 32], replicated
- opm_w_out: bfloat16 [2, 1024, 128], replicated
- opm_b_out: bfloat16 [2, 128], replicated
- tri_norm_in: bfloat16 [2, 2, 128], replicated
- tri_w_ab: bfloat16 [2, 128, 4, 128], replicated
- tri_b_ab: bfloat16 [2, 4, 128], replicated
- tri_w_gate: bfloat16 [2, 128, 128], replicated
- tri_b_gate: bfloat16 [2, 128], replicated
- tri_norm_out: bfloat16 [2, 2, 128], replicated
- tri_w_out: bfloat16 [2, 128, 128], replicated
- tri_b_out: bfloat16 [2, 128], replicated
Outputs:
- output: bfloat16 [512, 512, 128], P(('batch', 'dap'))
All inputs are finite; a program needn't handle non-finite values.
Results may differ from a plain program's by a relative error of at most 0.0110511.
Values are sent between devices in bfloat16 or wider.
A program may use at most 768 MiB of HBM per device.

v0:
```python
import math
import jax
import jax.numpy as jnp
from jax import lax
from jax.sharding import PartitionSpec as P

LN_EPS = 1e-5
ROW_BLOCK = 8


def layer_norm(values, gain_scale, offset, norm_axis):
    x_f32 = values.astype(jnp.float32)
    mean_val = jnp.mean(x_f32, axis=norm_axis, keepdims=True)
    centered = x_f32 - mean_val
    var_val = jnp.mean(centered * centered, axis=norm_axis, keepdims=True)
    return (centered * lax.rsqrt(var_val + LN_EPS) * gain_scale + offset).astype(jnp.bfloat16)


def value_a15(value_a7, norm_w, w_in, b_in):
    normed = layer_norm(value_a7, norm_w[0].astype(jnp.float32), norm_w[1].astype(jnp.float32), -1)
    in_bias = b_in.astype(jnp.float32)
    left_proj = (jnp.einsum('sim,mc->sic', normed, w_in[:, 0, :], preferred_element_type=jnp.float32) + in_bias[0]).astype(jnp.bfloat16)
    right_proj = (jnp.einsum('sim,mc->sic', normed, w_in[:, 1, :], preferred_element_type=jnp.float32) + in_bias[1]).astype(jnp.bfloat16)
    return left_proj, right_proj


def outer_mean_rows(pair_act, left_proj, right_full, w_out, b_out):
    row_count, col_count, pair_dim = pair_act.shape
    value_a9 = left_proj.shape[0]
    opm_dim = left_proj.shape[2]
    row_blk = math.gcd(row_count, ROW_BLOCK)
    num_blocks = row_count // row_blk
    left_blocks = jnp.moveaxis(left_proj.reshape(value_a9, num_blocks, row_blk, opm_dim), 1, 0)
    pair_blocks = pair_act.reshape(num_blocks, row_blk, col_count, pair_dim)
    w_out_r = w_out.reshape(opm_dim, opm_dim, pair_dim)
    out_bias = b_out.astype(jnp.float32)

    def block_update(block_args):
        left_blk, pair_blk = block_args
        outer_prod = jnp.einsum('sic,sjd->icjd', left_blk, right_full, preferred_element_type=jnp.float32)
        outer_prod = (outer_prod / value_a9).astype(jnp.bfloat16)
        pair_upd = (jnp.einsum('icjd,cdz->ijz', outer_prod, w_out_r, preferred_element_type=jnp.float32) + out_bias).astype(jnp.bfloat16)
        return (pair_blk.astype(jnp.float32) + pair_upd.astype(jnp.float32)).astype(jnp.bfloat16)

    return lax.map(block_update, (left_blocks, pair_blocks)).reshape(row_count, col_count, pair_dim)


def gated_projection(normed, mask_f, w_pair, b_pair):
    projected = jnp.einsum('zqc,ikz->qcik', w_pair, normed, preferred_element_type=jnp.float32)
    projected = projected + b_pair.astype(jnp.float32)[:, :, None, None]
    return (mask_f[None] * jax.nn.sigmoid(projected[1]) * projected[0]).astype(jnp.bfloat16)


def triangle_finish(pair_act, normed, tri_prod, w_gate, b_gate, norm_out, w_out, b_out):
    gate_val = jax.nn.sigmoid(jnp.einsum('ikz,zy->iky', normed, w_gate, preferred_element_type=jnp.float32) + b_gate.astype(jnp.float32))
    out_gains = norm_out.astype(jnp.float32)[:, :, None, None]
    prod_norm = layer_norm(tri_prod, out_gains[0], out_gains[1], 0)
    pair_upd = (jnp.einsum('cij,cz->ijz', prod_norm, w_out, preferred_element_type=jnp.float32) + b_out.astype(jnp.float32)).astype(jnp.bfloat16)
    return (pair_act.astype(jnp.float32) + gate_val * pair_upd.astype(jnp.float32)).astype(jnp.bfloat16)


def solution(mesh):
    pair_spec = P(('batch', 'dap'), None, None)
    mask_spec = P(('batch', 'dap'), None)
    array_b8 = P(None, ('batch', 'dap'), None)

    def device_fn(pair_act, pair_mask, value_a7, opm_norm, opm_w_in, opm_b_in, opm_w_out, opm_b_out, tri_norm_in, tri_w_ab, tri_b_ab, tri_w_gate, tri_b_gate, tri_norm_out, tri_w_out, tri_b_out):
        mask_f = pair_mask.astype(jnp.float32)
        for layer_idx in range(opm_norm.shape[0]):
            value_a8, array_b9 = value_a15(value_a7, opm_norm[layer_idx], opm_w_in[layer_idx], opm_b_in[layer_idx])
            value_a14 = lax.all_gather(array_b9, 'dap', axis=1, tiled=True)
            pair_act = outer_mean_rows(pair_act, value_a8, value_a14, opm_w_out[layer_idx], opm_b_out[layer_idx])
            norm_in = tri_norm_in[layer_idx].astype(jnp.float32)
            normed = layer_norm(pair_act, norm_in[0], norm_in[1], -1)
            w_ab = tri_w_ab[layer_idx]
            b_ab = tri_b_ab[layer_idx]
            right_tri = gated_projection(normed, mask_f, w_ab[:, 2:4], b_ab[2:4])
            right_full = lax.all_gather(right_tri, 'dap', axis=1, tiled=True)
            left_tri = gated_projection(normed, mask_f, w_ab[:, 0:2], b_ab[0:2])
            tri_prod = jnp.einsum('cik,cjk->cij', left_tri, right_full, preferred_element_type=jnp.float32)
            pair_act = triangle_finish(pair_act, normed, tri_prod, tri_w_gate[layer_idx], tri_b_gate[layer_idx], tri_norm_out[layer_idx], tri_w_out[layer_idx], tri_b_out[layer_idx])
        return pair_act

    return jax.shard_map(device_fn, mesh=mesh, in_specs=(pair_spec, mask_spec, array_b8) + (P(),) * 13, out_specs=pair_spec, check_vma=False)
```

profile of v0, /device:TPU:103, one launch (start us, length us, event | category | flops | bytes accessed | tf_op | source)
XLA Modules:
  0.0 1109.4 jit_solution(14079893685279587721)
XLA Ops:
  10.1 14.1 %fusion.52 = f32[512,16]{1,0:T(8,128)S(1)} fusion(bf16[512,16,256]{2,1,0:T(8,128)(2,1)S(1)} %copy-done, f32[512,16]{1,0:T(8,128)S(1)} %broadcast_multiply_fusion), kind=kLoop, calls=%fused_computation.44 | loop fusion | flops 8380416 | bytes 4259840 | tf_op jit(solution)/shard_map/reduce_sum | solution.py:15
  24.4 4.8 fusion.114
  33.7 6.2 fusion.110
  43.8 6.2 fusion.116
  59.5 44.4 %all-gather.5.cloned.1.call-done = bf16[512,512,32]{0,2,1:T(8,128)(2,1)} async-done(((bf16[512,16,32]{0,2,1:T(8,128)(2,1)}), bf16[512,512,32]{0,2,1:T(8,128)(2,1)}) %all-gather.5.cloned.1.call-update) | async-done | bytes 16777232 | tf_op jit(solution)/shard_map/all_gather | solution.py:71
  104.0 86.5 %copy.40 = bf16[512,512,32]{2,1,0:T(8,128)(2,1)} copy(bf16[512,512,32]{0,2,1:T(8,128)(2,1)} %all-gather.5.cloned.1.call-done) | data formatting | bytes 33554432 | tf_op jit(solution)/shard_map/while | solution.py:45
  190.9 181.2 %while.20 = (s32[]{:T(128)}, bf16[2,8,512,128]{3,2,1,0:T(8,128)(2,1)S(1)}, bf16[2,8,512,128]{3,2,1,0:T(8,128)(2,1)}, bf16[2,512,8,32]{3,2,1,0:T(8,128)(2,1)}, bf...) while((s32[]{:T(128)}, ...), condition=%wide.region_3.4_spmd, body=%wide.region_2.3_spmd.sunk | while | flops 5380243456 | bytes 95421048 | solution.py:45
  192.4 60.7 %copy.135 = bf16[512,512,32,1]{1,0,2,3:T(8,128)(2,1)} copy(bf16[512,512,32,1]{2,1,0,3:T(8,128)(2,1)} %bitcast.320) | data formatting | bytes 33554432 | tf_op jit(solution)/shard_map
  253.1 11.9 %fusion.156 = f32[8,32,512,32]{2,1,3,0:T(8,128)} fusion(bf16[512,512,32,1]{1,0,2,3:T(8,128)(2,1)} %copy.135, bf16[512,8,32,1]{2,1,0,3:T(8,128)(2,1)S(1)} %dynamic-slice_bitcast_fusion.4), kind=kOutput, calls=%fused_computation.10.clone.1 | convolution fusion | flops 4294967296 | bytes 33816576 | tf_op jit(solution)/shard_map/while/body/eval_jaxpr/sic,sjd->icjd/dot_general | solution.py:40
  265.0 16.4 %fusion.157 = bf16[2,8,512,128]{3,2,1,0:T(8,128)(2,1)S(1)} fusion(bf16[2,8,512,128]{3,2,1,0:T(8,128)(2,1)S(1)} %get-tuple-element.292, s32[]{:T(128)} %get-tuple-element.291, f32[8,32,512,32]{2,1,3,0:T(8,128)} %fusion.156, f32[128]{0:T(128)S(1)} %get-tuple-element.305, bf16[2,8,512,128]{3,2,1,0:T(8,128)(2,1)S(1)} %copy-done.45, ...), kind=kOutput, calls=%fused_computation.9.clone.1 | convolution fusion | flops 1085276160 | bytes 19137028 | tf_op jit(solution)/shard_map/while/body/eval_jaxpr/icjd,cdz->ijz/dot_general | solution.py:42
  282.7 60.7 %copy.135 = bf16[512,512,32,1]{1,0,2,3:T(8,128)(2,1)} copy(bf16[512,512,32,1]{2,1,0,3:T(8,128)(2,1)} %bitcast.320) | data formatting | bytes 33554432 | tf_op jit(solution)/shard_map
  343.4 11.9 %fusion.156 = f32[8,32,512,32]{2,1,3,0:T(8,128)} fusion(bf16[512,512,32,1]{1,0,2,3:T(8,128)(2,1)} %copy.135, bf16[512,8,32,1]{2,1,0,3:T(8,128)(2,1)S(1)} %dynamic-slice_bitcast_fusion.4), kind=kOutput, calls=%fused_computation.10.clone.1 | convolution fusion | flops 4294967296 | bytes 33816576 | tf_op jit(solution)/shard_map/while/body/eval_jaxpr/sic,sjd->icjd/dot_general | solution.py:40
  355.3 16.4 %fusion.157 = bf16[2,8,512,128]{3,2,1,0:T(8,128)(2,1)S(1)} fusion(bf16[2,8,512,128]{3,2,1,0:T(8,128)(2,1)S(1)} %get-tuple-element.292, s32[]{:T(128)} %get-tuple-element.291, f32[8,32,512,32]{2,1,3,0:T(8,128)} %fusion.156, f32[128]{0:T(128)S(1)} %get-tuple-element.305, bf16[2,8,512,128]{3,2,1,0:T(8,128)(2,1)S(1)} %copy-done.45, ...), kind=kOutput, calls=%fused_computation.9.clone.1 | convolution fusion | flops 1085276160 | bytes 19137028 | tf_op jit(solution)/shard_map/while/body/eval_jaxpr/icjd,cdz->ijz/dot_general | solution.py:42
  380.3 3.8 fusion.68
  384.1 4.0 copy.44
  388.2 6.2 fusion.112
  403.3 4.5 copy.45
  407.7 86.5 %copy.51 = bf16[512,512,32]{2,1,0:T(8,128)(2,1)} copy(bf16[512,512,32]{0,2,1:T(8,128)(2,1)} %all-gather.9.cloned.1.call-done) | data formatting | bytes 33554432 | tf_op jit(solution)/shard_map/while | solution.py:45
  497.7 85.8 %all-gather.7.cloned.1.call-done = bf16[128,512,512]{2,0,1:T(8,128)(2,1)} async-done(((bf16[128,16,512]{2,0,1:T(8,128)(2,1)}), bf16[128,512,512]{2,0,1:T(8,128)(2,1)}) %all-gather.7.cloned.1.call-update) | async-done | bytes 67108880 | tf_op jit(solution)/shard_map/all_gather | solution.py:78
  583.5 56.7 %fusion.132 = (f32[16,512]{1,0:T(8,128)S(1)}, f32[128,16,512]{2,1,0:T(8,128)S(1)}) fusion(bf16[128,16,512]{2,1,0:T(8,128)(2,1)} %copy.45, bf16[128,512,512]{2,0,1:T(8,128)(2,1)} %all-gather.7.cloned.1.call-done), kind=kOutput, calls=%fused_computation.204 | convolution fusion | flops 1074782208 | bytes 73433088 | tf_op jit(solution)/shard_map/cik,cjk->cij/dot_general | solution.py:80
  647.4 181.0 %while.21 = (s32[]{:T(128)}, bf16[2,8,512,128]{3,2,1,0:T(8,128)(2,1)S(1)}, bf16[2,8,512,128]{3,2,1,0:T(8,128)(2,1)}, bf16[2,512,8,32]{3,2,1,0:T(8,128)(2,1)}, bf...) while((s32[]{:T(128)}, ...), condition=%wide.region_9.10_spmd, body=%wide.region_8.9_spmd.sunk | while | flops 5380243456 | bytes 95421048 | solution.py:45
  648.7 60.7 %copy.138 = bf16[512,512,32,1]{1,0,2,3:T(8,128)(2,1)} copy(bf16[512,512,32,1]{2,1,0,3:T(8,128)(2,1)} %bitcast.327) | data formatting | bytes 33554432 | tf_op jit(solution)/shard_map
  709.3 11.9 %fusion.162 = f32[8,32,512,32]{2,1,3,0:T(8,128)} fusion(bf16[512,512,32,1]{1,0,2,3:T(8,128)(2,1)} %copy.138, bf16[512,8,32,1]{2,1,0,3:T(8,128)(2,1)S(1)} %dynamic-slice_bitcast_fusion.5), kind=kOutput, calls=%fused_computation.25.clone.1 | convolution fusion | flops 4294967296 | bytes 33816576 | tf_op jit(solution)/shard_map/while/body/eval_jaxpr/sic,sjd->icjd/dot_general | solution.py:40
  721.3 16.4 %fusion.163 = bf16[2,8,512,128]{3,2,1,0:T(8,128)(2,1)S(1)} fusion(bf16[2,8,512,128]{3,2,1,0:T(8,128)(2,1)S(1)} %get-tuple-element.316, s32[]{:T(128)} %get-tuple-element.315, f32[8,32,512,32]{2,1,3,0:T(8,128)} %fusion.162, f32[128]{0:T(128)S(1)} %get-tuple-element.329, bf16[2,8,512,128]{3,2,1,0:T(8,128)(2,1)S(1)} %copy-done.48, ...), kind=kOutput, calls=%fused_computation.24.clone.1 | convolution fusion | flops 1085276160 | bytes 19137028 | tf_op jit(solution)/shard_map/while/body/eval_jaxpr/icjd,cdz->ijz/dot_general | solution.py:42
  739.0 60.7 %copy.138 = bf16[512,512,32,1]{1,0,2,3:T(8,128)(2,1)} copy(bf16[512,512,32,1]{2,1,0,3:T(8,128)(2,1)} %bitcast.327) | data formatting | bytes 33554432 | tf_op jit(solution)/shard_map
  799.7 11.9 %fusion.162 = f32[8,32,512,32]{2,1,3,0:T(8,128)} fusion(bf16[512,512,32,1]{1,0,2,3:T(8,128)(2,1)} %copy.138, bf16[512,8,32,1]{2,1,0,3:T(8,128)(2,1)S(1)} %dynamic-slice_bitcast_fusion.5), kind=kOutput, calls=%fused_computation.25.clone.1 | convolution fusion | flops 4294967296 | bytes 33816576 | tf_op jit(solution)/shard_map/while/body/eval_jaxpr/sic,sjd->icjd/dot_general | solution.py:40
  811.6 16.4 %fusion.163 = bf16[2,8,512,128]{3,2,1,0:T(8,128)(2,1)S(1)} fusion(bf16[2,8,512,128]{3,2,1,0:T(8,128)(2,1)S(1)} %get-tuple-element.316, s32[]{:T(128)} %get-tuple-element.315, f32[8,32,512,32]{2,1,3,0:T(8,128)} %fusion.162, f32[128]{0:T(128)S(1)} %get-tuple-element.329, bf16[2,8,512,128]{3,2,1,0:T(8,128)(2,1)S(1)} %copy-done.48, ...), kind=kOutput, calls=%fused_computation.24.clone.1 | convolution fusion | flops 1085276160 | bytes 19137028 | tf_op jit(solution)/shard_map/while/body/eval_jaxpr/icjd,cdz->ijz/dot_general | solution.py:42
  836.6 3.8 fusion.54
  840.4 3.9 copy.55
  844.4 4.5 copy.56
  852.3 187.0 %all-gather.11.cloned.1.call-done = bf16[128,512,512]{2,0,1:T(8,128)(2,1)} async-done(((bf16[128,16,512]{2,0,1:T(8,128)(2,1)}), bf16[128,512,512]{2,0,1:T(8,128)(2,1)}) %all-gather.11.cloned.1.call-update) | async-done | bytes 67108880 | tf_op jit(solution)/shard_map/all_gather | solution.py:78
  1039.3 56.7 %fusion.133 = (f32[16,512]{1,0:T(8,128)S(1)}, f32[128,16,512]{2,1,0:T(8,128)S(1)}) fusion(bf16[128,16,512]{2,1,0:T(8,128)(2,1)} %copy.56, bf16[128,512,512]{2,0,1:T(8,128)(2,1)} %all-gather.11.cloned.1.call-done), kind=kOutput, calls=%fused_computation.205 | convolution fusion | flops 1074782208 | bytes 73433088 | tf_op jit(solution)/shard_map/cik,cjk->cij/dot_general | solution.py:80
  (175 shorter events, 72.6 us)
Async XLA Ops:
  6.5 17.7 %copy-start.23 = (bf16[2,2,256]{2,1,0:T(2,128)(2,1)S(1)}, bf16[2,2,256]{2,1,0:T(2,128)(2,1)}, u32[]{:S(2)}) copy-start(bf16[2,2,256]{2,1,0:T(2,128)(2,1)} %param.23) | copy-start | bytes 6148
  6.5 17.8 %copy-start.16 = (bf16[2,256,2,32]{1,3,2,0:T(8,128)(2,1)S(1)}, bf16[2,256,2,32]{1,3,2,0:T(8,128)(2,1)}, u32[]{:S(2)}) copy-start(bf16[2,256,2,32]{1,3,2,0:T(8,128)(2,1)} %param.24) | copy-start | bytes 196612
  6.6 97.4 %all-gather.5.cloned.1.call-start = ((), (), s32[]{:S(2)}) async-start(), calls=%async_computation | async-start | bytes 17301504 | tf_op jit(solution)/shard_map/all_gather | solution.py:71
  10.1 33.7 %copy-start.3 = (f32[512,16]{1,0:T(8,128)}, f32[512,16]{1,0:T(8,128)S(1)}, u32[]{:S(2)}) copy-start(f32[512,16]{1,0:T(8,128)S(1)} %broadcast_multiply_fusion) | copy-start | bytes 98308
  24.3 19.5 %copy-start.11 = (f32[512,16]{1,0:T(8,128)}, f32[512,16]{1,0:T(8,128)S(1)}, u32[]{:S(2)}) copy-start(f32[512,16]{1,0:T(8,128)S(1)} %add_rsqrt_fusion) | copy-start | bytes 98308
  24.3 9.3 copy-start.39
  24.4 9.3 copy-start.41
  24.4 9.3 copy-start.18
  33.6 374.2 %all-gather.9.cloned.1.call-start = ((), (), s32[]{:S(2)}) async-start(), calls=%async_computation.2 | async-start | bytes 17301504 | tf_op jit(solution)/shard_map/all_gather | solution.py:71
  43.7 539.8 %all-gather.7.cloned.1.call-start = ((), (), s32[]{:S(2)}) async-start(), calls=%async_computation.1 | async-start | bytes 69206016 | tf_op jit(solution)/shard_map/all_gather | solution.py:78
  50.0 5.6 copy-start.17
  50.0 6.2 copy-start.33
  50.0 6.8 copy-start.37
  50.0 7.4 copy-start.32
  50.0 8.0 copy-start.10
  50.0 8.8 copy-start.7
  253.0 11.9 %copy-start.45 = (bf16[2,8,512,128]{3,2,1,0:T(8,128)(2,1)S(1)}, bf16[2,8,512,128]{3,2,1,0:T(8,128)(2,1)}, u32[]{:S(2)}) copy-start(bf16[2,8,512,128]{3,2,1,0:T(8,128)(2,1)} %get-tuple-element.301) | copy-start | bytes 6291460 | tf_op jit(solution)/shard_map/while
  343.4 11.9 %copy-start.45 = (bf16[2,8,512,128]{3,2,1,0:T(8,128)(2,1)S(1)}, bf16[2,8,512,128]{3,2,1,0:T(8,128)(2,1)}, u32[]{:S(2)}) copy-start(bf16[2,8,512,128]{3,2,1,0:T(8,128)(2,1)} %get-tuple-element.301) | copy-start | bytes 6291460 | tf_op jit(solution)/shard_map/while
  372.2 5.6 copy-start.6
  372.2 5.6 copy-start.29
  384.1 4.1 copy-start.12
  384.1 4.2 copy-start.19
  384.1 4.2 copy-start.40
  384.1 4.2 copy-start.42
  388.1 651.2 %all-gather.11.cloned.1.call-start = ((), (), s32[]{:S(2)}) async-start(), calls=%async_computation.3 | async-start | bytes 69206016 | tf_op jit(solution)/shard_map/all_gather | solution.py:78
  394.4 7.2 copy-start.34
  394.4 7.7 copy-start.35
  394.4 8.2 copy-start.38
  709.3 11.9 %copy-start.48 = (bf16[2,8,512,128]{3,2,1,0:T(8,128)(2,1)S(1)}, bf16[2,8,512,128]{3,2,1,0:T(8,128)(2,1)}, u32[]{:S(2)}) copy-start(bf16[2,8,512,128]{3,2,1,0:T(8,128)(2,1)} %get-tuple-element.325) | copy-start | bytes 6291460 | tf_op jit(solution)/shard_map/while
  799.7 11.9 %copy-start.48 = (bf16[2,8,512,128]{3,2,1,0:T(8,128)(2,1)S(1)}, bf16[2,8,512,128]{3,2,1,0:T(8,128)(2,1)}, u32[]{:S(2)}) copy-start(bf16[2,8,512,128]{3,2,1,0:T(8,128)(2,1)} %get-tuple-element.325) | copy-start | bytes 6291460 | tf_op jit(solution)/shard_map/while
  828.4 5.6 copy-start.5
  828.5 5.6 copy-start.21
  (23 other events, 60.2 us)
Sparse Core Ops, SparseCore 0:
  33.7 70.2 all-gather.4
  106.1 66.6 all-gather.8
  388.2 195.2 all-gather.6
  844.5 194.8 all-gather.10
where the time goes:
time: 1130 us; the launch traced here: 1110 us
  local copies, waits for them, and re-layouts  459 us (41%)
  waiting for transfers between devices  317 us (28%)
  matrix products  266 us (24%)
  other arithmetic  52.1 us (5%)
  between operations  14.1 us (1%)
    all_gather x2, waiting for transfers between devices, device_fn(): right_full = lax.all_gather(right_tri, 'dap', axis=1, tiled=True)  273 us
    another operation x6, local copies, waits for them, and re-layouts  243 us
    while x2, local copies, waits for them, and re-layouts, outer_mean_rows(): lax.map(block_update, (left_blocks, pair_blocks))  173 us
    dot_general x2, matrix products, device_fn(): jnp.einsum('cik,cjk->cij', left_tri, right_full, preferred_element_type=j...  113 us
    dot_general x4, matrix products, block_update(): jnp.einsum('icjd,cdz->ijz', outer_prod, w_out_r, preferred_element_type=j...  65.7 us
    dot_general x4, matrix products, block_update(): jnp.einsum('sic,sjd->icjd', left_blk, right_full, preferred_element_type=...  47.7 us
    all_gather x2, waiting for transfers between devices, device_fn(): value_a14 = lax.all_gather(array_b9, 'dap', axis=1, tiled=True)  44.5 us
  transfers between devices with their start and end apart: 4, of which 3 were waited for; matrix products, arithmetic and copies ran while one was open for 38% of the time, Pallas kernels for 0%

commit v1 on v0

--- a/solution.py
+++ b/solution.py
@@ -75,9 +75,11 @@
             w_ab = tri_w_ab[layer_idx]
             b_ab = tri_b_ab[layer_idx]
             right_tri = gated_projection(normed, mask_f, w_ab[:, 2:4], b_ab[2:4])
-            right_full = lax.all_gather(right_tri, 'dap', axis=1, tiled=True)
+            right_ch = lax.all_to_all(right_tri, 'dap', 0, 1, tiled=True)
             left_tri = gated_projection(normed, mask_f, w_ab[:, 0:2], b_ab[0:2])
-            tri_prod = jnp.einsum('cik,cjk->cij', left_tri, right_full, preferred_element_type=jnp.float32)
+            left_ch = lax.all_to_all(left_tri, 'dap', 0, 1, tiled=True)
+            tri_ch = jnp.einsum('cik,cjk->cij', left_ch, right_ch, preferred_element_type=jnp.float32)
+            tri_prod = lax.all_to_all(tri_ch, 'dap', 1, 0, tiled=True)
             pair_act = triangle_finish(pair_act, normed, tri_prod, tri_w_gate[layer_idx], tri_b_gate[layer_idx], tri_norm_out[layer_idx], tri_w_out[layer_idx], tri_b_out[layer_idx])
         return pair_act
 

time: 1130 us -> 570 us (0.50); the launches traced: 1110 us -> 563 us
  local copies, waits for them, and re-layouts: 459 us -> 117 us
  matrix products: 266 us -> 116 us
  waiting for transfers between devices: 317 us -> 217 us
  starting transfers between devices: 0.2 us -> 31.8 us
  other arithmetic: 52.1 us -> 65.9 us
    all_gather x2 -> x0, waiting for transfers between devices: 273 us -> none  [device_fn(): right_full = lax.all_gather(right_tri, 'dap', axis=1, tiled=True)]
    another operation x6 -> x2, local copies, waits for them, and re-layouts: 243 us -> 0.79 us
    all_to_all x0 -> x6, waiting for transfers between devices: none -> 167 us  [the longest x2 70.2 us: device_fn(): tri_prod = lax.all_to_all(tri_ch, 'dap', 1, 0, tiled=True)]
    while x2 -> x4, local copies, waits for them, and re-layouts: 173 us -> 52.8 us  [outer_mean_rows(): lax.map(block_update, (left_blocks, pair_blocks))]
    dot_general x2, matrix products: 113 us -> 2.56 us  [device_fn(): jnp.einsum('cik,cjk->cij', left_ch, right_ch, preferred_element_type=jnp....]
    dot_general x4, matrix products: 65.7 us -> 24.7 us  [block_update(): jnp.einsum('icjd,cdz->ijz', outer_prod, w_out_r, preferred_element_type=j...]
    all_to_all x0 -> x6, starting transfers between devices: none -> 31.5 us  [the longest x2 13 us: device_fn(): tri_prod = lax.all_to_all(tri_ch, 'dap', 1, 0, tiled=True)]
    all_to_all x0 -> x6, local copies, waits for them, and re-layouts: none -> 21.2 us  [the longest x2 11.1 us: device_fn(): tri_prod = lax.all_to_all(tri_ch, 'dap', 1, 0, tiled=True)]
  transfers between devices with their start and end apart: 4 -> 8, of which waited for: 3 -> 7; matrix products, arithmetic and copies ran while one was open for 38% -> 30% of each run, Pallas kernels for 0% -> 0%
where the time goes in v1:
time: 570 us; the launch traced here: 563 us
  waiting for transfers between devices  217 us (38%)
  local copies, waits for them, and re-layouts  117 us (21%)
  matrix products  116 us (20%)
  other arithmetic  65.9 us (12%)
  starting transfers between devices  31.8 us (6%)
  between operations  14.8 us (3%)
    all_to_all x2, waiting for transfers between devices, device_fn(): tri_prod = lax.all_to_all(tri_ch, 'dap', 1, 0, tiled=True)  70.2 us
    while x4, local copies, waits for them, and re-layouts, outer_mean_rows(): lax.map(block_update, (left_blocks, pair_blocks))  52.8 us
    dot_general x4, matrix products, block_update(): jnp.einsum('sic,sjd->icjd', left_blk, right_full, preferred_element_type=...  51.4 us
    all_gather x2, waiting for transfers between devices, device_fn(): value_a14 = lax.all_gather(array_b9, 'dap', axis=1, tiled=True)  49.7 us
    all_to_all x2, waiting for transfers between devices, device_fn(): right_ch = lax.all_to_all(right_tri, 'dap', 0, 1, tiled=True)  49.2 us
    all_to_all x2, waiting for transfers between devices, device_fn(): left_ch = lax.all_to_all(left_tri, 'dap', 0, 1, tiled=True)  47.9 us
    dot_general x4, matrix products, block_update(): jnp.einsum('icjd,cdz->ijz', outer_prod, w_out_r, preferred_element_type=j...  24.7 us
    reduce_sum x5, other arithmetic, layer_norm(): var_val = jnp.mean(centered * centered, axis=norm_axis, keepdims=True)  24.2 us
  transfers between devices with their start and end apart: 8, of which 7 were waited for; matrix products, arithmetic and copies ran while one was open for 30% of the time, Pallas kernels for 0%

profile of v1, /device:TPU:103, one launch (start us, length us, event | category | flops | bytes accessed | tf_op | source)
XLA Modules:
  0.0 563.0 jit_solution(8327565916677630773)
XLA Ops:
  10.1 14.1 %fusion.32 = f32[512,16]{1,0:T(8,128)S(1)} fusion(bf16[512,16,256]{2,1,0:T(8,128)(2,1)S(1)} %copy-done, f32[512,16]{1,0:T(8,128)S(1)} %broadcast_multiply_fusion), kind=kLoop, calls=%fused_computation.36 | loop fusion | flops 8380416 | bytes 4259840 | tf_op jit(solution)/shard_map/reduce_sum | solution.py:15
  24.4 4.9 fusion.93
  34.0 6.2 %fusion.90 = f32[512,16,32]{2,1,0:T(8,128)} fusion(bf16[512,16,256]{2,1,0:T(8,128)(2,1)} %param.22, f32[256]{0:T(256)S(1)} %bitcast.382, f32[256]{0:T(256)S(1)} %bitcast.380, f32[512,16]{1,0:T(8,128)S(1)} %add_rsqrt_fusion, f32[512,16]{1,0:T(8,128)S(1)} %broadcast_multiply_fusion, bf16[256,2,32]{0,2,1:T(8,128)(2,1)S(1)} %get-tuple-element.201), kind=kOutput, calls=%fused_computation.122 | convolution fusion | flops 146800640 | bytes 5785600 | tf_op jit(solution)/shard_map/sim,mc->sic/dot_general | solution.py:23
  44.1 4.6 fusion.96
  54.4 49.7 %all-gather.3.cloned.1.call-done = bf16[512,512,32]{0,2,1:T(8,128)(2,1)} async-done(((bf16[512,16,32]{0,2,1:T(8,128)(2,1)}), bf16[512,512,32]{0,2,1:T(8,128)(2,1)}) %all-gather.3.cloned.1.call-update) | async-done | bytes 16777232 | tf_op jit(solution)/shard_map/all_gather | solution.py:71
  104.1 26.2 %copy.161 = bf16[512,512,32]{1,0,2:T(8,128)(2,1)} copy(bf16[512,512,32]{0,2,1:T(8,128)(2,1)} %all-gather.3.cloned.1.call-done) | data formatting | bytes 33554432 | tf_op jit(solution)/shard_map/while | solution.py:45
  130.7 38.1 %while.20 = (s32[]{:T(128)}, bf16[2,8,512,128]{3,2,1,0:T(8,128)(2,1)S(1)}, bf16[2,8,512,128]{3,2,1,0:T(8,128)(2,1)}, bf16[2,512,8,32]{1,3,2,0:T(8,128)(2,1)S(1)}...) while((s32[]{:T(128)}, ...), condition=%wide.region_3.4_spmd, body=%wide.region_2.3_spmd.sunk | while | flops 5380243456 | bytes 44565112 | solution.py:45
  130.7 12.9 %multiply_convert_fusion.4 = bf16[8,32,512,32]{2,1,3,0:T(8,128)(2,1)} fusion(bf16[512,512,32]{1,0,2:T(8,128)(2,1)} %get-tuple-element.357, bf16[2,512,8,32]{1,3,2,0:T(8,128)(2,1)S(1)} %get-tuple-element.356, s32[]{:T(128)} %get-tuple-element.345), kind=kOutput, calls=%fused_computation.2.clone.1 | convolution fusion | flops 4303355904 | bytes 25427972 | tf_op jit(solution)/shard_map/while/body/eval_jaxpr/sic,sjd->icjd/dot_general | solution.py:40
  143.6 6.2 %fusion.140 = bf16[2,8,512,128]{3,2,1,0:T(8,128)(2,1)S(1)} fusion(bf16[2,8,512,128]{3,2,1,0:T(8,128)(2,1)S(1)} %get-tuple-element.346, s32[]{:T(128)} %get-tuple-element.345, bf16[8,32,512,32]{2,1,3,0:T(8,128)(2,1)} %multiply_convert_fusion.4, f32[128]{0:T(128)S(1)} %get-tuple-element.359, bf16[2,8,512,128]{3,2,1,0:T(8,128)(2,1)S(1)} %copy-done.44, ...), kind=kOutput, calls=%fused_computation.8.clone.1 | convolution fusion | flops 1076887552 | bytes 10748420 | tf_op jit(solution)/shard_map/while/body/eval_jaxpr/icjd,cdz->ijz/dot_general | solution.py:42
  149.8 12.9 %multiply_convert_fusion.4 = bf16[8,32,512,32]{2,1,3,0:T(8,128)(2,1)} fusion(bf16[512,512,32]{1,0,2:T(8,128)(2,1)} %get-tuple-element.357, bf16[2,512,8,32]{1,3,2,0:T(8,128)(2,1)S(1)} %get-tuple-element.356, s32[]{:T(128)} %get-tuple-element.345), kind=kOutput, calls=%fused_computation.2.clone.1 | convolution fusion | flops 4303355904 | bytes 25427972 | tf_op jit(solution)/shard_map/while/body/eval_jaxpr/sic,sjd->icjd/dot_general | solution.py:40
  162.6 6.2 %fusion.140 = bf16[2,8,512,128]{3,2,1,0:T(8,128)(2,1)S(1)} fusion(bf16[2,8,512,128]{3,2,1,0:T(8,128)(2,1)S(1)} %get-tuple-element.346, s32[]{:T(128)} %get-tuple-element.345, bf16[8,32,512,32]{2,1,3,0:T(8,128)(2,1)} %multiply_convert_fusion.4, f32[128]{0:T(128)S(1)} %get-tuple-element.359, bf16[2,8,512,128]{3,2,1,0:T(8,128)(2,1)S(1)} %copy-done.44, ...), kind=kOutput, calls=%fused_computation.8.clone.1 | convolution fusion | flops 1076887552 | bytes 10748420 | tf_op jit(solution)/shard_map/while/body/eval_jaxpr/icjd,cdz->ijz/dot_general | solution.py:42
  194.7 24.1 %all-to-all-done = bf16[128,16,512]{2,1,0:T(8,128)(2,1)} async-done(((bf16[128,16,512]{2,1,0:T(8,128)(2,1)}), bf16[128,16,512]{2,1,0:T(8,128)(2,1)}, u32[]{:S(2)}, u32[]{:S(2)}) %all-to-all-start) | async-done | bytes 2097184 | tf_op jit(solution)/shard_map/all_to_all | solution.py:80
  218.9 4.9 all-to-all-start.1
  226.9 24.2 %all-to-all-done.1 = bf16[128,16,512]{2,1,0:T(8,128)(2,1)} async-done(((bf16[128,16,512]{2,1,0:T(8,128)(2,1)}), bf16[128,16,512]{2,1,0:T(8,128)(2,1)}, u32[]{:S(2)}, u32[]{:S(2)}) %all-to-all-start.1) | async-done | bytes 2097184 | tf_op jit(solution)/shard_map/all_to_all | solution.py:78
  254.6 4.7 copy.170
  259.3 7.4 %all-to-all-start.2 = ((f32[4,512,512]{2,0,1:T(4,128)}), f32[4,512,512]{2,0,1:T(4,128)}, u32[]{:S(2)}, u32[]{:S(2)}) async-start(f32[4,512,512]{2,0,1:T(4,128)} %copy.170), calls=%async_computation.2 | async-start | bytes 8388608 | tf_op jit(solution)/shard_map/all_to_all | solution.py:82
  267.7 5.7 %fusion.99 = bf16[512,2,8,32]{3,2,1,0:T(8,128)(2,1)} fusion(f32[32]{0:T(128)S(1)} %copy-done.43, bf16[512,16,256]{2,1,0:T(8,128)(2,1)} %param.22, f32[256]{0:T(256)S(1)} %bitcast.383, f32[256]{0:T(256)S(1)} %bitcast.381, f32[512,16]{1,0:T(8,128)S(1)} %copy-done.14, f32[512,16]{1,0:T(8,128)S(1)} %copy-done.6, bf16[256,2,32]{0,2,1:T(8,128)(2,1)S(1)} %copy-done.20), kind=kOutput, calls=%fused_computation.125 | convolution fusion | flops 147324928 | bytes 5261824 | tf_op jit(solution)/shard_map/sim,mc->sic/dot_general | solution.py:22
  277.2 26.3 %copy.178 = bf16[512,512,32]{1,0,2:T(8,128)(2,1)} copy(bf16[512,512,32]{0,2,1:T(8,128)(2,1)} %all-gather.5.cloned.1.call-done) | data formatting | bytes 33554432 | tf_op jit(solution)/shard_map/while | solution.py:45
  307.0 16.6 %all-to-all-done.2 = f32[4,512,512]{2,0,1:T(4,128)} async-done(((f32[4,512,512]{2,0,1:T(4,128)}), f32[4,512,512]{2,0,1:T(4,128)}, u32[]{:S(2)}, u32[]{:S(2)}) %all-to-all-start.2) | async-done | bytes 4194336 | tf_op jit(solution)/shard_map/all_to_all | solution.py:82
  323.6 5.5 copy.171
  343.9 38.3 %while.21 = (s32[]{:T(128)}, bf16[2,8,512,128]{3,2,1,0:T(8,128)(2,1)S(1)}, bf16[2,8,512,128]{3,2,1,0:T(8,128)(2,1)}, bf16[2,512,8,32]{1,3,2,0:T(8,128)(2,1)S(1)}...) while((s32[]{:T(128)}, ...), condition=%wide.region_9.10_spmd, body=%wide.region_8.9_spmd.sunk | while | flops 5380243456 | bytes 44565112 | solution.py:45
  344.1 12.9 %multiply_convert_fusion.5 = bf16[8,32,512,32]{2,1,3,0:T(8,128)(2,1)} fusion(bf16[512,512,32]{1,0,2:T(8,128)(2,1)} %get-tuple-element.381, bf16[2,512,8,32]{1,3,2,0:T(8,128)(2,1)S(1)} %get-tuple-element.380, s32[]{:T(128)} %get-tuple-element.369), kind=kOutput, calls=%fused_computation.15.clone.1 | convolution fusion | flops 4303355904 | bytes 25427972 | tf_op jit(solution)/shard_map/while/body/eval_jaxpr/sic,sjd->icjd/dot_general | solution.py:40
  357.0 6.2 %fusion.145 = bf16[2,8,512,128]{3,2,1,0:T(8,128)(2,1)S(1)} fusion(bf16[2,8,512,128]{3,2,1,0:T(8,128)(2,1)S(1)} %get-tuple-element.370, s32[]{:T(128)} %get-tuple-element.369, bf16[8,32,512,32]{2,1,3,0:T(8,128)(2,1)} %multiply_convert_fusion.5, f32[128]{0:T(128)S(1)} %get-tuple-element.383, bf16[2,8,512,128]{3,2,1,0:T(8,128)(2,1)S(1)} %copy-done.47, ...), kind=kOutput, calls=%fused_computation.21.clone.1 | convolution fusion | flops 1076887552 | bytes 10748420 | tf_op jit(solution)/shard_map/while/body/eval_jaxpr/icjd,cdz->ijz/dot_general | solution.py:42
  363.2 12.8 %multiply_convert_fusion.5 = bf16[8,32,512,32]{2,1,3,0:T(8,128)(2,1)} fusion(bf16[512,512,32]{1,0,2:T(8,128)(2,1)} %get-tuple-element.381, bf16[2,512,8,32]{1,3,2,0:T(8,128)(2,1)S(1)} %get-tuple-element.380, s32[]{:T(128)} %get-tuple-element.369), kind=kOutput, calls=%fused_computation.15.clone.1 | convolution fusion | flops 4303355904 | bytes 25427972 | tf_op jit(solution)/shard_map/while/body/eval_jaxpr/sic,sjd->icjd/dot_general | solution.py:40
  376.0 6.2 %fusion.145 = bf16[2,8,512,128]{3,2,1,0:T(8,128)(2,1)S(1)} fusion(bf16[2,8,512,128]{3,2,1,0:T(8,128)(2,1)S(1)} %get-tuple-element.370, s32[]{:T(128)} %get-tuple-element.369, bf16[8,32,512,32]{2,1,3,0:T(8,128)(2,1)} %multiply_convert_fusion.5, f32[128]{0:T(128)S(1)} %get-tuple-element.383, bf16[2,8,512,128]{3,2,1,0:T(8,128)(2,1)S(1)} %copy-done.47, ...), kind=kOutput, calls=%fused_computation.21.clone.1 | convolution fusion | flops 1076887552 | bytes 10748420 | tf_op jit(solution)/shard_map/while/body/eval_jaxpr/icjd,cdz->ijz/dot_general | solution.py:42
  407.0 23.8 %all-to-all-done.3 = bf16[128,16,512]{2,1,0:T(8,128)(2,1)} async-done(((bf16[128,16,512]{2,1,0:T(8,128)(2,1)}), bf16[128,16,512]{2,1,0:T(8,128)(2,1)}, u32[]{:S(2)}, u32[]{:S(2)}) %all-to-all-start.3) | async-done | bytes 2097184 | tf_op jit(solution)/shard_map/all_to_all | solution.py:80
  430.8 5.5 all-to-all-start.4
  439.5 25.0 %all-to-all-done.4 = bf16[128,16,512]{2,1,0:T(8,128)(2,1)} async-done(((bf16[128,16,512]{2,1,0:T(8,128)(2,1)}), bf16[128,16,512]{2,1,0:T(8,128)(2,1)}, u32[]{:S(2)}, u32[]{:S(2)}) %all-to-all-start.4) | async-done | bytes 2097184 | tf_op jit(solution)/shard_map/all_to_all | solution.py:78
  468.0 4.7 copy.187
  472.7 5.6 all-to-all-start.5
  482.2 53.6 %all-to-all-done.5 = f32[4,512,512]{2,0,1:T(4,128)} async-done(((f32[4,512,512]{2,0,1:T(4,128)}), f32[4,512,512]{2,0,1:T(4,128)}, u32[]{:S(2)}, u32[]{:S(2)}) %all-to-all-start.5) | async-done | bytes 4194336 | tf_op jit(solution)/shard_map/all_to_all | solution.py:82
  535.7 5.6 copy.188
  (188 shorter events, 122.8 us)
Async XLA Ops:
  6.5 17.7 %copy-start.24 = (bf16[2,2,256]{2,1,0:T(2,128)(2,1)S(1)}, bf16[2,2,256]{2,1,0:T(2,128)(2,1)}, u32[]{:S(2)}) copy-start(bf16[2,2,256]{2,1,0:T(2,128)(2,1)} %param.23) | copy-start | bytes 6148
  6.5 17.8 %copy-start.17 = (bf16[2,256,2,32]{1,3,2,0:T(8,128)(2,1)S(1)}, bf16[2,256,2,32]{1,3,2,0:T(8,128)(2,1)}, u32[]{:S(2)}) copy-start(bf16[2,256,2,32]{1,3,2,0:T(8,128)(2,1)} %param.24) | copy-start | bytes 196612
  6.6 97.5 %all-gather.3.cloned.1.call-start = ((), (), s32[]{:S(2)}) async-start(), calls=%async_computation.6 | async-start | bytes 17301504 | tf_op jit(solution)/shard_map/all_gather | solution.py:71
  10.1 34.0 %copy-start.5 = (f32[512,16]{1,0:T(8,128)}, f32[512,16]{1,0:T(8,128)S(1)}, u32[]{:S(2)}) copy-start(f32[512,16]{1,0:T(8,128)S(1)} %broadcast_multiply_fusion) | copy-start | bytes 98308
  24.3 19.8 %copy-start.13 = (f32[512,16]{1,0:T(8,128)}, f32[512,16]{1,0:T(8,128)S(1)}, u32[]{:S(2)}) copy-start(f32[512,16]{1,0:T(8,128)S(1)} %add_rsqrt_fusion) | copy-start | bytes 98308
  24.3 9.7 %copy-start.37 = (f32[1,1,256]{2,1,0:T(1,128)}, f32[1,1,256]{2,1,0:T(1,128)S(1)}, u32[]{:S(2)}) copy-start(f32[1,1,256]{2,1,0:T(1,128)S(1)} %get-tuple-element.219) | copy-start | bytes 3076
  24.4 9.7 %copy-start.39 = (f32[1,1,256]{2,1,0:T(1,128)}, f32[1,1,256]{2,1,0:T(1,128)S(1)}, u32[]{:S(2)}) copy-start(f32[1,1,256]{2,1,0:T(1,128)S(1)} %get-tuple-element.222) | copy-start | bytes 3076
  24.4 9.6 %copy-start.19 = (bf16[256,2,32]{0,2,1:T(8,128)(2,1)}, bf16[256,2,32]{0,2,1:T(8,128)(2,1)S(1)}, u32[]{:S(2)}) copy-start(bf16[256,2,32]{0,2,1:T(8,128)(2,1)S(1)} %get-tuple-element.201) | copy-start | bytes 98308
  33.7 243.5 %all-gather.5.cloned.1.call-start = ((), (), s32[]{:S(2)}) async-start(), calls=%async_computation.7 | async-start | bytes 17301504 | tf_op jit(solution)/shard_map/all_gather | solution.py:71
  44.1 6.3 %copy-start.9 = (bf16[2,1024,128]{2,1,0:T(8,128)(2,1)S(1)}, bf16[2,1024,128]{2,1,0:T(8,128)(2,1)}, u32[]{:S(2)}) copy-start(bf16[2,1024,128]{2,1,0:T(8,128)(2,1)} %param.26) | copy-start | bytes 1572868
  130.7 12.9 %copy-start.44 = (bf16[2,8,512,128]{3,2,1,0:T(8,128)(2,1)S(1)}, bf16[2,8,512,128]{3,2,1,0:T(8,128)(2,1)}, u32[]{:S(2)}) copy-start(bf16[2,8,512,128]{3,2,1,0:T(8,128)(2,1)} %get-tuple-element.355) | copy-start | bytes 6291460 | tf_op jit(solution)/shard_map/while
  149.8 12.9 %copy-start.44 = (bf16[2,8,512,128]{3,2,1,0:T(8,128)(2,1)S(1)}, bf16[2,8,512,128]{3,2,1,0:T(8,128)(2,1)}, u32[]{:S(2)}) copy-start(bf16[2,8,512,128]{3,2,1,0:T(8,128)(2,1)} %get-tuple-element.355) | copy-start | bytes 6291460 | tf_op jit(solution)/shard_map/while
  185.7 33.2 %all-to-all-start = ((bf16[128,16,512]{2,1,0:T(8,128)(2,1)}), bf16[128,16,512]{2,1,0:T(8,128)(2,1)}, u32[]{:S(2)}, u32[]{:S(2)}) async-start(bf16[128,16,512]{2,1,0:T(8,128)(2,1)} %copy.165), calls=%async_computation | async-start | bytes 4194304 | tf_op jit(solution)/shard_map/all_to_all | solution.py:80
  218.9 32.2 %all-to-all-start.1 = ((bf16[128,16,512]{2,1,0:T(8,128)(2,1)}), bf16[128,16,512]{2,1,0:T(8,128)(2,1)}, u32[]{:S(2)}, u32[]{:S(2)}) async-start(bf16[128,16,512]{2,1,0:T(8,128)(2,1)} %copy.168), calls=%async_computation.1 | async-start | bytes 4194304 | tf_op jit(solution)/shard_map/all_to_all | solution.py:78
  259.3 7.4 %copy-start.36 = (bf16[2,2,128]{2,1,0:T(2,128)(2,1)S(1)}, bf16[2,2,128]{2,1,0:T(2,128)(2,1)}, u32[]{:S(2)}) copy-start(bf16[2,2,128]{2,1,0:T(2,128)(2,1)} %param.33) | copy-start | bytes 3076
  259.3 8.4 %copy-start.6 = (f32[512,16]{1,0:T(8,128)S(1)}, f32[512,16]{1,0:T(8,128)}, u32[]{:S(2)}) copy-start(f32[512,16]{1,0:T(8,128)} %copy-done.5) | copy-start | bytes 98308
  259.3 8.4 %copy-start.14 = (f32[512,16]{1,0:T(8,128)S(1)}, f32[512,16]{1,0:T(8,128)}, u32[]{:S(2)}) copy-start(f32[512,16]{1,0:T(8,128)} %copy-done.13) | copy-start | bytes 98308
  259.3 8.4 %copy-start.20 = (bf16[256,2,32]{0,2,1:T(8,128)(2,1)S(1)}, bf16[256,2,32]{0,2,1:T(8,128)(2,1)}, u32[]{:S(2)}) copy-start(bf16[256,2,32]{0,2,1:T(8,128)(2,1)} %copy-done.19) | copy-start | bytes 98308
  259.3 8.4 %copy-start.38 = (f32[1,1,256]{2,1,0:T(1,128)S(1)}, f32[1,1,256]{2,1,0:T(1,128)}, u32[]{:S(2)}) copy-start(f32[1,1,256]{2,1,0:T(1,128)} %copy-done.37) | copy-start | bytes 3076
  259.3 8.4 %copy-start.40 = (f32[1,1,256]{2,1,0:T(1,128)S(1)}, f32[1,1,256]{2,1,0:T(1,128)}, u32[]{:S(2)}) copy-start(f32[1,1,256]{2,1,0:T(1,128)} %copy-done.39) | copy-start | bytes 3076
  259.3 8.4 %copy-start.43 = (f32[32]{0:T(128)S(1)}, f32[32]{0:T(128)}, u32[]{:S(2)}) copy-start(f32[32]{0:T(128)} %get-tuple-element.230) | copy-start | bytes 388
  259.3 64.3 %all-to-all-start.2 = ((f32[4,512,512]{2,0,1:T(4,128)}), f32[4,512,512]{2,0,1:T(4,128)}, u32[]{:S(2)}, u32[]{:S(2)}) async-start(f32[4,512,512]{2,0,1:T(4,128)} %copy.170), calls=%async_computation.2 | async-start | bytes 8388608 | tf_op jit(solution)/shard_map/all_to_all | solution.py:82
  267.7 8.2 %copy-start.7 = (bf16[1,1024,128]{2,1,0:T(8,128)(2,1)S(1)}, bf16[1,1024,128]{2,1,0:T(8,128)(2,1)}, u32[]{:S(2)}) copy-start(bf16[1,1024,128]{2,1,0:T(8,128)(2,1)} %get-tuple-element.197) | copy-start | bytes 786436
  267.7 8.3 %copy-start.30 = (bf16[2,128]{1,0:T(2,128)(2,1)S(1)}, bf16[2,128]{1,0:T(2,128)(2,1)}, u32[]{:S(2)}) copy-start(bf16[2,128]{1,0:T(2,128)(2,1)} %param.35) | copy-start | bytes 1540
  267.7 8.9 %copy-start.31 = (bf16[2,128]{1,0:T(2,128)(2,1)S(1)}, bf16[2,128]{1,0:T(2,128)(2,1)}, u32[]{:S(2)}) copy-start(bf16[2,128]{1,0:T(2,128)(2,1)} %param.32) | copy-start | bytes 1540
  344.1 12.9 %copy-start.47 = (bf16[2,8,512,128]{3,2,1,0:T(8,128)(2,1)S(1)}, bf16[2,8,512,128]{3,2,1,0:T(8,128)(2,1)}, u32[]{:S(2)}) copy-start(bf16[2,8,512,128]{3,2,1,0:T(8,128)(2,1)} %get-tuple-element.379) | copy-start | bytes 6291460 | tf_op jit(solution)/shard_map/while
  363.2 12.9 %copy-start.47 = (bf16[2,8,512,128]{3,2,1,0:T(8,128)(2,1)S(1)}, bf16[2,8,512,128]{3,2,1,0:T(8,128)(2,1)}, u32[]{:S(2)}) copy-start(bf16[2,8,512,128]{3,2,1,0:T(8,128)(2,1)} %get-tuple-element.379) | copy-start | bytes 6291460 | tf_op jit(solution)/shard_map/while
  398.7 32.0 %all-to-all-start.3 = ((bf16[128,16,512]{2,1,0:T(8,128)(2,1)}), bf16[128,16,512]{2,1,0:T(8,128)(2,1)}, u32[]{:S(2)}, u32[]{:S(2)}) async-start(bf16[128,16,512]{2,1,0:T(8,128)(2,1)} %copy.182), calls=%async_computation.3 | async-start | bytes 4194304 | tf_op jit(solution)/shard_map/all_to_all | solution.py:80
  430.8 33.7 %all-to-all-start.4 = ((bf16[128,16,512]{2,1,0:T(8,128)(2,1)}), bf16[128,16,512]{2,1,0:T(8,128)(2,1)}, u32[]{:S(2)}, u32[]{:S(2)}) async-start(bf16[128,16,512]{2,1,0:T(8,128)(2,1)} %copy.185), calls=%async_computation.4 | async-start | bytes 4194304 | tf_op jit(solution)/shard_map/all_to_all | solution.py:78
  472.7 5.6 %copy-start.33 = (f32[128]{0:T(128)S(1)}, f32[128]{0:T(128)}, u32[]{:S(2)}) copy-start(f32[128]{0:T(128)} %get-tuple-element.165) | copy-start | bytes 1540
  472.7 5.8 %copy-start.32 = (f32[128]{0:T(128)S(1)}, f32[128]{0:T(128)}, u32[]{:S(2)}) copy-start(f32[128]{0:T(128)} %get-tuple-element.166) | copy-start | bytes 1540
  472.7 63.0 %all-to-all-start.5 = ((f32[4,512,512]{2,0,1:T(4,128)}), f32[4,512,512]{2,0,1:T(4,128)}, u32[]{:S(2)}, u32[]{:S(2)}) async-start(f32[4,512,512]{2,0,1:T(4,128)} %copy.187), calls=%async_computation.5 | async-start | bytes 8388608 | tf_op jit(solution)/shard_map/all_to_all | solution.py:82
  (26 other events, 80.1 us)
Sparse Core Ops, SparseCore 0:
  33.8 70.1 all-gather.2
  106.1 66.6 all-gather.4

commit v2 on v0

v2 whole, which is shorter than its diff:
```python
import functools
import math
import jax
import jax.numpy as jnp
from jax import lax
from jax.experimental import pallas as pl
from jax.experimental.pallas import tpu as pltpu
from jax.sharding import PartitionSpec as P

LN_EPS = 1e-5
LANES = 128
AG_CHUNKS = 1
F32 = jnp.float32
BF16 = jnp.bfloat16


def dot_nn(a, b):
    return lax.dot_general(a, b, (((1,), (0,)), ((), ())), preferred_element_type=F32)


def dot_nt(a, b):
    return lax.dot_general(a, b, (((1,), (1,)), ((), ())), preferred_element_type=F32)


I_STRIDE = 24
S_GROUP = 16


def msa_kernel(m_ref, norm_ref, w_ref, bias_ref, a_ref, b_ref, y_ref, t_ref):
    s_blk, n_i, _ = m_ref.shape
    layers, n_c = a_ref.shape[0], b_ref.shape[1]
    group = S_GROUP

    def rows(g, carry):
        base = pl.multiple_of(g * group, group)
        x = m_ref[pl.ds(base, group)].astype(F32).reshape(group * n_i, -1)
        mean_val = jnp.mean(x, axis=-1, keepdims=True)
        centered = x - mean_val
        var_val = jnp.mean(centered * centered, axis=-1, keepdims=True)
        scaled = centered * lax.rsqrt(var_val + LN_EPS)
        normed = jnp.concatenate([(scaled * norm_ref[l, 0:1] + norm_ref[l, 1:2]).astype(BF16) for l in range(layers)], axis=1)
        proj = dot_nn(normed, w_ref[...]) + bias_ref[...]
        for s in range(group):
            y_ref[pl.ds(pl.multiple_of((base + s) * I_STRIDE, 8), n_i), :] = proj[s * n_i:(s + 1) * n_i]
        return carry
    lax.fori_loop(0, s_blk // group, rows, 0)

    def columns(i, carry):
        flip = y_ref[pl.ds(i, s_blk, stride=I_STRIDE), :].T
        for l in range(layers):
            top = 2 * l * n_c
            a_ref[l, pl.ds(pl.multiple_of(i * n_c, n_c), n_c), :] = flip[top:top + n_c].astype(BF16)
            t_ref[l, pl.ds(i, n_c, stride=I_STRIDE), :] = flip[top + n_c:top + 2 * n_c]
        return carry
    lax.fori_loop(0, n_i, columns, 0)
    for l in range(layers):
        for d in range(n_c):
            b_ref[l, d] = t_ref[l, d * I_STRIDE:d * I_STRIDE + n_i, :].astype(BF16)


def msa_project(msa_act, norm_w, w_bd, bias):
    seqs, n_i, n_m = msa_act.shape
    layers = norm_w.shape[0]
    n_c = w_bd.shape[1] // (2 * layers)
    s_blk = LANES
    return pl.pallas_call(
        msa_kernel, grid=(seqs // s_blk,),
        in_specs=[
            pl.BlockSpec((s_blk, n_i, n_m), lambda s: (s, 0, 0)),
            pl.BlockSpec(norm_w.shape, lambda s: (0, 0, 0)),
            pl.BlockSpec(w_bd.shape, lambda s: (0, 0)),
            pl.BlockSpec(bias.shape, lambda s: (0, 0)),
        ],
        out_specs=(pl.BlockSpec((layers, n_i * n_c, s_blk), lambda s: (0, 0, s)),
                   pl.BlockSpec((layers, n_c, n_i, s_blk), lambda s: (0, 0, 0, s))),
        out_shape=(jax.ShapeDtypeStruct((layers, n_i * n_c, seqs), BF16),
                   jax.ShapeDtypeStruct((layers, n_c, n_i, seqs), BF16)),
        scratch_shapes=[pltpu.VMEM((s_blk * I_STRIDE, w_bd.shape[1]), F32),
                        pltpu.VMEM((layers, n_c * I_STRIDE, s_blk), F32)],
        compiler_params=pltpu.CompilerParams(dimension_semantics=('arbitrary',)),
        cost_estimate=pl.CostEstimate(flops=2 * seqs * n_i * n_m * 2 * n_c * layers,
                                      bytes_accessed=2 * seqs * n_i * (n_m + 2 * n_c * layers), transcendentals=0),
        name='msa_project',
    )(msa_act, norm_w, w_bd, bias)


def opm_kernel(inv_s, first, last, a_ref, b_ref, w_ref, bias_ref, *rest):
    acc_ref, out_ref, q_ref = (None,) * first + rest
    part = pl.program_id(1)
    dev, d_blk, j_loc, seqs = b_ref.shape
    n_i, _, j_blk = q_ref.shape
    n_c = a_ref.shape[0] // n_i
    for d in range(d_blk):
        rhs = b_ref[:, d, :, :].reshape(dev * j_loc, seqs)
        prod = (dot_nt(a_ref[...], rhs) * inv_s).astype(BF16)
        base = pl.multiple_of((part * d_blk + d) * n_c, n_c)
        q_ref[:, pl.ds(base, n_c), :] = prod.reshape(n_i, n_c, j_blk)

    @pl.when(part == pl.num_programs(1) - 1)
    def _():
        def body(i, carry):
            upd = dot_nn(w_ref[...], q_ref[i])
            if not first:
                upd = acc_ref[i] + upd
            out_ref[i] = (upd + bias_ref[...]).astype(BF16) if last else upd
            return carry
        lax.fori_loop(0, n_i, body, 0)


def opm_update(a_t, b_all, w_t, bias, acc=None, last=True):
    n_dev, n_d, j_loc, seqs = b_all.shape
    rows_c = a_t.shape[0]
    n_z = w_t.shape[0]
    n_c = w_t.shape[1] // n_d
    n_i = rows_c // n_c
    cols = n_dev * j_loc
    j_blk = 2 * LANES
    dev_blk = j_blk // j_loc
    d_blk = math.gcd(n_d, 8)
    grid = (cols // j_blk, n_d // d_blk)
    row_spec = pl.BlockSpec((n_i, n_z, j_blk), lambda j, d: (0, 0, j))
    first = acc is None
    return pl.pallas_call(
        functools.partial(opm_kernel, 1.0 / seqs, first, last),
        grid=grid,
        in_specs=[
            pl.BlockSpec((rows_c, seqs), lambda j, d: (0, 0)),
            pl.BlockSpec((dev_blk, d_blk, j_loc, seqs), lambda j, d: (j, d, 0, 0)),
            pl.BlockSpec(w_t.shape, lambda j, d: (0, 0)),
            pl.BlockSpec(bias.shape, lambda j, d: (0, 0)),
        ] + ([] if first else [row_spec]),
        out_specs=row_spec,
        out_shape=jax.ShapeDtypeStruct((n_i, n_z, cols), BF16 if last else F32),
        scratch_shapes=[pltpu.VMEM((n_i, n_d * n_c, j_blk), BF16)],
        compiler_params=pltpu.CompilerParams(dimension_semantics=('arbitrary', 'arbitrary')),
        cost_estimate=pl.CostEstimate(
            flops=2 * rows_c * seqs * cols * n_d + 2 * n_i * cols * n_d * n_c * n_z,
            bytes_accessed=2 * (n_dev * n_d * j_loc * seqs + n_i * n_z * cols), transcendentals=0),
        name='opm_update',
    )(a_t, b_all, w_t, bias, *(() if first else (acc,)))


def norm_columns(x_f32, gain, offset):
    mean_val = jnp.mean(x_f32, axis=0, keepdims=True)
    centered = x_f32 - mean_val
    var_val = jnp.mean(centered * centered, axis=0, keepdims=True)
    return (centered * lax.rsqrt(var_val + LN_EPS) * gain + offset).astype(BF16)


def project_row(i, z_f32, mask_row, nin_ref, w_ref, b_ref, gate_ref, s_refs):
    zn = norm_columns(z_f32, nin_ref[0], nin_ref[1])
    n_z = z_f32.shape[0]
    lanes = z_f32.shape[1]
    gate_ref[i] = jax.nn.sigmoid(dot_nn(w_ref[4], zn) + b_ref[4])
    for q in range(2):
        lin = dot_nn(w_ref[2 * q], zn) + b_ref[2 * q]
        sig = jax.nn.sigmoid(dot_nn(w_ref[2 * q + 1], zn) + b_ref[2 * q + 1])
        val = mask_row * sig * lin
        for t in range(lanes // LANES):
            s_refs[q][t, pl.ds(i, n_z, stride=I_STRIDE), :] = val[:, t * LANES:(t + 1) * LANES]


def emit_ab(ab_ref, s_refs):
    n_dev, _, n_cl, n_i, lanes = ab_ref.shape

    def body(dev, carry):
        for q in range(2):
            for c in range(n_cl):
                base = pl.multiple_of((dev * n_cl + c) * I_STRIDE, 8)
                for t in range(lanes // LANES):
                    ab_ref[dev, q, c, :, t * LANES:(t + 1) * LANES] = s_refs[q][t, pl.ds(base, n_i), :].astype(BF16)
        return carry
    lax.fori_loop(0, n_dev, body, 0)


def start_kernel(z_ref, u_ref, mask_ref, nin_ref, w_ref, b_ref, z_out, gate_ref, ab_ref, s_a, s_b):
    n_i = z_ref.shape[0]

    def body(i, carry):
        z_new = (z_ref[i].astype(F32) + u_ref[i].astype(F32)).astype(BF16)
        z_out[i] = z_new
        project_row(i, z_new.astype(F32), mask_ref[pl.ds(i, 1), :], nin_ref, w_ref, b_ref, gate_ref, (s_a, s_b))
        return carry
    lax.fori_loop(0, n_i, body, 0)
    emit_ab(ab_ref, (s_a, s_b))


def finish_stats(o_ref, s_o):
    n_c, n_i, lanes = o_ref.shape
    mean_val = jnp.mean(o_ref[...], axis=0)
    centered = o_ref[...] - mean_val[None]
    var_val = jnp.mean(centered * centered, axis=0)
    rstd = lax.rsqrt(var_val + LN_EPS)

    def body(c, carry):
        base = pl.multiple_of(c * I_STRIDE, 8)
        norm = (o_ref[c] - mean_val) * rstd
        for t in range(lanes // LANES):
            s_o[t, pl.ds(base, n_i), :] = norm[:, t * LANES:(t + 1) * LANES]
        return carry
    lax.fori_loop(0, n_c, body, 0)


def finish_row(i, z_ref, gate_ref, nout_ref, wo_ref, bo_ref, s_o):
    tiles, rows, _ = s_o.shape
    n_c = rows // I_STRIDE
    norm = jnp.concatenate([s_o[t, pl.ds(i, n_c, stride=I_STRIDE), :] for t in range(tiles)], axis=1)
    norm = (norm * nout_ref[0] + nout_ref[1]).astype(BF16)
    upd = (dot_nn(wo_ref[...], norm) + bo_ref[...]).astype(BF16)
    return (z_ref[i].astype(F32) + gate_ref[i] * upd.astype(F32)).astype(BF16)


def middle_kernel(o_ref, zin_ref, gin_ref, nout_ref, wo_ref, bo_ref, u_ref, mask_ref, nin_ref, w_ref, b_ref,
                  z_out, gate_ref, ab_ref, s_a, s_b, s_o):
    n_i = zin_ref.shape[0]
    finish_stats(o_ref, s_o)

    def body(i, carry):
        z_mid = finish_row(i, zin_ref, gin_ref, nout_ref, wo_ref, bo_ref, s_o)
        z_new = (z_mid.astype(F32) + u_ref[i].astype(F32)).astype(BF16)
        z_out[i] = z_new
        project_row(i, z_new.astype(F32), mask_ref[pl.ds(i, 1), :], nin_ref, w_ref, b_ref, gate_ref, (s_a, s_b))
        return carry
    lax.fori_loop(0, n_i, body, 0)
    emit_ab(ab_ref, (s_a, s_b))


def end_kernel(o_ref, zin_ref, gin_ref, nout_ref, wo_ref, bo_ref, z_out, s_o):
    n_i = zin_ref.shape[0]
    finish_stats(o_ref, s_o)

    def body(i, carry):
        z_new = finish_row(i, zin_ref, gin_ref, nout_ref, wo_ref, bo_ref, s_o)
        z_out[i] = z_new.astype(F32).T.astype(BF16)
        return carry
    lax.fori_loop(0, n_i, body, 0)


J_BLK = 256


def tri_call(kind, n_dev, args):
    kernels = {'start': start_kernel, 'middle': middle_kernel, 'end': end_kernel}
    if kind == 'start':
        n_i, n_z, cols = args[0].shape
    else:
        n_i, n_z, cols = args[1].shape
    n_ch = n_z

    def blk(arr, which):
        shape = arr.shape
        if which == 'j':
            return pl.BlockSpec(shape[:-1] + (J_BLK,), lambda j: (0,) * (len(shape) - 1) + (j,))
        return pl.BlockSpec(shape, lambda j: (0,) * len(shape))

    tiles = J_BLK // LANES
    fin = ['j', 'j', 'j', 'w', 'w', 'w']
    pro = ['j', 'j', 'w', 'w', 'w']
    kinds = {'start': ['j'] + pro, 'middle': fin + pro, 'end': fin}[kind]
    scr = pltpu.VMEM((tiles, n_ch * I_STRIDE, LANES), F32)
    if kind == 'end':
        out_shape = jax.ShapeDtypeStruct((n_i, cols, n_z), BF16)
        out_specs = pl.BlockSpec((n_i, J_BLK, n_z), lambda j: (0, j, 0))
        scratch = [scr]
    else:
        out_shape = (jax.ShapeDtypeStruct((n_i, n_z, cols), BF16),
                     jax.ShapeDtypeStruct((n_i, n_z, cols), F32),
                     jax.ShapeDtypeStruct((n_dev, 2, n_ch // n_dev, n_i, cols), BF16))
        out_specs = tuple(blk(s, 'j') for s in out_shape)
        scratch = [scr, scr] + ([scr] if kind == 'middle' else [])
    return pl.pallas_call(
        kernels[kind], grid=(cols // J_BLK,),
        in_specs=[blk(a, k) for a, k in zip(args, kinds)],
        out_specs=out_specs, out_shape=out_shape, scratch_shapes=scratch,
        compiler_params=pltpu.CompilerParams(dimension_semantics=('arbitrary',)),
        cost_estimate=pl.CostEstimate(flops=12 * n_i * cols * n_z * n_z, bytes_accessed=16 * n_i * cols * n_z,
                                      transcendentals=3 * n_i * cols * n_z),
        name='tri_' + kind,
    )(*args)


def product_kernel(ab_ref, o_ref):
    n_dev, _, _, n_i, cols = ab_ref.shape
    left = ab_ref[:, 0, 0].reshape(n_dev * n_i, cols)
    right = ab_ref[:, 1, 0].reshape(n_dev * n_i, cols)
    half = cols // 2
    for h in range(2):
        o_ref[:, 0, :, h * half:(h + 1) * half] = dot_nt(left, right[h * half:(h + 1) * half]).reshape(n_dev, n_i, half)


def tri_product(ab):
    n_dev, _, n_cl, n_i, cols = ab.shape
    rows = n_dev * n_i
    return pl.pallas_call(
        product_kernel, grid=(n_cl,),
        in_specs=[pl.BlockSpec((n_dev, 2, 1, n_i, cols), lambda c: (0, 0, c, 0, 0))],
        out_specs=pl.BlockSpec((n_dev, 1, n_i, cols), lambda c: (0, c, 0, 0)),
        out_shape=jax.ShapeDtypeStruct((n_dev, n_cl, n_i, cols), F32),
        compiler_params=pltpu.CompilerParams(dimension_semantics=('arbitrary',)),
        cost_estimate=pl.CostEstimate(flops=2 * n_cl * rows * rows * cols, bytes_accessed=8 * n_cl * rows * cols,
                                      transcendentals=0),
        name='tri_product',
    )(ab)


def solution(mesh):
    pair_spec = P(('batch', 'dap'), None, None)
    mask_spec = P(('batch', 'dap'), None)
    msa_spec = P(None, ('batch', 'dap'), None)
    n_dev = mesh.shape['dap']

    def column(vec):
        return vec.astype(F32)[..., None]

    def device_fn(pair_act, pair_mask, msa_act, opm_norm, opm_w_in, opm_b_in, opm_w_out, opm_b_out, tri_norm_in, tri_w_ab, tri_b_ab, tri_w_gate, tri_b_gate, tri_norm_out, tri_w_out, tri_b_out):
        layers = opm_norm.shape[0]
        n_i, cols, n_z = pair_act.shape
        n_c = opm_w_in.shape[-1]
        mask_f = pair_mask.astype(F32)
        n_m = msa_act.shape[-1]
        w_bd = jnp.zeros((layers, n_m, layers, 2 * n_c), BF16)
        for l in range(layers):
            w_bd = w_bd.at[l, :, l].set(opm_w_in[l].reshape(n_m, 2 * n_c))
        left, right = msa_project(msa_act, opm_norm.astype(F32), w_bd.reshape(layers * n_m, layers * 2 * n_c),
                                  opm_b_in.astype(F32).reshape(1, -1))
        chunks = [AG_CHUNKS] + [1] * (layers - 1)
        gathered = []
        for l in range(layers):
            size = n_c // chunks[l]
            gathered.append([lax.all_gather(right[l, k * size:(k + 1) * size], 'dap', axis=0) for k in range(chunks[l])])
        updates = []
        for l in range(layers):
            w_t = opm_w_out[l].reshape(n_c, n_c, n_z).transpose(2, 1, 0).reshape(n_z, n_c * n_c)
            acc, part = None, n_c * n_c // chunks[l]
            for k in range(chunks[l]):
                acc = opm_update(left[l], gathered[l][k], w_t[:, k * part:(k + 1) * part], column(opm_b_out[l]), acc,
                                 last=k == chunks[l] - 1)
            updates.append(acc)
        z_t = jnp.swapaxes(pair_act, 1, 2)
        fin = None
        for l in range(layers):
            w_all = jnp.concatenate([tri_w_ab[l].transpose(1, 2, 0), tri_w_gate[l].T[None]], axis=0)
            b_all = column(jnp.concatenate([tri_b_ab[l], tri_b_gate[l][None]], axis=0))
            pro = (updates[l], mask_f, column(tri_norm_in[l]), w_all, b_all)
            if l == 0:
                z_t, gate, ab = tri_call('start', n_dev, (z_t,) + pro)
            else:
                z_t, gate, ab = tri_call('middle', n_dev, fin + pro)
            ab = lax.all_to_all(ab.reshape(n_dev, -1, cols), 'dap', 0, 0, tiled=True).reshape(ab.shape)
            prod = lax.all_to_all(tri_product(ab), 'dap', 0, 0, tiled=True)
            fin = (prod.reshape(-1, n_i, cols), z_t, gate, column(tri_norm_out[l]), tri_w_out[l].T, column(tri_b_out[l]))
        return tri_call('end', n_dev, fin)

    return jax.shard_map(device_fn, mesh=mesh, in_specs=(pair_spec, mask_spec, msa_spec) + (P(),) * 13, out_specs=pair_spec, check_vma=False)
```

time: 1130 us -> 465 us (0.41); the launches traced: 1110 us -> 464 us
  local copies, waits for them, and re-layouts: 459 us -> 26.4 us
  matrix products: 266 us -> 0 us
  waiting for transfers between devices: 317 us -> 138 us
  Pallas kernels: 0 us -> 141 us
  blocking collectives: 0 us -> 129 us
  other arithmetic: 52.1 us -> 5.45 us
    dot_general x22 -> x0, matrix products: 266 us -> none  [the longest x2 113 us: device_fn(): jnp.einsum('cik,cjk->cij', left_tri, right_full, preferred_element_type=j...]
    all_gather x4 -> x2, waiting for transfers between devices: 317 us -> 54.4 us  [device_fn(): lax.all_gather(right[l, k * size:(k + 1) * size], 'dap', axis=0)]
    another operation x6 -> x2, local copies, waits for them, and re-layouts: 243 us -> 0.1 us
    while x10 -> x0, local copies, waits for them, and re-layouts: 173 us -> none  [the longest x2 173 us: outer_mean_rows(): lax.map(block_update, (left_blocks, pair_blocks))]
    pallas_call x0 -> x8, Pallas kernels: none -> 141 us  [the longest x3 62.8 us: tri_call(): pl.pallas_call(kernels[kind], grid=(cols // J_BLK,), in_specs=[blk(a, k)...]
    all_to_all x0 -> x2, blocking collectives: none -> 129 us  [device_fn(): lax.all_to_all(ab.reshape(n_dev, -1, cols), 'dap', 0, 0, tiled=True)]
    all_to_all x0 -> x2, waiting for transfers between devices: none -> 82.6 us  [device_fn(): prod = lax.all_to_all(tri_product(ab), 'dap', 0, 0, tiled=True)]
    reduce_sum x8 -> x0, other arithmetic: 24.5 us -> none  [the longest x5 19.8 us: layer_norm(): var_val = jnp.mean(centered * centered, axis=norm_axis, keepdims=True)]
  transfers between devices with their start and end apart: 4 -> 4, of which waited for: 3 -> 3; matrix products, arithmetic and copies ran while one was open for 38% -> 5% of each run, Pallas kernels for 0% -> 15%
where the time goes in v2:
time: 465 us; the launch traced here: 464 us
  Pallas kernels  141 us (30%)
  waiting for transfers between devices  138 us (30%)
  blocking collectives  129 us (28%)
  local copies, waits for them, and re-layouts  26.4 us (6%)
  between operations  13.6 us (3%)
  starting transfers between devices  11.3 us (2%)
  other arithmetic  5.45 us (1%)
    all_to_all x2, blocking collectives, device_fn(): lax.all_to_all(ab.reshape(n_dev, -1, cols), 'dap', 0, 0, tiled=True)  129 us
    all_to_all x2, waiting for transfers between devices, device_fn(): prod = lax.all_to_all(tri_product(ab), 'dap', 0, 0, tiled=True)  82.6 us
    pallas_call x3, Pallas kernels, tri_call(): pl.pallas_call(kernels[kind], grid=(cols // J_BLK,), in_specs=[blk(a, k)...  62.8 us
    all_gather x2, waiting for transfers between devices, device_fn(): lax.all_gather(right[l, k * size:(k + 1) * size], 'dap', axis=0)  54.4 us
    pallas_call x2, Pallas kernels, opm_update(): pl.pallas_call(functools.partial(opm_kernel, 1.0 / seqs, first, last), gr...  44.8 us
    pallas_call x1, Pallas kernels, msa_project(): pl.pallas_call(msa_kernel, grid=(seqs // s_blk,), in_specs=[pl.BlockSpec(...  21.6 us
    pallas_call x2, Pallas kernels, tri_product(): pl.pallas_call(product_kernel, grid=(n_cl,), in_specs=[pl.BlockSpec((n_de...  11.3 us
    all_to_all x2, starting transfers between devices, device_fn(): prod = lax.all_to_all(tri_product(ab), 'dap', 0, 0, tiled=True)  11.3 us
  transfers between devices with their start and end apart: 4, of which 3 were waited for; matrix products, arithmetic and copies ran while one was open for 5% of the time, Pallas kernels for 15%

profile of v2, /device:TPU:103, one launch (start us, length us, event | category | flops | bytes accessed | tf_op | source)
XLA Modules:
  0.0 463.8 jit_solution(17776888353764615505)
XLA Ops:
  6.6 1.3 reshape.282.bias_ref
  7.9 1.3 convert_element_type.131.norm_ref
  9.2 0.8 fusion.5
  10.2 0.9 scatter.9
  11.9 21.6 %msa_project.1 = (bf16[2,512,512]{2,1,0:T(8,128)(2,1)}, bf16[2,32,16,512]{3,2,1,0:T(8,128)(2,1)}) custom-call(bf16[512,16,256]{2,1,0:T(8,128)(2,1)} %m_ref.1, f32[2,2,256]{2,1,0:T(2,128)} %convert_element_type.131.norm_ref, bf16[512,128]{1,0:T(8,128)(2,1)} %copy.113.w_ref, f32[1,128]{1,0:T(1,128)} %reshape.282.bias_ref), custom_call_target="tpu_custom_call" | custom-call | flops 536870912 | bytes 6291456 | tf_op jit(solution)/shard_map/msa_project/pallas_call | solution.py:66
  33.6 2.4 fusion
  40.9 0.8 copy.119
  42.4 0.8 copy.121.nin_ref
  44.1 1.8 fusion.1
  46.0 0.9 copy.115.w_ref
  46.9 2.6 copy.110
  50.2 0.8 maximum_convert_fusion.b_ref
  50.9 1.1 slice_bitcast_fusion
  52.0 54.4 %all-gather.3.cloned.1.call-done.b_ref = bf16[32,32,16,512]{3,2,1,0:T(8,128)(2,1)} async-done(((bf16[1,32,16,512]{3,2,1,0:T(8,128)(2,1)}), bf16[32,32,16,512]{3,2,1,0:T(8,128)(2,1)}) %all-gather.3.cloned.1.call-update) | async-done | bytes 16777232 | tf_op jit(solution)/shard_map/all_gather | solution.py:330
  106.4 22.4 %opm_update.2.u_ref = bf16[16,128,512]{2,1,0:T(8,128)(2,1)} custom-call(bf16[512,512]{1,0:T(8,128)(2,1)} %get-tuple-element.48.a_ref, bf16[32,32,16,512]{3,2,1,0:T(8,128)(2,1)} %all-gather.3.cloned.1.call-done.b_ref, bf16[128,1024]{1,0:T(8,128)(2,1)} %copy.115.w_ref, f32[128,1]{1,0:T(8,128)} %copy.116.bias_ref), custom_call_target="tpu_custom_call" | custom-call | flops 10737418240 | bytes 18874368 | tf_op jit(solution)/shard_map/opm_update/pallas_call | solution.py:123
  128.8 16.9 %tri_start.1 = (bf16[16,128,512]{2,1,0:T(8,128)(2,1)}, f32[16,128,512]{2,1,0:T(8,128)}, bf16[32,2,4,16,512]{4,3,2,1,0:T(8,128)(2,1)}) custom-call(bf16[16,128,512]{2,1,0:T(8,128)(2,1)} %bitcast.84, bf16[16,128,512]{2,1,0:T(8,128)(2,1)} %opm_update.2.u_ref, f32[16,512]{1,0:T(8,128)} %convert_element_type.134.mask_ref, f32[2,128,1]{2,1,0:T(8,128)} %copy.121.nin_ref, ...), custom_call_target="tpu_custom_call" | custom-call | flops 1610612736 | bytes 16777216 | tf_op jit(solution)/shard_map/tri_start/pallas_call | solution.py:271
  145.7 73.1 %all_to_all.20 = bf16[32,128,512]{2,1,0:T(8,128)(2,1)} all-to-all(bf16[32,128,512]{2,1,0:T(8,128)(2,1)} %bitcast.83), channel_id=1, replica_groups=mesh['batch'=1,'dap'=32] {'dap'}, dimensions={0} | all-to-all | bytes 8388608 | tf_op jit(solution)/shard_map/all_to_all | solution.py:349
  218.8 5.7 %tri_product.2 = f32[32,4,16,512]{3,2,1,0:T(8,128)} custom-call(bf16[32,2,4,16,512]{4,3,2,1,0:T(8,128)(2,1)} %bitcast.80), custom_call_target="tpu_custom_call" | custom-call | flops 1073741824 | bytes 8388608 | tf_op jit(solution)/shard_map/tri_product/pallas_call | solution.py:294
  224.5 5.2 %all-to-all-start.1 = ((f32[32,4,16,512]{3,2,1,0:T(8,128)}), f32[32,4,16,512]{3,2,1,0:T(8,128)}, u32[]{:S(2)}, u32[]{:S(2)}) async-start(f32[32,4,16,512]{3,2,1,0:T(8,128)} %tri_product.2), calls=%async_computation.1 | async-start | bytes 8388608 | tf_op jit(solution)/shard_map/all_to_all | solution.py:350
  232.3 0.8 copy.132.nin_ref
  233.2 0.8 copy.130.nout_ref
  234.2 0.8 copy.124.w_ref
  235.7 0.8 maximum_convert_fusion.1.b_ref
  236.5 22.3 %opm_update.3.u_ref = bf16[16,128,512]{2,1,0:T(8,128)(2,1)} custom-call(bf16[512,512]{1,0:T(8,128)(2,1)} %get-tuple-element.47.a_ref, bf16[32,32,16,512]{3,2,1,0:T(8,128)(2,1)} %all-gather.5.cloned.1.call-done.b_ref, bf16[128,1024]{1,0:T(8,128)(2,1)} %copy.124.w_ref, f32[128,1]{1,0:T(8,128)} %copy.125.bias_ref), custom_call_target="tpu_custom_call" | custom-call | flops 10737418240 | bytes 18874368 | tf_op jit(solution)/shard_map/opm_update/pallas_call | solution.py:123
  258.8 27.5 %all-to-all-done.1 = f32[32,4,16,512]{3,2,1,0:T(8,128)} async-done(((f32[32,4,16,512]{3,2,1,0:T(8,128)}), f32[32,4,16,512]{3,2,1,0:T(8,128)}, u32[]{:S(2)}, u32[]{:S(2)}) %all-to-all-start.1) | async-done | bytes 4194336 | tf_op jit(solution)/shard_map/all_to_all | solution.py:350
  286.3 28.6 %tri_middle.1 = (bf16[16,128,512]{2,1,0:T(8,128)(2,1)}, f32[16,128,512]{2,1,0:T(8,128)}, bf16[32,2,4,16,512]{4,3,2,1,0:T(8,128)(2,1)}) custom-call(f32[128,16,512]{2,1,0:T(8,128)} %bitcast.18.o_ref, bf16[16,128,512]{2,1,0:T(8,128)(2,1)} %get-tuple-element.40.zin_ref, f32[16,128,512]{2,1,0:T(8,128)} %get-tuple-element.41.gin_ref, ...), custom_call_target="tpu_custom_call" | custom-call | flops 1610612736 | bytes 16777216 | tf_op jit(solution)/shard_map/tri_middle/pallas_call | solution.py:271
  314.9 55.6 %all_to_all.21 = bf16[32,128,512]{2,1,0:T(8,128)(2,1)} all-to-all(bf16[32,128,512]{2,1,0:T(8,128)(2,1)} %bitcast.82), channel_id=1, replica_groups=mesh['batch'=1,'dap'=32] {'dap'}, dimensions={0} | all-to-all | bytes 8388608 | tf_op jit(solution)/shard_map/all_to_all | solution.py:349
  370.5 5.7 %tri_product.3 = f32[32,4,16,512]{3,2,1,0:T(8,128)} custom-call(bf16[32,2,4,16,512]{4,3,2,1,0:T(8,128)(2,1)} %bitcast.81), custom_call_target="tpu_custom_call" | custom-call | flops 1073741824 | bytes 8388608 | tf_op jit(solution)/shard_map/tri_product/pallas_call | solution.py:294
  376.2 6.1 %all-to-all-start.3 = ((f32[32,4,16,512]{3,2,1,0:T(8,128)}), f32[32,4,16,512]{3,2,1,0:T(8,128)}, u32[]{:S(2)}, u32[]{:S(2)}) async-start(f32[32,4,16,512]{3,2,1,0:T(8,128)} %tri_product.3), calls=%async_computation.3 | async-start | bytes 8388608 | tf_op jit(solution)/shard_map/all_to_all | solution.py:350
  383.7 0.8 copy.134.nout_ref
  384.5 55.2 %all-to-all-done.3 = f32[32,4,16,512]{3,2,1,0:T(8,128)} async-done(((f32[32,4,16,512]{3,2,1,0:T(8,128)}), f32[32,4,16,512]{3,2,1,0:T(8,128)}, u32[]{:S(2)}, u32[]{:S(2)}) %all-to-all-start.3) | async-done | bytes 4194336 | tf_op jit(solution)/shard_map/all_to_all | solution.py:350
  439.7 17.3 %tri_end.1 = bf16[16,512,128]{2,1,0:T(8,128)(2,1)} custom-call(f32[128,16,512]{2,1,0:T(8,128)} %bitcast.38.o_ref, bf16[16,128,512]{2,1,0:T(8,128)(2,1)} %get-tuple-element.43.zin_ref, f32[16,128,512]{2,1,0:T(8,128)} %get-tuple-element.44.gin_ref, f32[2,128,1]{2,1,0:T(8,128)} %copy.134.nout_ref, bf16[128,128]{1,0:T(8,128)(2,1)} %bitcast.94, ...), custom_call_target="tpu_custom_call" | custom-call | flops 1610612736 | bytes 16777216 | tf_op jit(solution)/shard_map/tri_end/pallas_call | solution.py:271
  (69 shorter events, 13.3 us)
Async XLA Ops:
  6.5 99.8 %all-gather.3.cloned.1.call-start = ((), (), s32[]{:S(2)}) async-start(), calls=%async_computation.4 | async-start | bytes 17301504 | tf_op jit(solution)/shard_map/all_gather | solution.py:330
  10.1 26.8 %copy-start.11 = (s32[16,512]{1,0:T(8,128)S(1)}, s32[16,512]{1,0:T(8,128)}, u32[]{:S(2)}) copy-start(s32[16,512]{1,0:T(8,128)} %param.21) | copy-start | bytes 98308
  10.1 27.4 %copy-start.12 = (bf16[2,128]{1,0:T(2,128)(2,1)S(1)}, bf16[2,128]{1,0:T(2,128)(2,1)}, u32[]{:S(2)}) copy-start(bf16[2,128]{1,0:T(2,128)(2,1)} %param.32) | copy-start | bytes 1540
  10.1 28.1 %copy-start.13 = (bf16[2,128]{1,0:T(2,128)(2,1)S(1)}, bf16[2,128]{1,0:T(2,128)(2,1)}, u32[]{:S(2)}) copy-start(bf16[2,128]{1,0:T(2,128)(2,1)} %param.27) | copy-start | bytes 1540
  10.2 28.7 %copy-start.9 = (bf16[2,128,128]{2,1,0:T(8,128)(2,1)S(1)}, bf16[2,128,128]{2,1,0:T(8,128)(2,1)}, u32[]{:S(2)}) copy-start(bf16[2,128,128]{2,1,0:T(8,128)(2,1)} %param.31) | copy-start | bytes 196612
  11.2 32.1 %copy-start.5 = (bf16[2,128,4,128]{3,2,1,0:T(4,128)(2,1)S(1)}, bf16[2,128,4,128]{3,2,1,0:T(4,128)(2,1)}, u32[]{:S(2)}) copy-start(bf16[2,128,4,128]{3,2,1,0:T(4,128)(2,1)} %param.29) | copy-start | bytes 786436
  33.5 13.3 %copy-start = (bf16[16,512,128]{2,1,0:T(8,128)(2,1)S(1)}, bf16[16,512,128]{2,1,0:T(8,128)(2,1)}, u32[]{:S(2)}) copy-start(bf16[16,512,128]{2,1,0:T(8,128)(2,1)} %param.20) | copy-start | bytes 6291460
  36.0 200.5 %all-gather.5.cloned.1.call-start = ((), (), s32[]{:S(2)}) async-start(), calls=%async_computation.5 | async-start | bytes 17301504 | tf_op jit(solution)/shard_map/all_gather | solution.py:330
  38.9 12.0 %copy-start.1 = (bf16[2,512,512]{2,1,0:T(8,128)(2,1)S(1)}, bf16[2,512,512]{2,1,0:T(8,128)(2,1)}, u32[]{:S(2)}) copy-start(bf16[2,512,512]{2,1,0:T(8,128)(2,1)} %get-tuple-element.37) | copy-start | bytes 3145732
  46.9 2.6 copy-start.6
  46.9 3.3 copy-start.4
  46.9 3.3 copy-start.8
  224.5 6.1 %copy-start.14 = (bf16[2,128]{1,0:T(2,128)(2,1)S(1)}, bf16[2,128]{1,0:T(2,128)(2,1)}, u32[]{:S(2)}) copy-start(bf16[2,128]{1,0:T(2,128)(2,1)} %param.35) | copy-start | bytes 1540
  224.5 6.8 %copy-start.7 = (bf16[1,128,128]{2,1,0:T(8,128)(2,1)S(1)}, bf16[1,128,128]{2,1,0:T(8,128)(2,1)}, u32[]{:S(2)}) copy-start(bf16[1,128,128]{2,1,0:T(8,128)(2,1)} %get-tuple-element.55) | copy-start | bytes 98308
  224.5 6.9 %copy-start.10 = (bf16[2,128,128]{2,1,0:T(8,128)(2,1)S(1)}, bf16[2,128,128]{2,1,0:T(8,128)(2,1)}, u32[]{:S(2)}) copy-start(bf16[2,128,128]{2,1,0:T(8,128)(2,1)} %param.34) | copy-start | bytes 196612
  224.5 8.7 %copy-start.15 = (bf16[2,2,128]{2,1,0:T(2,128)(2,1)S(1)}, bf16[2,2,128]{2,1,0:T(2,128)(2,1)}, u32[]{:S(2)}) copy-start(bf16[2,2,128]{2,1,0:T(2,128)(2,1)} %param.33) | copy-start | bytes 3076
  224.5 9.5 %copy-start.3 = (bf16[1,128,4,128]{3,2,1,0:T(4,128)(2,1)S(1)}, bf16[1,128,4,128]{3,2,1,0:T(4,128)(2,1)}, u32[]{:S(2)}) copy-start(bf16[1,128,4,128]{3,2,1,0:T(4,128)(2,1)} %get-tuple-element.51) | copy-start | bytes 393220
  224.5 9.6 %copy-start.2 = (bf16[1,1024,128]{2,1,0:T(8,128)(2,1)S(1)}, bf16[1,1024,128]{2,1,0:T(8,128)(2,1)}, u32[]{:S(2)}) copy-start(bf16[1,1024,128]{2,1,0:T(8,128)(2,1)} %get-tuple-element.49) | copy-start | bytes 786436
  224.5 61.8 %all-to-all-start.1 = ((f32[32,4,16,512]{3,2,1,0:T(8,128)}), f32[32,4,16,512]{3,2,1,0:T(8,128)}, u32[]{:S(2)}, u32[]{:S(2)}) async-start(f32[32,4,16,512]{3,2,1,0:T(8,128)} %tri_product.2), calls=%async_computation.1 | async-start | bytes 8388608 | tf_op jit(solution)/shard_map/all_to_all | solution.py:350
  376.2 63.5 %all-to-all-start.3 = ((f32[32,4,16,512]{3,2,1,0:T(8,128)}), f32[32,4,16,512]{3,2,1,0:T(8,128)}, u32[]{:S(2)}, u32[]{:S(2)}) async-start(f32[32,4,16,512]{3,2,1,0:T(8,128)} %tri_product.3), calls=%async_computation.3 | async-start | bytes 8388608 | tf_op jit(solution)/shard_map/all_to_all | solution.py:350
Sparse Core Ops, SparseCore 0:
  36.1 70.2 all-gather.2
  108.5 105.6 all-gather.4

commit v3 on v2

--- a/solution.py
+++ b/solution.py
@@ -9,7 +9,7 @@
 
 LN_EPS = 1e-5
 LANES = 128
-AG_CHUNKS = 1
+ROW_UNROLL = 4
 F32 = jnp.float32
 BF16 = jnp.bfloat16
 
@@ -23,12 +23,15 @@
 
 
 I_STRIDE = 24
-S_GROUP = 16
-
-
-def msa_kernel(m_ref, norm_ref, w_ref, bias_ref, a_ref, b_ref, y_ref, t_ref):
+S_GROUP = 32
+
+
+def msa_kernel(m_ref, norm_ref, w_ref, bias_ref, *refs):
+    y_ref, t_ref = refs[-2:]
+    layers = t_ref.shape[0]
+    a_refs, b_refs = refs[:layers], refs[layers:2 * layers]
     s_blk, n_i, _ = m_ref.shape
-    layers, n_c = a_ref.shape[0], b_ref.shape[1]
+    n_c = b_refs[0].shape[0]
     group = S_GROUP
 
     def rows(g, carry):
@@ -43,19 +46,19 @@
         for s in range(group):
             y_ref[pl.ds(pl.multiple_of((base + s) * I_STRIDE, 8), n_i), :] = proj[s * n_i:(s + 1) * n_i]
         return carry
-    lax.fori_loop(0, s_blk // group, rows, 0)
+    lax.fori_loop(0, s_blk // group, rows, 0, unroll=2)
 
     def columns(i, carry):
         flip = y_ref[pl.ds(i, s_blk, stride=I_STRIDE), :].T
         for l in range(layers):
             top = 2 * l * n_c
-            a_ref[l, pl.ds(pl.multiple_of(i * n_c, n_c), n_c), :] = flip[top:top + n_c].astype(BF16)
+            a_refs[l][pl.ds(pl.multiple_of(i * n_c, n_c), n_c), :] = flip[top:top + n_c].astype(BF16)
             t_ref[l, pl.ds(i, n_c, stride=I_STRIDE), :] = flip[top + n_c:top + 2 * n_c]
         return carry
-    lax.fori_loop(0, n_i, columns, 0)
+    lax.fori_loop(0, n_i, columns, 0, unroll=4)
     for l in range(layers):
         for d in range(n_c):
-            b_ref[l, d] = t_ref[l, d * I_STRIDE:d * I_STRIDE + n_i, :].astype(BF16)
+            b_refs[l][d] = t_ref[l, d * I_STRIDE:d * I_STRIDE + n_i, :].astype(BF16)
 
 
 def msa_project(msa_act, norm_w, w_bd, bias):
@@ -71,10 +74,10 @@
             pl.BlockSpec(w_bd.shape, lambda s: (0, 0)),
             pl.BlockSpec(bias.shape, lambda s: (0, 0)),
         ],
-        out_specs=(pl.BlockSpec((layers, n_i * n_c, s_blk), lambda s: (0, 0, s)),
-                   pl.BlockSpec((layers, n_c, n_i, s_blk), lambda s: (0, 0, 0, s))),
-        out_shape=(jax.ShapeDtypeStruct((layers, n_i * n_c, seqs), BF16),
-                   jax.ShapeDtypeStruct((layers, n_c, n_i, seqs), BF16)),
+        out_specs=(pl.BlockSpec((n_i * n_c, s_blk), lambda s: (0, s)),) * layers
+        + (pl.BlockSpec((n_c, n_i, s_blk), lambda s: (0, 0, s)),) * layers,
+        out_shape=(jax.ShapeDtypeStruct((n_i * n_c, seqs), BF16),) * layers
+        + (jax.ShapeDtypeStruct((n_c, n_i, seqs), BF16),) * layers,
         scratch_shapes=[pltpu.VMEM((s_blk * I_STRIDE, w_bd.shape[1]), F32),
                         pltpu.VMEM((layers, n_c * I_STRIDE, s_blk), F32)],
         compiler_params=pltpu.CompilerParams(dimension_semantics=('arbitrary',)),
@@ -104,7 +107,7 @@
                 upd = acc_ref[i] + upd
             out_ref[i] = (upd + bias_ref[...]).astype(BF16) if last else upd
             return carry
-        lax.fori_loop(0, n_i, body, 0)
+        lax.fori_loop(0, n_i, body, 0, unroll=4)
 
 
 def opm_update(a_t, b_all, w_t, bias, acc=None, last=True):
@@ -147,17 +150,44 @@
     return (centered * lax.rsqrt(var_val + LN_EPS) * gain + offset).astype(BF16)
 
 
-def project_row(i, z_f32, mask_row, nin_ref, w_ref, b_ref, gate_ref, s_refs):
+def sigmoid(x):
+    return 0.5 * jnp.tanh(0.5 * x) + 0.5
+
+
+def project_row(i, z_f32, mask_row, nin_ref, w_ref, b_ref, s_refs):
     zn = norm_columns(z_f32, nin_ref[0], nin_ref[1])
-    n_z = z_f32.shape[0]
-    lanes = z_f32.shape[1]
-    gate_ref[i] = jax.nn.sigmoid(dot_nn(w_ref[4], zn) + b_ref[4])
+    n_z, lanes = z_f32.shape
+    n_ch = w_ref.shape[0] // 4
+    proj = dot_nn(w_ref[...], zn) + b_ref[...]
     for q in range(2):
-        lin = dot_nn(w_ref[2 * q], zn) + b_ref[2 * q]
-        sig = jax.nn.sigmoid(dot_nn(w_ref[2 * q + 1], zn) + b_ref[2 * q + 1])
+        lin = proj[2 * q * n_ch:(2 * q + 1) * n_ch]
+        sig = sigmoid(proj[(2 * q + 1) * n_ch:(2 * q + 2) * n_ch])
         val = mask_row * sig * lin
         for t in range(lanes // LANES):
-            s_refs[q][t, pl.ds(i, n_z, stride=I_STRIDE), :] = val[:, t * LANES:(t + 1) * LANES]
+            s_refs[q][t, pl.ds(i, n_ch, stride=I_STRIDE), :] = val[:, t * LANES:(t + 1) * LANES]
+
+
+def gate_kernel(z_ref, nin_ref, w_ref, b_ref, gate_ref):
+    def body(i, carry):
+        zn = norm_columns(z_ref[i].astype(F32), nin_ref[0], nin_ref[1])
+        gate_ref[i] = sigmoid(dot_nn(w_ref[...], zn) + b_ref[...])
+        return carry
+    lax.fori_loop(0, z_ref.shape[0], body, 0, unroll=4)
+
+
+def gate_call(z_t, norm_in, w_gate, b_gate):
+    n_i, n_z, cols = z_t.shape
+    row_spec = pl.BlockSpec((n_i, n_z, J_BLK), lambda j: (0, 0, j))
+    return pl.pallas_call(
+        gate_kernel, grid=(cols // J_BLK,),
+        in_specs=[row_spec, pl.BlockSpec(norm_in.shape, lambda j: (0, 0, 0)), pl.BlockSpec(w_gate.shape, lambda j: (0, 0)),
+                  pl.BlockSpec(b_gate.shape, lambda j: (0, 0))],
+        out_specs=row_spec, out_shape=jax.ShapeDtypeStruct(z_t.shape, F32),
+        compiler_params=pltpu.CompilerParams(dimension_semantics=('arbitrary',)),
+        cost_estimate=pl.CostEstimate(flops=12 * n_i * cols * n_z * n_z, bytes_accessed=6 * n_i * cols * n_z,
+                                      transcendentals=n_i * cols * n_z),
+        name='tri_gate',
+    )(z_t, norm_in, w_gate, b_gate)
 
 
 def emit_ab(ab_ref, s_refs):
@@ -170,70 +200,69 @@
                 for t in range(lanes // LANES):
                     ab_ref[dev, q, c, :, t * LANES:(t + 1) * LANES] = s_refs[q][t, pl.ds(base, n_i), :].astype(BF16)
         return carry
-    lax.fori_loop(0, n_dev, body, 0)
-
-
-def start_kernel(z_ref, u_ref, mask_ref, nin_ref, w_ref, b_ref, z_out, gate_ref, ab_ref, s_a, s_b):
+    lax.fori_loop(0, n_dev, body, 0, unroll=2)
+
+
+def start_kernel(z_ref, u_ref, mask_ref, nin_ref, w_ref, b_ref, z_out, ab_ref, s_a, s_b):
     n_i = z_ref.shape[0]
 
     def body(i, carry):
         z_new = (z_ref[i].astype(F32) + u_ref[i].astype(F32)).astype(BF16)
         z_out[i] = z_new
-        project_row(i, z_new.astype(F32), mask_ref[pl.ds(i, 1), :], nin_ref, w_ref, b_ref, gate_ref, (s_a, s_b))
-        return carry
-    lax.fori_loop(0, n_i, body, 0)
+        project_row(i, z_new.astype(F32), mask_ref[pl.ds(i, 1), :], nin_ref, w_ref, b_ref, (s_a, s_b))
+        return carry
+    lax.fori_loop(0, n_i, body, 0, unroll=ROW_UNROLL)
     emit_ab(ab_ref, (s_a, s_b))
 
 
-def finish_stats(o_ref, s_o):
+def finish_stats(o_ref, s_o, r_ref):
     n_c, n_i, lanes = o_ref.shape
-    mean_val = jnp.mean(o_ref[...], axis=0)
-    centered = o_ref[...] - mean_val[None]
-    var_val = jnp.mean(centered * centered, axis=0)
-    rstd = lax.rsqrt(var_val + LN_EPS)
-
-    def body(c, carry):
+    total = lax.fori_loop(0, n_c, lambda c, acc: acc + o_ref[c], jnp.zeros((n_i, lanes), F32), unroll=16)
+    mean_val = total / n_c
+
+    def body(c, acc):
         base = pl.multiple_of(c * I_STRIDE, 8)
-        norm = (o_ref[c] - mean_val) * rstd
+        centered = o_ref[c] - mean_val
         for t in range(lanes // LANES):
-            s_o[t, pl.ds(base, n_i), :] = norm[:, t * LANES:(t + 1) * LANES]
-        return carry
-    lax.fori_loop(0, n_c, body, 0)
-
-
-def finish_row(i, z_ref, gate_ref, nout_ref, wo_ref, bo_ref, s_o):
+            s_o[t, pl.ds(base, n_i), :] = centered[:, t * LANES:(t + 1) * LANES]
+        return acc + centered * centered
+    square = lax.fori_loop(0, n_c, body, jnp.zeros((n_i, lanes), F32), unroll=16)
+    r_ref[...] = lax.rsqrt(square / n_c + LN_EPS)
+
+
+def finish_row(i, z_ref, gate_ref, nout_ref, wo_ref, bo_ref, s_o, r_ref):
     tiles, rows, _ = s_o.shape
     n_c = rows // I_STRIDE
-    norm = jnp.concatenate([s_o[t, pl.ds(i, n_c, stride=I_STRIDE), :] for t in range(tiles)], axis=1)
-    norm = (norm * nout_ref[0] + nout_ref[1]).astype(BF16)
+    centered = jnp.concatenate([s_o[t, pl.ds(i, n_c, stride=I_STRIDE), :] for t in range(tiles)], axis=1)
+    norm = (centered * r_ref[pl.ds(i, 1), :] * nout_ref[0] + nout_ref[1]).astype(BF16)
     upd = (dot_nn(wo_ref[...], norm) + bo_ref[...]).astype(BF16)
     return (z_ref[i].astype(F32) + gate_ref[i] * upd.astype(F32)).astype(BF16)
 
 
 def middle_kernel(o_ref, zin_ref, gin_ref, nout_ref, wo_ref, bo_ref, u_ref, mask_ref, nin_ref, w_ref, b_ref,
-                  z_out, gate_ref, ab_ref, s_a, s_b, s_o):
+                  z_out, ab_ref, s_a, s_b, s_o, r_ref):
     n_i = zin_ref.shape[0]
-    finish_stats(o_ref, s_o)
+    finish_stats(o_ref, s_o, r_ref)
 
     def body(i, carry):
-        z_mid = finish_row(i, zin_ref, gin_ref, nout_ref, wo_ref, bo_ref, s_o)
+        z_mid = finish_row(i, zin_ref, gin_ref, nout_ref, wo_ref, bo_ref, s_o, r_ref)
         z_new = (z_mid.astype(F32) + u_ref[i].astype(F32)).astype(BF16)
         z_out[i] = z_new
-        project_row(i, z_new.astype(F32), mask_ref[pl.ds(i, 1), :], nin_ref, w_ref, b_ref, gate_ref, (s_a, s_b))
-        return carry
-    lax.fori_loop(0, n_i, body, 0)
+        project_row(i, z_new.astype(F32), mask_ref[pl.ds(i, 1), :], nin_ref, w_ref, b_ref, (s_a, s_b))
+        return carry
+    lax.fori_loop(0, n_i, body, 0, unroll=ROW_UNROLL)
     emit_ab(ab_ref, (s_a, s_b))
 
 
-def end_kernel(o_ref, zin_ref, gin_ref, nout_ref, wo_ref, bo_ref, z_out, s_o):
+def end_kernel(o_ref, zin_ref, gin_ref, nout_ref, wo_ref, bo_ref, z_out, s_o, r_ref):
     n_i = zin_ref.shape[0]
-    finish_stats(o_ref, s_o)
+    finish_stats(o_ref, s_o, r_ref)
 
     def body(i, carry):
-        z_new = finish_row(i, zin_ref, gin_ref, nout_ref, wo_ref, bo_ref, s_o)
+        z_new = finish_row(i, zin_ref, gin_ref, nout_ref, wo_ref, bo_ref, s_o, r_ref)
         z_out[i] = z_new.astype(F32).T.astype(BF16)
         return carry
-    lax.fori_loop(0, n_i, body, 0)
+    lax.fori_loop(0, n_i, body, 0, unroll=ROW_UNROLL)
 
 
 J_BLK = 256
@@ -258,16 +287,16 @@
     pro = ['j', 'j', 'w', 'w', 'w']
     kinds = {'start': ['j'] + pro, 'middle': fin + pro, 'end': fin}[kind]
     scr = pltpu.VMEM((tiles, n_ch * I_STRIDE, LANES), F32)
+    stat = pltpu.VMEM((n_i, J_BLK), F32)
     if kind == 'end':
         out_shape = jax.ShapeDtypeStruct((n_i, cols, n_z), BF16)
         out_specs = pl.BlockSpec((n_i, J_BLK, n_z), lambda j: (0, j, 0))
-        scratch = [scr]
+        scratch = [scr, stat]
     else:
         out_shape = (jax.ShapeDtypeStruct((n_i, n_z, cols), BF16),
-                     jax.ShapeDtypeStruct((n_i, n_z, cols), F32),
                      jax.ShapeDtypeStruct((n_dev, 2, n_ch // n_dev, n_i, cols), BF16))
         out_specs = tuple(blk(s, 'j') for s in out_shape)
-        scratch = [scr, scr] + ([scr] if kind == 'middle' else [])
+        scratch = [scr, scr] + ([scr, stat] if kind == 'middle' else [])
     return pl.pallas_call(
         kernels[kind], grid=(cols // J_BLK,),
         in_specs=[blk(a, k) for a, k in zip(args, kinds)],
@@ -321,33 +350,28 @@
         w_bd = jnp.zeros((layers, n_m, layers, 2 * n_c), BF16)
         for l in range(layers):
             w_bd = w_bd.at[l, :, l].set(opm_w_in[l].reshape(n_m, 2 * n_c))
-        left, right = msa_project(msa_act, opm_norm.astype(F32), w_bd.reshape(layers * n_m, layers * 2 * n_c),
+        sides = msa_project(msa_act, opm_norm.astype(F32), w_bd.reshape(layers * n_m, layers * 2 * n_c),
                                   opm_b_in.astype(F32).reshape(1, -1))
-        chunks = [AG_CHUNKS] + [1] * (layers - 1)
-        gathered = []
-        for l in range(layers):
-            size = n_c // chunks[l]
-            gathered.append([lax.all_gather(right[l, k * size:(k + 1) * size], 'dap', axis=0) for k in range(chunks[l])])
+        left, right = sides[:layers], sides[layers:]
+        gathered = [lax.all_gather(r, 'dap', axis=0, tiled=True).reshape((n_dev,) + r.shape) for r in right]
         updates = []
         for l in range(layers):
             w_t = opm_w_out[l].reshape(n_c, n_c, n_z).transpose(2, 1, 0).reshape(n_z, n_c * n_c)
-            acc, part = None, n_c * n_c // chunks[l]
-            for k in range(chunks[l]):
-                acc = opm_update(left[l], gathered[l][k], w_t[:, k * part:(k + 1) * part], column(opm_b_out[l]), acc,
-                                 last=k == chunks[l] - 1)
-            updates.append(acc)
+            updates.append(opm_update(left[l], gathered[l], w_t, column(opm_b_out[l])))
         z_t = jnp.swapaxes(pair_act, 1, 2)
         fin = None
         for l in range(layers):
-            w_all = jnp.concatenate([tri_w_ab[l].transpose(1, 2, 0), tri_w_gate[l].T[None]], axis=0)
-            b_all = column(jnp.concatenate([tri_b_ab[l], tri_b_gate[l][None]], axis=0))
-            pro = (updates[l], mask_f, column(tri_norm_in[l]), w_all, b_all)
+            w_all = tri_w_ab[l].transpose(1, 2, 0).reshape(-1, n_z)
+            norm_in = column(tri_norm_in[l])
+            pro = (updates[l], mask_f, norm_in, w_all, column(tri_b_ab[l].reshape(-1)))
             if l == 0:
-                z_t, gate, ab = tri_call('start', n_dev, (z_t,) + pro)
+                z_t, ab = tri_call('start', n_dev, (z_t,) + pro)
             else:
-                z_t, gate, ab = tri_call('middle', n_dev, fin + pro)
+                z_t, ab = tri_call('middle', n_dev, fin + pro)
             ab = lax.all_to_all(ab.reshape(n_dev, -1, cols), 'dap', 0, 0, tiled=True).reshape(ab.shape)
-            prod = lax.all_to_all(tri_product(ab), 'dap', 0, 0, tiled=True)
+            prod, z_g = lax.optimization_barrier((tri_product(ab), z_t))
+            gate = gate_call(z_g, norm_in, tri_w_gate[l].T, column(tri_b_gate[l]))
+            prod = lax.all_to_all(prod, 'dap', 0, 0, tiled=True)
             fin = (prod.reshape(-1, n_i, cols), z_t, gate, column(tri_norm_out[l]), tri_w_out[l].T, column(tri_b_out[l]))
         return tri_call('end', n_dev, fin)
 

time: 465 us -> 432 us (0.929)
  Pallas kernels: 141 us -> 108 us
  blocking collectives: 129 us -> 138 us
    pallas_call x3, Pallas kernels: 62.8 us -> 37.5 us  [tri_call(): pl.pallas_call(kernels[kind], grid=(cols // J_BLK,), in_specs=[blk(a, k)...]
    pallas_call x0 -> x2, Pallas kernels: none -> 12.2 us  [gate_call(): pl.pallas_call(gate_kernel, grid=(cols // J_BLK,), in_specs=[row_spec, pl...]
    pallas_call x1, Pallas kernels: 21.6 us -> 10.4 us  [msa_project(): pl.pallas_call(msa_kernel, grid=(seqs // s_blk,), in_specs=[pl.BlockSpec(...]
    all_to_all x2, waiting for transfers between devices: 82.6 us -> 72.7 us  [device_fn(): prod = lax.all_to_all(prod, 'dap', 0, 0, tiled=True)]
    all_to_all x2, blocking collectives: 129 us -> 138 us  [device_fn(): lax.all_to_all(ab.reshape(n_dev, -1, cols), 'dap', 0, 0, tiled=True)]
    pallas_call x2, Pallas kernels: 44.8 us -> 36.5 us  [opm_update(): pl.pallas_call(functools.partial(opm_kernel, 1.0 / seqs, first, last), gr...]
    all_gather x2, waiting for transfers between devices: 54.4 us -> 62.1 us  [device_fn(): lax.all_gather(r, 'dap', axis=0, tiled=True).reshape((n_dev,) + r.shape)]
    convert_element_type x8 -> x12, local copies, waits for them, and re-layouts: 6.13 us -> 9.36 us  [column(): return vec.astype(F32)[..., None]]
  transfers between devices with their start and end apart: 4 -> 4, of which waited for: 3 -> 3; matrix products, arithmetic and copies ran while one was open for 5% -> 4% of each run, Pallas kernels for 15% -> 15%
where the time goes in v3:
time: 432 us
  blocking collectives  138 us (32%)
  waiting for transfers between devices  136 us (31%)
  Pallas kernels  108 us (25%)
  local copies, waits for them, and re-layouts  22.5 us (5%)
  between operations  13.6 us (3%)
  starting transfers between devices  11.7 us (3%)
    all_to_all x2, blocking collectives, device_fn(): lax.all_to_all(ab.reshape(n_dev, -1, cols), 'dap', 0, 0, tiled=True)  138 us
    all_to_all x2, waiting for transfers between devices, device_fn(): prod = lax.all_to_all(prod, 'dap', 0, 0, tiled=True)  72.7 us
    all_gather x2, waiting for transfers between devices, device_fn(): lax.all_gather(r, 'dap', axis=0, tiled=True).reshape((n_dev,) + r.shape)  62.1 us
    pallas_call x3, Pallas kernels, tri_call(): pl.pallas_call(kernels[kind], grid=(cols // J_BLK,), in_specs=[blk(a, k)...  37.5 us
    pallas_call x2, Pallas kernels, opm_update(): pl.pallas_call(functools.partial(opm_kernel, 1.0 / seqs, first, last), gr...  36.5 us
    pallas_call x2, Pallas kernels, gate_call(): pl.pallas_call(gate_kernel, grid=(cols // J_BLK,), in_specs=[row_spec, pl...  12.2 us
    all_to_all x2, starting transfers between devices, device_fn(): prod = lax.all_to_all(prod, 'dap', 0, 0, tiled=True)  11.6 us
    pallas_call x2, Pallas kernels, tri_product(): pl.pallas_call(product_kernel, grid=(n_cl,), in_specs=[pl.BlockSpec((n_de...  11.3 us
  transfers between devices with their start and end apart: 4, of which 3 were waited for; matrix products, arithmetic and copies ran while one was open for 4% of the time, Pallas kernels for 15%

profile of v3, /device:TPU:103, one launch (start us, length us, event | category | flops | bytes accessed | tf_op | source)
XLA Modules:
  0.0 431.5 jit_solution(6295429822445532719)
XLA Ops:
  6.6 1.4 reshape.286.bias_ref
  8.0 1.3 convert_element_type.163.norm_ref
  9.3 0.8 fusion.3
  10.3 0.9 scatter.9
  12.0 10.4 %msa_project.1 = (bf16[512,512]{1,0:T(8,128)(2,1)}, bf16[512,512]{1,0:T(8,128)(2,1)}, bf16[32,16,512]{2,1,0:T(8,128)(2,1)}, bf16[32,16,512]{2,1,0:T(8,128)(2,1)}) custom-call(bf16[512,16,256]{2,1,0:T(8,128)(2,1)} %m_ref.1, f32[2,2,256]{2,1,0:T(2,128)} %convert_element_type.163.norm_ref, bf16[512,128]{1,0:T(8,128)(2,1)} %copy.91.w_ref, ...), custom_call_target="tpu_custom_call" | custom-call | flops 536870912 | bytes 6291456 | tf_op jit(solution)/shard_map/msa_project/pallas_call | solution.py:69
  24.6 0.8 copy.96.nin_ref
  25.4 0.9 copy.97.b_ref
  26.3 0.8 copy.95
  27.3 0.8 copy.93.w_ref
  28.1 2.6 copy.88
  30.7 62.1 %all-gather.3.cloned.1.call-done = bf16[1024,16,512]{2,1,0:T(8,128)(2,1)} async-done(((bf16[32,16,512]{2,1,0:T(8,128)(2,1)}), bf16[1024,16,512]{2,1,0:T(8,128)(2,1)}) %all-gather.3.cloned.1.call-update) | async-done | bytes 16777232 | tf_op jit(solution)/shard_map/all_gather | solution.py:356
  92.8 18.3 %opm_update.2.u_ref = bf16[16,128,512]{2,1,0:T(8,128)(2,1)} custom-call(bf16[512,512]{1,0:T(8,128)(2,1)} %get-tuple-element.41.a_ref, bf16[32,32,16,512]{3,2,1,0:T(8,128)(2,1)} %bitcast.100, bf16[128,1024]{1,0:T(8,128)(2,1)} %copy.93.w_ref, f32[128,1]{1,0:T(8,128)} %copy.94.bias_ref), custom_call_target="tpu_custom_call" | custom-call | flops 10737418240 | bytes 18874368 | tf_op jit(solution)/shard_map/opm_update/pallas_call | solution.py:126
  111.1 11.0 %tri_start.1 = (bf16[16,128,512]{2,1,0:T(8,128)(2,1)}, bf16[32,2,4,16,512]{4,3,2,1,0:T(8,128)(2,1)}) custom-call(bf16[16,128,512]{2,1,0:T(8,128)(2,1)} %bitcast.82, bf16[16,128,512]{2,1,0:T(8,128)(2,1)} %opm_update.2.u_ref, f32[16,512]{1,0:T(8,128)} %convert_element_type.166.mask_ref, f32[2,128,1]{2,1,0:T(8,128)} %copy.96.nin_ref, ...), custom_call_target="tpu_custom_call" | custom-call | flops 1610612736 | bytes 16777216 | tf_op jit(solution)/shard_map/tri_start/pallas_call | solution.py:300
  122.1 83.1 %all_to_all.20 = bf16[32,128,512]{2,1,0:T(8,128)(2,1)} all-to-all(bf16[32,128,512]{2,1,0:T(8,128)(2,1)} %bitcast.81), channel_id=1, replica_groups=mesh['batch'=1,'dap'=32] {'dap'}, dimensions={0} | all-to-all | bytes 8388608 | tf_op jit(solution)/shard_map/all_to_all | solution.py:371
  205.2 5.6 %tri_product.2 = f32[32,4,16,512]{3,2,1,0:T(8,128)} custom-call(bf16[32,2,4,16,512]{4,3,2,1,0:T(8,128)(2,1)} %bitcast.78), custom_call_target="tpu_custom_call" | custom-call | flops 1073741824 | bytes 8388608 | tf_op jit(solution)/shard_map/tri_product/pallas_call | solution.py:323
  210.8 5.5 %all-to-all-start.1 = ((f32[32,4,16,512]{3,2,1,0:T(8,128)}), f32[32,4,16,512]{3,2,1,0:T(8,128)}, u32[]{:S(2)}, u32[]{:S(2)}) async-start(f32[32,4,16,512]{3,2,1,0:T(8,128)} %tri_product.2), calls=%async_computation.1 | async-start | bytes 8388608 | tf_op jit(solution)/shard_map/all_to_all | solution.py:374
  220.0 0.8 copy.108.nin_ref
  220.8 0.8 copy.106.nout_ref
  221.6 0.9 copy.109.b_ref
  222.5 0.8 copy.105
  223.4 0.9 copy.103.w_ref
  224.2 18.3 %opm_update.3.u_ref = bf16[16,128,512]{2,1,0:T(8,128)(2,1)} custom-call(bf16[512,512]{1,0:T(8,128)(2,1)} %get-tuple-element.47.a_ref, bf16[32,32,16,512]{3,2,1,0:T(8,128)(2,1)} %bitcast.99, bf16[128,1024]{1,0:T(8,128)(2,1)} %copy.103.w_ref, f32[128,1]{1,0:T(8,128)} %copy.104.bias_ref), custom_call_target="tpu_custom_call" | custom-call | flops 10737418240 | bytes 18874368 | tf_op jit(solution)/shard_map/opm_update/pallas_call | solution.py:126
  242.5 6.1 %tri_gate.2.gin_ref = f32[16,128,512]{2,1,0:T(8,128)} custom-call(bf16[16,128,512]{2,1,0:T(8,128)(2,1)} %get-tuple-element.46.z_ref.zin_ref, f32[2,128,1]{2,1,0:T(8,128)} %copy.96.nin_ref, bf16[128,128]{1,0:T(8,128)(2,1)} %bitcast.91, f32[128,1]{1,0:T(8,128)} %copy.100.b_ref), custom_call_target="tpu_custom_call" | custom-call | flops 1610612736 | bytes 6291456 | tf_op jit(solution)/shard_map/tri_gate/pallas_call | solution.py:181
  248.6 25.1 %all-to-all-done.1 = f32[32,4,16,512]{3,2,1,0:T(8,128)} async-done(((f32[32,4,16,512]{3,2,1,0:T(8,128)}), f32[32,4,16,512]{3,2,1,0:T(8,128)}, u32[]{:S(2)}, u32[]{:S(2)}) %all-to-all-start.1) | async-done | bytes 4194336 | tf_op jit(solution)/shard_map/all_to_all | solution.py:374
  273.7 17.3 %tri_middle.1 = (bf16[16,128,512]{2,1,0:T(8,128)(2,1)}, bf16[32,2,4,16,512]{4,3,2,1,0:T(8,128)(2,1)}) custom-call(f32[128,16,512]{2,1,0:T(8,128)} %bitcast.15.o_ref, bf16[16,128,512]{2,1,0:T(8,128)(2,1)} %get-tuple-element.46.z_ref.zin_ref, f32[16,128,512]{2,1,0:T(8,128)} %tri_gate.2.gin_ref, f32[2,128,1]{2,1,0:T(8,128)} %copy.106.nout_ref, ...), custom_call_target="tpu_custom_call" | custom-call | flops 1610612736 | bytes 16777216 | tf_op jit(solution)/shard_map/tri_middle/pallas_call | solution.py:300
  291.0 55.3 %all_to_all.21 = bf16[32,128,512]{2,1,0:T(8,128)(2,1)} all-to-all(bf16[32,128,512]{2,1,0:T(8,128)(2,1)} %bitcast.80), channel_id=1, replica_groups=mesh['batch'=1,'dap'=32] {'dap'}, dimensions={0} | all-to-all | bytes 8388608 | tf_op jit(solution)/shard_map/all_to_all | solution.py:371
  346.3 5.6 %tri_product.3 = f32[32,4,16,512]{3,2,1,0:T(8,128)} custom-call(bf16[32,2,4,16,512]{4,3,2,1,0:T(8,128)(2,1)} %bitcast.79), custom_call_target="tpu_custom_call" | custom-call | flops 1073741824 | bytes 8388608 | tf_op jit(solution)/shard_map/tri_product/pallas_call | solution.py:323
  352.0 6.1 %all-to-all-start.3 = ((f32[32,4,16,512]{3,2,1,0:T(8,128)}), f32[32,4,16,512]{3,2,1,0:T(8,128)}, u32[]{:S(2)}, u32[]{:S(2)}) async-start(f32[32,4,16,512]{3,2,1,0:T(8,128)} %tri_product.3), calls=%async_computation.3 | async-start | bytes 8388608 | tf_op jit(solution)/shard_map/all_to_all | solution.py:374
  361.0 0.8 copy.114.nout_ref
  361.8 6.1 %tri_gate.3.gin_ref = f32[16,128,512]{2,1,0:T(8,128)} custom-call(bf16[16,128,512]{2,1,0:T(8,128)(2,1)} %get-tuple-element.52.z_ref.zin_ref, f32[2,128,1]{2,1,0:T(8,128)} %copy.108.nin_ref, bf16[128,128]{1,0:T(8,128)(2,1)} %bitcast.93, f32[128,1]{1,0:T(8,128)} %copy.112.b_ref), custom_call_target="tpu_custom_call" | custom-call | flops 1610612736 | bytes 6291456 | tf_op jit(solution)/shard_map/tri_gate/pallas_call | solution.py:181
  367.8 47.6 %all-to-all-done.3 = f32[32,4,16,512]{3,2,1,0:T(8,128)} async-done(((f32[32,4,16,512]{3,2,1,0:T(8,128)}), f32[32,4,16,512]{3,2,1,0:T(8,128)}, u32[]{:S(2)}, u32[]{:S(2)}) %all-to-all-start.3) | async-done | bytes 4194336 | tf_op jit(solution)/shard_map/all_to_all | solution.py:374
  415.5 9.2 %tri_end.1 = bf16[16,512,128]{2,1,0:T(8,128)(2,1)} custom-call(f32[128,16,512]{2,1,0:T(8,128)} %bitcast.35.o_ref, bf16[16,128,512]{2,1,0:T(8,128)(2,1)} %get-tuple-element.52.z_ref.zin_ref, f32[16,128,512]{2,1,0:T(8,128)} %tri_gate.3.gin_ref, f32[2,128,1]{2,1,0:T(8,128)} %copy.114.nout_ref, bf16[128,128]{1,0:T(8,128)(2,1)} %bitcast.92, f32[128,1]{1,0:T(8,128)} %copy.115.bo_ref), custom_call_target="tpu_custom_call" | custom-call | flops 1610612736 | bytes 16777216 | tf_op jit(solution)/shard_map/tri_end/pallas_call | solution.py:300
  (57 shorter events, 10.2 us)
Async XLA Ops:
  6.5 16.7 %copy-start.5 = (s32[16,512]{1,0:T(8,128)S(1)}, s32[16,512]{1,0:T(8,128)}, u32[]{:S(2)}) copy-start(s32[16,512]{1,0:T(8,128)} %param.21) | copy-start | bytes 98308
  6.5 17.3 %copy-start.7 = (bf16[2,128]{1,0:T(2,128)(2,1)S(1)}, bf16[2,128]{1,0:T(2,128)(2,1)}, u32[]{:S(2)}) copy-start(bf16[2,128]{1,0:T(2,128)(2,1)} %param.27) | copy-start | bytes 1540
  6.6 18.0 %copy-start.10 = (bf16[2,2,128]{2,1,0:T(2,128)(2,1)S(1)}, bf16[2,2,128]{2,1,0:T(2,128)(2,1)}, u32[]{:S(2)}) copy-start(bf16[2,2,128]{2,1,0:T(2,128)(2,1)} %param.28) | copy-start | bytes 3076
  6.6 18.8 %copy-start.6 = (bf16[2,4,128]{2,1,0:T(4,128)(2,1)S(1)}, bf16[2,4,128]{2,1,0:T(4,128)(2,1)}, u32[]{:S(2)}) copy-start(bf16[2,4,128]{2,1,0:T(4,128)(2,1)} %param.30) | copy-start | bytes 6148
  6.6 19.7 %copy-start.2 = (bf16[2,128,4,128]{3,2,1,0:T(4,128)(2,1)S(1)}, bf16[2,128,4,128]{3,2,1,0:T(4,128)(2,1)}, u32[]{:S(2)}) copy-start(bf16[2,128,4,128]{3,2,1,0:T(4,128)(2,1)} %param.29) | copy-start | bytes 786436
  6.6 20.6 %copy-start.1 = (bf16[2,1024,128]{2,1,0:T(8,128)(2,1)S(1)}, bf16[2,1024,128]{2,1,0:T(8,128)(2,1)}, u32[]{:S(2)}) copy-start(bf16[2,1024,128]{2,1,0:T(8,128)(2,1)} %param.26) | copy-start | bytes 1572868
  6.6 86.2 %all-gather.3.cloned.1.call-start = ((), (), s32[]{:S(2)}) async-start(), calls=%async_computation.4 | async-start | bytes 17301504 | tf_op jit(solution)/shard_map/all_gather | solution.py:356
  12.0 16.1 %copy-start = (bf16[16,512,128]{2,1,0:T(8,128)(2,1)S(1)}, bf16[16,512,128]{2,1,0:T(8,128)(2,1)}, u32[]{:S(2)}) copy-start(bf16[16,512,128]{2,1,0:T(8,128)(2,1)} %param.20) | copy-start | bytes 6291460
  22.4 201.8 %all-gather.5.cloned.1.call-start = ((), (), s32[]{:S(2)}) async-start(), calls=%async_computation.5 | async-start | bytes 17301504 | tf_op jit(solution)/shard_map/all_gather | solution.py:356
  210.8 6.2 %copy-start.8 = (bf16[2,128]{1,0:T(2,128)(2,1)S(1)}, bf16[2,128]{1,0:T(2,128)(2,1)}, u32[]{:S(2)}) copy-start(bf16[2,128]{1,0:T(2,128)(2,1)} %param.35) | copy-start | bytes 1540
  210.8 7.0 %copy-start.9 = (bf16[2,128]{1,0:T(2,128)(2,1)S(1)}, bf16[2,128]{1,0:T(2,128)(2,1)}, u32[]{:S(2)}) copy-start(bf16[2,128]{1,0:T(2,128)(2,1)} %param.32) | copy-start | bytes 1540
  210.8 7.7 %copy-start.3 = (bf16[2,128,128]{2,1,0:T(8,128)(2,1)S(1)}, bf16[2,128,128]{2,1,0:T(8,128)(2,1)}, u32[]{:S(2)}) copy-start(bf16[2,128,128]{2,1,0:T(8,128)(2,1)} %param.31) | copy-start | bytes 196612
  210.8 8.5 %copy-start.4 = (bf16[2,128,128]{2,1,0:T(8,128)(2,1)S(1)}, bf16[2,128,128]{2,1,0:T(8,128)(2,1)}, u32[]{:S(2)}) copy-start(bf16[2,128,128]{2,1,0:T(8,128)(2,1)} %param.34) | copy-start | bytes 196612
  210.8 10.0 %copy-start.11 = (bf16[2,2,128]{2,1,0:T(2,128)(2,1)S(1)}, bf16[2,2,128]{2,1,0:T(2,128)(2,1)}, u32[]{:S(2)}) copy-start(bf16[2,2,128]{2,1,0:T(2,128)(2,1)} %param.33) | copy-start | bytes 3076
  210.8 62.9 %all-to-all-start.1 = ((f32[32,4,16,512]{3,2,1,0:T(8,128)}), f32[32,4,16,512]{3,2,1,0:T(8,128)}, u32[]{:S(2)}, u32[]{:S(2)}) async-start(f32[32,4,16,512]{3,2,1,0:T(8,128)} %tri_product.2), calls=%async_computation.1 | async-start | bytes 8388608 | tf_op jit(solution)/shard_map/all_to_all | solution.py:374
  352.0 63.5 %all-to-all-start.3 = ((f32[32,4,16,512]{3,2,1,0:T(8,128)}), f32[32,4,16,512]{3,2,1,0:T(8,128)}, u32[]{:S(2)}, u32[]{:S(2)}) async-start(f32[32,4,16,512]{3,2,1,0:T(8,128)} %tri_product.3), calls=%async_computation.3 | async-start | bytes 8388608 | tf_op jit(solution)/shard_map/all_to_all | solution.py:374
Sparse Core Ops, SparseCore 0:
  22.5 70.2 all-gather.2
  94.9 109.9 all-gather.4

commit v4 on v3

--- a/solution.py
+++ b/solution.py
@@ -143,6 +143,207 @@
     )(a_t, b_all, w_t, bias, *(() if first else (acc,)))
 
 
+MESH_ID = pl.DeviceIdType.MESH
+AG_UNITS = 4
+
+
+class RingGather:
+    def __init__(self, n, axis, src_ref, out_ref, r_sem, p_sem, s_sem, l_sem):
+        self.n, self.side, self.axis = n, math.isqrt(n // 2), axis
+        self.src, self.out = src_ref, out_ref
+        self.r_sem, self.p_sem, self.s_sem, self.l_sem = r_sem, p_sem, s_sem, l_sem
+        me = lax.axis_index(axis)
+        self.me, self.core = me, me % 2
+        self.x, self.y = (me // 2) % self.side, me // (2 * self.side)
+        self.size = src_ref.shape[0] // AG_UNITS
+
+    def at(self, u, k1, k2, other=False):
+        kx, ky = (k1, k2) if u < AG_UNITS // 2 else (k2, k1)
+        core = 1 - self.core if other else self.core
+        return (((self.y + ky) % self.side) * self.side + (self.x + kx) % self.side) * 2 + core
+
+    def neighbours(self):
+        last = self.side - 1
+        return [self.at(0, 1, 0), self.at(0, last, 0), self.at(0, 0, 1), self.at(0, 0, last), self.at(0, 0, 0, True)]
+
+    def barrier(self):
+        sem = pltpu.get_barrier_semaphore()
+        peers = self.neighbours()
+        for p in peers:
+            pl.semaphore_signal(sem, inc=1, device_id={self.axis: p}, device_id_type=MESH_ID)
+        pl.semaphore_wait(sem, len(peers))
+
+    def copy(self, u, k1, k2, way):
+        rows = pl.ds(u * self.size, self.size)
+        owner = self.at(u, k1, k2)
+        src = self.src.at[rows] if (k1, k2) == (0, 0) else self.out.at[owner, rows]
+        step = (1, self.side - 1)[way % 2]
+        if way < 2:
+            dest, rk, sems = self.at(u, step, 0), ((k1 - step) % self.side, k2), self.r_sem
+        elif way < 4:
+            dest, rk, sems = self.at(u, 0, step), (k1, (k2 - step) % self.side), self.r_sem
+        else:
+            dest, rk, sems = self.at(u, 0, 0, True), (k1, k2), self.p_sem
+        return pltpu.make_async_remote_copy(src, self.out.at[owner, rows], self.s_sem.at[u, k1, k2, way], sems.at[u, rk[0], rk[1]],
+                                            device_id={self.axis: dest}, device_id_type=MESH_ID)
+
+    def ways(self, u, k1, k2):
+        last = self.side - 1
+        plus = u % 2 == 0
+        out = []
+        if k2 == 0:
+            if k1 == 0:
+                out += [0, 1]
+            elif k1 == last and plus:
+                out.append(0)
+            elif k1 == 1 and not plus:
+                out.append(1)
+            out += [2, 3]
+        elif k2 == last and plus:
+            out.append(2)
+        elif k2 == 1 and not plus:
+            out.append(3)
+        return out + [4]
+
+    def arrived(self, u, k1, k2, sems, other=False):
+        rows = pl.ds(u * self.size, self.size)
+        dst = self.out.at[self.at(u, k1, k2, other), rows]
+        pltpu.make_async_remote_copy(dst, dst, self.s_sem.at[u, k1, k2, 4], sems.at[u, k1, k2],
+                                     device_id={self.axis: self.at(0, 0, 0, True)}, device_id_type=MESH_ID).wait_recv()
+
+    def steps(self):
+        last = self.side - 1
+        units = range(AG_UNITS)
+        own = pltpu.make_async_copy(self.src, self.out.at[self.me], self.l_sem)
+
+        def begin():
+            own.start()
+            for pair in ((0, 1), (2, 3), (4,)):
+                for u in units:
+                    for way in pair:
+                        self.copy(u, 0, 0, way).start()
+
+        def relay(k1, k2):
+            for u in units:
+                self.arrived(u, k1, k2, self.r_sem)
+                for way in self.ways(u, k1, k2):
+                    self.copy(u, k1, k2, way).start()
+
+        def finish():
+            for k1 in range(self.side):
+                for k2 in range(self.side):
+                    for u in units:
+                        self.arrived(u, k1, k2, self.p_sem, True)
+            for k1 in range(self.side):
+                for k2 in range(self.side):
+                    for u in units:
+                        for way in self.ways(u, k1, k2):
+                            self.copy(u, k1, k2, way).wait_send()
+            own.wait()
+        order = [(last, 0), (1, 0), (0, last), (0, 1), (2, 0)]
+        order += [(k1, k2) for k1 in (last, 1, 2) for k2 in (last, 1)]
+        order += [(k1, 2) for k1 in (0, last, 1, 2)]
+        return [begin] + [functools.partial(relay, *o) for o in order] + [finish]
+
+
+def gather_kernel(n, axis, src_ref, out_ref, *sems):
+    ring = RingGather(n, axis, src_ref, out_ref, *sems)
+    ring.barrier()
+    for step in ring.steps():
+        step()
+
+
+def gather_scratch(side):
+    dma = pltpu.SemaphoreType.DMA
+    return [dma((AG_UNITS, side, side)), dma((AG_UNITS, side, side)), dma((AG_UNITS, side, side, 5)), dma]
+
+
+def ring_gather(block, n, axis, cid):
+    side = math.isqrt(n // 2)
+    assert 2 * side * side == n and side == 4
+    return pl.pallas_call(
+        functools.partial(gather_kernel, n, axis),
+        out_shape=jax.ShapeDtypeStruct((n,) + block.shape, block.dtype),
+        in_specs=[pl.BlockSpec(memory_space=pl.ANY)], out_specs=pl.BlockSpec(memory_space=pl.ANY),
+        scratch_shapes=gather_scratch(side),
+        compiler_params=pltpu.CompilerParams(collective_id=cid, has_side_effects=True),
+        name='ring_gather',
+    )(block)
+
+
+def gather_opm_kernel(n, axis, inv_s, src_ref, a_ref, b_ref, w_ref, bias_ref, out_ref, upd_ref, buf, q_ref, b_sem, *sems):
+    ring = RingGather(n, axis, src_ref, out_ref, *sems)
+    _, dev_blk, d_blk, j_loc, seqs = buf.shape
+    n_i, _, j_blk = q_ref.shape
+    n_c = a_ref.shape[0] // n_i
+    parts = b_ref.shape[1] // d_blk
+    total = (b_ref.shape[0] // dev_blk) * parts
+
+    def load(k):
+        j, part = k // parts, k % parts
+        return pltpu.make_async_copy(b_ref.at[pl.ds(j * dev_blk, dev_blk), pl.ds(part * d_blk, d_blk)], buf.at[k % 2], b_sem.at[k % 2])
+
+    def outer(k):
+        if k + 1 < total:
+            load(k + 1).start()
+        load(k).wait()
+
+        def body(d, carry):
+            rhs = buf[k % 2, :, d].reshape(dev_blk * j_loc, seqs)
+            prod = (dot_nt(a_ref[...], rhs) * inv_s).astype(BF16)
+            base = pl.multiple_of(((k % parts) * d_blk + d) * n_c, n_c)
+            q_ref[:, pl.ds(base, n_c), :] = prod.reshape(n_i, n_c, j_blk)
+            return carry
+        lax.fori_loop(0, d_blk, body, 0, unroll=2)
+
+    def contract(j, low, high):
+        def body(i, carry):
+            upd = dot_nn(w_ref[...], q_ref[i]) + bias_ref[...]
+            upd_ref[i, :, j * j_blk:(j + 1) * j_blk] = upd.astype(BF16)
+            return carry
+        lax.fori_loop(low, high, body, 0, unroll=4)
+    pieces = []
+    for k in range(total):
+        pieces.append(functools.partial(outer, k))
+        if k % parts == parts - 1:
+            for half in range(2):
+                pieces.append(functools.partial(contract, k // parts, half * n_i // 2, (half + 1) * n_i // 2))
+    load(0).start()
+    ring.barrier()
+    steps = ring.steps()
+    for k, step in enumerate(steps[:-1]):
+        step()
+        if k < len(pieces):
+            pieces[k]()
+    for piece in pieces[len(steps) - 1:]:
+        piece()
+    steps[-1]()
+
+
+def gather_with_opm(block, n, axis, cid, a_t, b_all, w_t, bias):
+    n_dev, n_d, j_loc, seqs = b_all.shape
+    n_z = w_t.shape[0]
+    n_c = w_t.shape[1] // n_d
+    n_i = a_t.shape[0] // n_c
+    cols = n_dev * j_loc
+    j_blk = 2 * LANES
+    d_blk = math.gcd(n_d, 8)
+    side = math.isqrt(n // 2)
+    assert 2 * side * side == n and side == 4
+    any_spec = pl.BlockSpec(memory_space=pl.ANY)
+    vmem_spec = pl.BlockSpec(memory_space=pltpu.VMEM)
+    return pl.pallas_call(
+        functools.partial(gather_opm_kernel, n, axis, 1.0 / seqs),
+        out_shape=(jax.ShapeDtypeStruct((n,) + block.shape, block.dtype), jax.ShapeDtypeStruct((n_i, n_z, cols), BF16)),
+        in_specs=[any_spec, vmem_spec, any_spec, vmem_spec, vmem_spec], out_specs=(any_spec, vmem_spec),
+        scratch_shapes=[pltpu.VMEM((2, j_blk // j_loc, d_blk, j_loc, seqs), BF16), pltpu.VMEM((n_i, n_d * n_c, j_blk), BF16),
+                        pltpu.SemaphoreType.DMA((2,))] + gather_scratch(side),
+        compiler_params=pltpu.CompilerParams(collective_id=cid, has_side_effects=True),
+        cost_estimate=pl.CostEstimate(flops=2 * a_t.shape[0] * seqs * cols * n_d * 4, bytes_accessed=2 * b_all.size, transcendentals=0),
+        name='ring_gather_opm',
+    )(block, a_t, b_all, w_t, bias)
+
+
 def norm_columns(x_f32, gain, offset):
     mean_val = jnp.mean(x_f32, axis=0, keepdims=True)
     centered = x_f32 - mean_val
@@ -353,11 +554,16 @@
         sides = msa_project(msa_act, opm_norm.astype(F32), w_bd.reshape(layers * n_m, layers * 2 * n_c),
                                   opm_b_in.astype(F32).reshape(1, -1))
         left, right = sides[:layers], sides[layers:]
-        gathered = [lax.all_gather(r, 'dap', axis=0, tiled=True).reshape((n_dev,) + r.shape) for r in right]
+        opm_w = [opm_w_out[l].reshape(n_c, n_c, n_z).transpose(2, 1, 0).reshape(n_z, n_c * n_c) for l in range(layers)]
+        gathered = ring_gather(right[0], n_dev, 'dap', 0)
         updates = []
         for l in range(layers):
-            w_t = opm_w_out[l].reshape(n_c, n_c, n_z).transpose(2, 1, 0).reshape(n_z, n_c * n_c)
-            updates.append(opm_update(left[l], gathered[l], w_t, column(opm_b_out[l])))
+            rest = (left[l], gathered, opm_w[l], column(opm_b_out[l]))
+            if l + 1 < layers:
+                gathered, update = gather_with_opm(right[l + 1], n_dev, 'dap', l + 1, *rest)
+            else:
+                update = opm_update(*rest)
+            updates.append(update)
         z_t = jnp.swapaxes(pair_act, 1, 2)
         fin = None
         for l in range(layers):

time: 432 us -> 422 us (0.977)
  Pallas kernels: 108 us -> 199 us
  waiting for transfers between devices: 136 us -> 72.7 us
  blocking collectives: 138 us -> 113 us
  between operations: 13.6 us -> 0.2 us
    pallas_call x0 -> x2, Pallas kernels: none -> 109 us  [the longest x1 54.5 us: gather_with_opm(): pl.pallas_call(functools.partial(gather_opm_kernel, n, axis, 1.0 / seqs),...]
    all_gather x2 -> x0, waiting for transfers between devices: 62.1 us -> none  [device_fn(): lax.all_gather(r, 'dap', axis=0, tiled=True).reshape((n_dev,) + r.shape)]
    all_to_all x2, blocking collectives: 138 us -> 113 us  [device_fn(): lax.all_to_all(ab.reshape(n_dev, -1, cols), 'dap', 0, 0, tiled=True)]
    pallas_call x2 -> x1, Pallas kernels: 36.5 us -> 18.2 us  [opm_update(): pl.pallas_call(functools.partial(opm_kernel, 1.0 / seqs, first, last), gr...]
  transfers between devices with their start and end apart: 4 -> 2, of which waited for: 3 -> 2; matrix products, arithmetic and copies ran while one was open for 4% -> 3% of each run, Pallas kernels for 15% -> 7%
where the time goes in v4:
time: 422 us; the launch traced here: 421 us
  Pallas kernels  199 us (47%)
  blocking collectives  113 us (27%)
  waiting for transfers between devices  72.7 us (17%)
  local copies, waits for them, and re-layouts  22.4 us (5%)
  starting transfers between devices  12.4 us (3%)
    all_to_all x2, blocking collectives, device_fn(): lax.all_to_all(ab.reshape(n_dev, -1, cols), 'dap', 0, 0, tiled=True)  113 us
    all_to_all x2, waiting for transfers between devices, device_fn(): prod = lax.all_to_all(prod, 'dap', 0, 0, tiled=True)  72.7 us
    pallas_call x1, Pallas kernels, gather_with_opm(): pl.pallas_call(functools.partial(gather_opm_kernel, n, axis, 1.0 / seqs),...  54.5 us
    pallas_call x1, Pallas kernels, ring_gather(): pl.pallas_call(functools.partial(gather_kernel, n, axis), out_shape=jax.S...  54.5 us
    pallas_call x3, Pallas kernels, tri_call(): pl.pallas_call(kernels[kind], grid=(cols // J_BLK,), in_specs=[blk(a, k)...  37.6 us
    pallas_call x1, Pallas kernels, opm_update(): pl.pallas_call(functools.partial(opm_kernel, 1.0 / seqs, first, last), gr...  18.2 us
    all_to_all x2, starting transfers between devices, device_fn(): prod = lax.all_to_all(prod, 'dap', 0, 0, tiled=True)  12.4 us
    pallas_call x2, Pallas kernels, gate_call(): pl.pallas_call(gate_kernel, grid=(cols // J_BLK,), in_specs=[row_spec, pl...  12.2 us
  transfers between devices with their start and end apart: 2, of which 2 were waited for; matrix products, arithmetic and copies ran while one was open for 3% of the time, Pallas kernels for 7%

profile of v4, /device:TPU:103, one launch (start us, length us, event | category | flops | bytes accessed | tf_op | source)
XLA Modules:
  0.0 421.0 jit_solution(16683566741067837803)
XLA Ops:
  0.0 0.8 fusion.3
  1.0 0.9 scatter.9
  2.7 1.3 convert_element_type.163.norm_ref
  4.0 1.3 reshape.278.bias_ref
  5.3 10.1 %msa_project.1 = (bf16[512,512]{1,0:T(8,128)(2,1)}, bf16[512,512]{1,0:T(8,128)(2,1)}, bf16[32,16,512]{2,1,0:T(8,128)(2,1)}, bf16[32,16,512]{2,1,0:T(8,128)(2,1)}) custom-call(bf16[512,16,256]{2,1,0:T(8,128)(2,1)} %m_ref.1, f32[2,2,256]{2,1,0:T(2,128)} %convert_element_type.163.norm_ref, bf16[512,128]{1,0:T(8,128)(2,1)} %copy.63.w_ref, ...), custom_call_target="tpu_custom_call" | custom-call | flops 536870912 | bytes 6291456 | tf_op jit(solution)/shard_map/msa_project/pallas_call | solution.py:69
  15.4 54.5 %ring_gather.1.b_ref = bf16[32,32,16,512]{3,2,1,0:T(8,128)(2,1)} custom-call(bf16[32,16,512]{2,1,0:T(8,128)(2,1)} %get-tuple-element.45.src_ref), custom_call_target="tpu_custom_call" | custom-call | tf_op jit(solution)/shard_map/ring_gather/pallas_call | solution.py:264
  70.1 0.8 copy.65.w_ref
  71.7 0.8 copy.68.nin_ref
  72.6 0.8 copy.67
  73.4 0.9 copy.69.b_ref
  74.9 2.6 copy.60
  77.5 54.5 %ring_gather_opm.1 = (bf16[32,32,16,512]{3,2,1,0:T(8,128)(2,1)}, bf16[16,128,512]{2,1,0:T(8,128)(2,1)}) custom-call(bf16[32,16,512]{2,1,0:T(8,128)(2,1)} %get-tuple-element.43.src_ref, bf16[512,512]{1,0:T(8,128)(2,1)} %get-tuple-element.44.a_ref, bf16[32,32,16,512]{3,2,1,0:T(8,128)(2,1)} %ring_gather.1.b_ref, bf16[128,1024]{1,0:T(8,128)(2,1)} %copy.65.w_ref, ...), custom_call_target="tpu_custom_call" | custom-call | flops 34359738368 | bytes 16777216 | tf_op jit(solution)/shard_map/ring_gather_opm/pallas_call | solution.py:335
  131.9 11.0 %tri_start.1 = (bf16[16,128,512]{2,1,0:T(8,128)(2,1)}, bf16[32,2,4,16,512]{4,3,2,1,0:T(8,128)(2,1)}) custom-call(bf16[16,128,512]{2,1,0:T(8,128)(2,1)} %bitcast.80, bf16[16,128,512]{2,1,0:T(8,128)(2,1)} %get-tuple-element.46.u_ref, f32[16,512]{1,0:T(8,128)} %convert_element_type.166.mask_ref, f32[2,128,1]{2,1,0:T(8,128)} %copy.68.nin_ref, ...), custom_call_target="tpu_custom_call" | custom-call | flops 1610612736 | bytes 16777216 | tf_op jit(solution)/shard_map/tri_start/pallas_call | solution.py:501
  143.0 57.4 %all_to_all.20 = bf16[32,128,512]{2,1,0:T(8,128)(2,1)} all-to-all(bf16[32,128,512]{2,1,0:T(8,128)(2,1)} %bitcast.79), channel_id=1, replica_groups=mesh['batch'=1,'dap'=32] {'dap'}, dimensions={0} | all-to-all | bytes 8388608 | tf_op jit(solution)/shard_map/all_to_all | solution.py:577
  200.4 5.8 %tri_product.2 = f32[32,4,16,512]{3,2,1,0:T(8,128)} custom-call(bf16[32,2,4,16,512]{4,3,2,1,0:T(8,128)(2,1)} %bitcast.76), custom_call_target="tpu_custom_call" | custom-call | flops 1073741824 | bytes 8388608 | tf_op jit(solution)/shard_map/tri_product/pallas_call | solution.py:524
  206.2 6.3 %all-to-all-start.1 = ((f32[32,4,16,512]{3,2,1,0:T(8,128)}), f32[32,4,16,512]{3,2,1,0:T(8,128)}, u32[]{:S(2)}, u32[]{:S(2)}) async-start(f32[32,4,16,512]{3,2,1,0:T(8,128)} %tri_product.2), calls=%async_computation.1 | async-start | bytes 8388608 | tf_op jit(solution)/shard_map/all_to_all | solution.py:580
  214.1 0.9 copy.75.w_ref
  215.7 0.8 copy.80.nin_ref
  216.5 0.8 copy.77
  217.2 0.9 copy.81.b_ref
  218.1 0.8 copy.78.nout_ref
  220.4 18.2 %opm_update.1.u_ref = bf16[16,128,512]{2,1,0:T(8,128)(2,1)} custom-call(bf16[512,512]{1,0:T(8,128)(2,1)} %get-tuple-element.51.a_ref, bf16[32,32,16,512]{3,2,1,0:T(8,128)(2,1)} %get-tuple-element.52.b_ref, bf16[128,1024]{1,0:T(8,128)(2,1)} %copy.75.w_ref, f32[128,1]{1,0:T(8,128)} %copy.76.bias_ref), custom_call_target="tpu_custom_call" | custom-call | flops 10737418240 | bytes 18874368 | tf_op jit(solution)/shard_map/opm_update/pallas_call | solution.py:126
  238.7 6.1 %tri_gate.2.gin_ref = f32[16,128,512]{2,1,0:T(8,128)} custom-call(bf16[16,128,512]{2,1,0:T(8,128)(2,1)} %get-tuple-element.50.z_ref.zin_ref, f32[2,128,1]{2,1,0:T(8,128)} %copy.68.nin_ref, bf16[128,128]{1,0:T(8,128)(2,1)} %bitcast.88, f32[128,1]{1,0:T(8,128)} %copy.72.b_ref), custom_call_target="tpu_custom_call" | custom-call | flops 1610612736 | bytes 6291456 | tf_op jit(solution)/shard_map/tri_gate/pallas_call | solution.py:382
  244.8 25.1 %all-to-all-done.1 = f32[32,4,16,512]{3,2,1,0:T(8,128)} async-done(((f32[32,4,16,512]{3,2,1,0:T(8,128)}), f32[32,4,16,512]{3,2,1,0:T(8,128)}, u32[]{:S(2)}, u32[]{:S(2)}) %all-to-all-start.1) | async-done | bytes 4194336 | tf_op jit(solution)/shard_map/all_to_all | solution.py:580
  269.9 17.3 %tri_middle.1 = (bf16[16,128,512]{2,1,0:T(8,128)(2,1)}, bf16[32,2,4,16,512]{4,3,2,1,0:T(8,128)(2,1)}) custom-call(f32[128,16,512]{2,1,0:T(8,128)} %bitcast.14.o_ref, bf16[16,128,512]{2,1,0:T(8,128)(2,1)} %get-tuple-element.50.z_ref.zin_ref, f32[16,128,512]{2,1,0:T(8,128)} %tri_gate.2.gin_ref, f32[2,128,1]{2,1,0:T(8,128)} %copy.78.nout_ref, ...), custom_call_target="tpu_custom_call" | custom-call | flops 1610612736 | bytes 16777216 | tf_op jit(solution)/shard_map/tri_middle/pallas_call | solution.py:501
  287.2 55.3 %all_to_all.21 = bf16[32,128,512]{2,1,0:T(8,128)(2,1)} all-to-all(bf16[32,128,512]{2,1,0:T(8,128)(2,1)} %bitcast.78), channel_id=1, replica_groups=mesh['batch'=1,'dap'=32] {'dap'}, dimensions={0} | all-to-all | bytes 8388608 | tf_op jit(solution)/shard_map/all_to_all | solution.py:577
  342.5 5.8 %tri_product.3 = f32[32,4,16,512]{3,2,1,0:T(8,128)} custom-call(bf16[32,2,4,16,512]{4,3,2,1,0:T(8,128)(2,1)} %bitcast.77), custom_call_target="tpu_custom_call" | custom-call | flops 1073741824 | bytes 8388608 | tf_op jit(solution)/shard_map/tri_product/pallas_call | solution.py:524
  348.3 6.1 %all-to-all-start.3 = ((f32[32,4,16,512]{3,2,1,0:T(8,128)}), f32[32,4,16,512]{3,2,1,0:T(8,128)}, u32[]{:S(2)}, u32[]{:S(2)}) async-start(f32[32,4,16,512]{3,2,1,0:T(8,128)} %tri_product.3), calls=%async_computation.3 | async-start | bytes 8388608 | tf_op jit(solution)/shard_map/all_to_all | solution.py:580
  355.8 0.8 copy.86.nout_ref
  358.1 6.1 %tri_gate.3.gin_ref = f32[16,128,512]{2,1,0:T(8,128)} custom-call(bf16[16,128,512]{2,1,0:T(8,128)(2,1)} %get-tuple-element.56.z_ref.zin_ref, f32[2,128,1]{2,1,0:T(8,128)} %copy.80.nin_ref, bf16[128,128]{1,0:T(8,128)(2,1)} %bitcast.91, f32[128,1]{1,0:T(8,128)} %copy.84.b_ref), custom_call_target="tpu_custom_call" | custom-call | flops 1610612736 | bytes 6291456 | tf_op jit(solution)/shard_map/tri_gate/pallas_call | solution.py:382
  364.2 47.6 %all-to-all-done.3 = f32[32,4,16,512]{3,2,1,0:T(8,128)} async-done(((f32[32,4,16,512]{3,2,1,0:T(8,128)}), f32[32,4,16,512]{3,2,1,0:T(8,128)}, u32[]{:S(2)}, u32[]{:S(2)}) %all-to-all-start.3) | async-done | bytes 4194336 | tf_op jit(solution)/shard_map/all_to_all | solution.py:580
  411.8 9.2 %tri_end.1 = bf16[16,512,128]{2,1,0:T(8,128)(2,1)} custom-call(f32[128,16,512]{2,1,0:T(8,128)} %bitcast.33.o_ref, bf16[16,128,512]{2,1,0:T(8,128)(2,1)} %get-tuple-element.56.z_ref.zin_ref, f32[16,128,512]{2,1,0:T(8,128)} %tri_gate.3.gin_ref, f32[2,128,1]{2,1,0:T(8,128)} %copy.86.nout_ref, bf16[128,128]{1,0:T(8,128)(2,1)} %bitcast.90, f32[128,1]{1,0:T(8,128)} %copy.87.bo_ref), custom_call_target="tpu_custom_call" | custom-call | flops 1610612736 | bytes 16777216 | tf_op jit(solution)/shard_map/tri_end/pallas_call | solution.py:501
  (52 shorter events, 9.3 us)
Async XLA Ops:
  15.4 54.5 %copy-start.1 = (bf16[2,1024,128]{2,1,0:T(8,128)(2,1)S(1)}, bf16[2,1024,128]{2,1,0:T(8,128)(2,1)}, u32[]{:S(2)}) copy-start(bf16[2,1024,128]{2,1,0:T(8,128)(2,1)} %param.26) | copy-start | bytes 1572868
  15.4 55.6 %copy-start.7 = (bf16[2,128]{1,0:T(2,128)(2,1)S(1)}, bf16[2,128]{1,0:T(2,128)(2,1)}, u32[]{:S(2)}) copy-start(bf16[2,128]{1,0:T(2,128)(2,1)} %param.27) | copy-start | bytes 1540
  15.4 56.3 %copy-start.10 = (bf16[2,2,128]{2,1,0:T(2,128)(2,1)S(1)}, bf16[2,2,128]{2,1,0:T(2,128)(2,1)}, u32[]{:S(2)}) copy-start(bf16[2,2,128]{2,1,0:T(2,128)(2,1)} %param.28) | copy-start | bytes 3076
  15.4 57.1 %copy-start.2 = (bf16[2,128,4,128]{3,2,1,0:T(4,128)(2,1)S(1)}, bf16[2,128,4,128]{3,2,1,0:T(4,128)(2,1)}, u32[]{:S(2)}) copy-start(bf16[2,128,4,128]{3,2,1,0:T(4,128)(2,1)} %param.29) | copy-start | bytes 786436
  15.4 58.0 %copy-start.6 = (bf16[2,4,128]{2,1,0:T(4,128)(2,1)S(1)}, bf16[2,4,128]{2,1,0:T(4,128)(2,1)}, u32[]{:S(2)}) copy-start(bf16[2,4,128]{2,1,0:T(4,128)(2,1)} %param.30) | copy-start | bytes 6148
  15.4 58.8 %copy-start.5 = (s32[16,512]{1,0:T(8,128)S(1)}, s32[16,512]{1,0:T(8,128)}, u32[]{:S(2)}) copy-start(s32[16,512]{1,0:T(8,128)} %param.21) | copy-start | bytes 98308
  69.9 4.9 %copy-start = (bf16[16,512,128]{2,1,0:T(8,128)(2,1)S(1)}, bf16[16,512,128]{2,1,0:T(8,128)(2,1)}, u32[]{:S(2)}) copy-start(bf16[16,512,128]{2,1,0:T(8,128)(2,1)} %param.20) | copy-start | bytes 6291460
  206.2 6.3 %copy-start.3 = (bf16[2,128,128]{2,1,0:T(8,128)(2,1)S(1)}, bf16[2,128,128]{2,1,0:T(8,128)(2,1)}, u32[]{:S(2)}) copy-start(bf16[2,128,128]{2,1,0:T(8,128)(2,1)} %param.31) | copy-start | bytes 196612
  206.2 7.1 %copy-start.8 = (bf16[2,128]{1,0:T(2,128)(2,1)S(1)}, bf16[2,128]{1,0:T(2,128)(2,1)}, u32[]{:S(2)}) copy-start(bf16[2,128]{1,0:T(2,128)(2,1)} %param.32) | copy-start | bytes 1540
  206.2 12.0 %copy-start.11 = (bf16[2,2,128]{2,1,0:T(2,128)(2,1)S(1)}, bf16[2,2,128]{2,1,0:T(2,128)(2,1)}, u32[]{:S(2)}) copy-start(bf16[2,2,128]{2,1,0:T(2,128)(2,1)} %param.33) | copy-start | bytes 3076
  206.2 12.8 %copy-start.4 = (bf16[2,128,128]{2,1,0:T(8,128)(2,1)S(1)}, bf16[2,128,128]{2,1,0:T(8,128)(2,1)}, u32[]{:S(2)}) copy-start(bf16[2,128,128]{2,1,0:T(8,128)(2,1)} %param.34) | copy-start | bytes 196612
  206.2 13.5 %copy-start.9 = (bf16[2,128]{1,0:T(2,128)(2,1)S(1)}, bf16[2,128]{1,0:T(2,128)(2,1)}, u32[]{:S(2)}) copy-start(bf16[2,128]{1,0:T(2,128)(2,1)} %param.35) | copy-start | bytes 1540
  206.2 63.7 %all-to-all-start.1 = ((f32[32,4,16,512]{3,2,1,0:T(8,128)}), f32[32,4,16,512]{3,2,1,0:T(8,128)}, u32[]{:S(2)}, u32[]{:S(2)}) async-start(f32[32,4,16,512]{3,2,1,0:T(8,128)} %tri_product.2), calls=%async_computation.1 | async-start | bytes 8388608 | tf_op jit(solution)/shard_map/all_to_all | solution.py:580
  348.3 63.5 %all-to-all-start.3 = ((f32[32,4,16,512]{3,2,1,0:T(8,128)}), f32[32,4,16,512]{3,2,1,0:T(8,128)}, u32[]{:S(2)}, u32[]{:S(2)}) async-start(f32[32,4,16,512]{3,2,1,0:T(8,128)} %tri_product.3), calls=%async_computation.3 | async-start | bytes 8388608 | tf_op jit(solution)/shard_map/all_to_all | solution.py:580

commit v5 on v4

--- a/solution.py
+++ b/solution.py
@@ -9,9 +9,26 @@
 
 LN_EPS = 1e-5
 LANES = 128
-ROW_UNROLL = 4
+ROW_UNROLL = 8
 F32 = jnp.float32
 BF16 = jnp.bfloat16
+
+
+COLUMN_PARTS = 11
+OPM_BIAS, NORM_IN, PROJ_BIAS, GATE_BIAS, NORM_OUT, OUT_BIAS = 0, 1, 3, 7, 8, 10
+
+
+def col(ref, part, count=1):
+    size = ref.shape[0] // COLUMN_PARTS
+    return ref[part * size:(part + count) * size]
+
+
+def pack_columns(parts):
+    total, offset, out = sum(p.shape[0] for p in parts), 0, 0.0
+    for p in parts:
+        out = out + lax.pad(p.astype(F32), jnp.float32(0), [(offset, total - offset - p.shape[0], 0)])
+        offset += p.shape[0]
+    return out[:, None]
 
 
 def dot_nn(a, b):
@@ -33,6 +50,7 @@
     s_blk, n_i, _ = m_ref.shape
     n_c = b_refs[0].shape[0]
     group = S_GROUP
+    gains = [norm_ref[l].astype(F32) for l in range(layers)]
 
     def rows(g, carry):
         base = pl.multiple_of(g * group, group)
@@ -41,7 +59,7 @@
         centered = x - mean_val
         var_val = jnp.mean(centered * centered, axis=-1, keepdims=True)
         scaled = centered * lax.rsqrt(var_val + LN_EPS)
-        normed = jnp.concatenate([(scaled * norm_ref[l, 0:1] + norm_ref[l, 1:2]).astype(BF16) for l in range(layers)], axis=1)
+        normed = jnp.concatenate([(scaled * gains[l][0:1] + gains[l][1:2]).astype(BF16) for l in range(layers)], axis=1)
         proj = dot_nn(normed, w_ref[...]) + bias_ref[...]
         for s in range(group):
             y_ref[pl.ds(pl.multiple_of((base + s) * I_STRIDE, 8), n_i), :] = proj[s * n_i:(s + 1) * n_i]
@@ -105,7 +123,7 @@
             upd = dot_nn(w_ref[...], q_ref[i])
             if not first:
                 upd = acc_ref[i] + upd
-            out_ref[i] = (upd + bias_ref[...]).astype(BF16) if last else upd
+            out_ref[i] = (upd + col(bias_ref, OPM_BIAS)).astype(BF16) if last else upd
             return carry
         lax.fori_loop(0, n_i, body, 0, unroll=4)
 
@@ -271,7 +289,8 @@
     )(block)
 
 
-def gather_opm_kernel(n, axis, inv_s, src_ref, a_ref, b_ref, w_ref, bias_ref, out_ref, upd_ref, buf, q_ref, b_sem, *sems):
+def gather_opm_kernel(n, axis, inv_s, src_ref, a_ref, b_ref, w_ref, c_ref, z_ref, mask_ref, w_ab_ref, out_ref, z_out, ab_ref,
+                      buf, q_ref, upd_ref, s_a, s_b, b_sem, *sems):
     ring = RingGather(n, axis, src_ref, out_ref, *sems)
     _, dev_blk, d_blk, j_loc, seqs = buf.shape
     n_i, _, j_blk = q_ref.shape
@@ -298,7 +317,7 @@
 
     def contract(j, low, high):
         def body(i, carry):
-            upd = dot_nn(w_ref[...], q_ref[i]) + bias_ref[...]
+            upd = dot_nn(w_ref[...], q_ref[i]) + col(c_ref, OPM_BIAS)
             upd_ref[i, :, j * j_blk:(j + 1) * j_blk] = upd.astype(BF16)
             return carry
         lax.fori_loop(low, high, body, 0, unroll=4)
@@ -308,19 +327,37 @@
         if k % parts == parts - 1:
             for half in range(2):
                 pieces.append(functools.partial(contract, k // parts, half * n_i // 2, (half + 1) * n_i // 2))
+
+    def project(j, low, high):
+        lanes = slice(j * j_blk, (j + 1) * j_blk)
+
+        def body(i, carry):
+            z_old = z_ref[i, lanes, :].astype(F32).T
+            z_new = (z_old + upd_ref[i, :, lanes].astype(F32)).astype(BF16)
+            z_out[i, :, lanes] = z_new
+            project_row(i, z_new.astype(F32), mask_ref[pl.ds(i, 1), lanes].astype(F32), w_ab_ref, c_ref, (s_a, s_b),
+                        j * j_blk // LANES)
+            return carry
+        lax.fori_loop(low, high, body, 0, unroll=2)
+    for j in range(total // parts):
+        for quarter in range(4):
+            pieces.append(functools.partial(project, j, quarter * n_i // 4, (quarter + 1) * n_i // 4))
+    n_dest = ab_ref.shape[0]
+    for half in range(2):
+        pieces.append(functools.partial(emit_ab, ab_ref, (s_a, s_b), half * n_dest // 2, (half + 1) * n_dest // 2))
     load(0).start()
     ring.barrier()
     steps = ring.steps()
+    done = 0
     for k, step in enumerate(steps[:-1]):
         step()
-        if k < len(pieces):
-            pieces[k]()
-    for piece in pieces[len(steps) - 1:]:
-        piece()
+        while done * (len(steps) - 1) < (k + 1) * len(pieces):
+            pieces[done]()
+            done += 1
     steps[-1]()
 
 
-def gather_with_opm(block, n, axis, cid, a_t, b_all, w_t, bias):
+def gather_with_opm(block, n, axis, cid, a_t, b_all, w_t, cols_l, pair_act, pair_mask, w_ab):
     n_dev, n_d, j_loc, seqs = b_all.shape
     n_z = w_t.shape[0]
     n_c = w_t.shape[1] // n_d
@@ -330,18 +367,20 @@
     d_blk = math.gcd(n_d, 8)
     side = math.isqrt(n // 2)
     assert 2 * side * side == n and side == 4
+    ab_scr = pltpu.VMEM((cols // LANES, n_z * I_STRIDE, LANES), F32)
     any_spec = pl.BlockSpec(memory_space=pl.ANY)
     vmem_spec = pl.BlockSpec(memory_space=pltpu.VMEM)
     return pl.pallas_call(
         functools.partial(gather_opm_kernel, n, axis, 1.0 / seqs),
-        out_shape=(jax.ShapeDtypeStruct((n,) + block.shape, block.dtype), jax.ShapeDtypeStruct((n_i, n_z, cols), BF16)),
-        in_specs=[any_spec, vmem_spec, any_spec, vmem_spec, vmem_spec], out_specs=(any_spec, vmem_spec),
+        out_shape=(jax.ShapeDtypeStruct((n,) + block.shape, block.dtype), jax.ShapeDtypeStruct((n_i, n_z, cols), BF16),
+                   jax.ShapeDtypeStruct((n, 2, n_z // n, n_i, cols), BF16)),
+        in_specs=[any_spec, vmem_spec, any_spec] + [vmem_spec] * 5, out_specs=(any_spec, vmem_spec, vmem_spec),
         scratch_shapes=[pltpu.VMEM((2, j_blk // j_loc, d_blk, j_loc, seqs), BF16), pltpu.VMEM((n_i, n_d * n_c, j_blk), BF16),
-                        pltpu.SemaphoreType.DMA((2,))] + gather_scratch(side),
+                        pltpu.VMEM((n_i, n_z, cols), BF16), ab_scr, ab_scr, pltpu.SemaphoreType.DMA((2,))] + gather_scratch(side),
         compiler_params=pltpu.CompilerParams(collective_id=cid, has_side_effects=True),
         cost_estimate=pl.CostEstimate(flops=2 * a_t.shape[0] * seqs * cols * n_d * 4, bytes_accessed=2 * b_all.size, transcendentals=0),
         name='ring_gather_opm',
-    )(block, a_t, b_all, w_t, bias)
+    )(block, a_t, b_all, w_t, cols_l, pair_act, pair_mask, w_ab)
 
 
 def norm_columns(x_f32, gain, offset):
@@ -355,44 +394,44 @@
     return 0.5 * jnp.tanh(0.5 * x) + 0.5
 
 
-def project_row(i, z_f32, mask_row, nin_ref, w_ref, b_ref, s_refs):
-    zn = norm_columns(z_f32, nin_ref[0], nin_ref[1])
+def project_row(i, z_f32, mask_row, w_ref, c_ref, s_refs, tile0=0):
+    zn = norm_columns(z_f32, col(c_ref, NORM_IN), col(c_ref, NORM_IN + 1))
     n_z, lanes = z_f32.shape
     n_ch = w_ref.shape[0] // 4
-    proj = dot_nn(w_ref[...], zn) + b_ref[...]
+    proj = dot_nn(w_ref[...], zn) + col(c_ref, PROJ_BIAS, 4)
     for q in range(2):
         lin = proj[2 * q * n_ch:(2 * q + 1) * n_ch]
         sig = sigmoid(proj[(2 * q + 1) * n_ch:(2 * q + 2) * n_ch])
         val = mask_row * sig * lin
         for t in range(lanes // LANES):
-            s_refs[q][t, pl.ds(i, n_ch, stride=I_STRIDE), :] = val[:, t * LANES:(t + 1) * LANES]
-
-
-def gate_kernel(z_ref, nin_ref, w_ref, b_ref, gate_ref):
+            s_refs[q][tile0 + t, pl.ds(i, n_ch, stride=I_STRIDE), :] = val[:, t * LANES:(t + 1) * LANES]
+
+
+def gate_kernel(z_ref, w_ref, c_ref, gate_ref):
     def body(i, carry):
-        zn = norm_columns(z_ref[i].astype(F32), nin_ref[0], nin_ref[1])
-        gate_ref[i] = sigmoid(dot_nn(w_ref[...], zn) + b_ref[...])
+        zn = norm_columns(z_ref[i].astype(F32), col(c_ref, NORM_IN), col(c_ref, NORM_IN + 1))
+        gate_ref[i] = sigmoid(dot_nn(w_ref[...], zn) + col(c_ref, GATE_BIAS))
         return carry
     lax.fori_loop(0, z_ref.shape[0], body, 0, unroll=4)
 
 
-def gate_call(z_t, norm_in, w_gate, b_gate):
+def gate_call(z_t, w_gate, cols_l):
     n_i, n_z, cols = z_t.shape
     row_spec = pl.BlockSpec((n_i, n_z, J_BLK), lambda j: (0, 0, j))
     return pl.pallas_call(
         gate_kernel, grid=(cols // J_BLK,),
-        in_specs=[row_spec, pl.BlockSpec(norm_in.shape, lambda j: (0, 0, 0)), pl.BlockSpec(w_gate.shape, lambda j: (0, 0)),
-                  pl.BlockSpec(b_gate.shape, lambda j: (0, 0))],
+        in_specs=[row_spec, pl.BlockSpec(w_gate.shape, lambda j: (0, 0)), pl.BlockSpec(cols_l.shape, lambda j: (0, 0))],
         out_specs=row_spec, out_shape=jax.ShapeDtypeStruct(z_t.shape, F32),
         compiler_params=pltpu.CompilerParams(dimension_semantics=('arbitrary',)),
         cost_estimate=pl.CostEstimate(flops=12 * n_i * cols * n_z * n_z, bytes_accessed=6 * n_i * cols * n_z,
                                       transcendentals=n_i * cols * n_z),
         name='tri_gate',
-    )(z_t, norm_in, w_gate, b_gate)
-
-
-def emit_ab(ab_ref, s_refs):
+    )(z_t, w_gate, cols_l)
+
+
+def emit_ab(ab_ref, s_refs, low=0, high=None):
     n_dev, _, n_cl, n_i, lanes = ab_ref.shape
+    high = n_dev if high is None else high
 
     def body(dev, carry):
         for q in range(2):
@@ -401,19 +440,7 @@
                 for t in range(lanes // LANES):
                     ab_ref[dev, q, c, :, t * LANES:(t + 1) * LANES] = s_refs[q][t, pl.ds(base, n_i), :].astype(BF16)
         return carry
-    lax.fori_loop(0, n_dev, body, 0, unroll=2)
-
-
-def start_kernel(z_ref, u_ref, mask_ref, nin_ref, w_ref, b_ref, z_out, ab_ref, s_a, s_b):
-    n_i = z_ref.shape[0]
-
-    def body(i, carry):
-        z_new = (z_ref[i].astype(F32) + u_ref[i].astype(F32)).astype(BF16)
-        z_out[i] = z_new
-        project_row(i, z_new.astype(F32), mask_ref[pl.ds(i, 1), :], nin_ref, w_ref, b_ref, (s_a, s_b))
-        return carry
-    lax.fori_loop(0, n_i, body, 0, unroll=ROW_UNROLL)
-    emit_ab(ab_ref, (s_a, s_b))
+    lax.fori_loop(low, high, body, 0, unroll=2)
 
 
 def finish_stats(o_ref, s_o, r_ref):
@@ -431,36 +458,36 @@
     r_ref[...] = lax.rsqrt(square / n_c + LN_EPS)
 
 
-def finish_row(i, z_ref, gate_ref, nout_ref, wo_ref, bo_ref, s_o, r_ref):
+def finish_row(i, z_ref, gate_ref, wo_ref, c_ref, s_o, r_ref):
     tiles, rows, _ = s_o.shape
     n_c = rows // I_STRIDE
     centered = jnp.concatenate([s_o[t, pl.ds(i, n_c, stride=I_STRIDE), :] for t in range(tiles)], axis=1)
-    norm = (centered * r_ref[pl.ds(i, 1), :] * nout_ref[0] + nout_ref[1]).astype(BF16)
-    upd = (dot_nn(wo_ref[...], norm) + bo_ref[...]).astype(BF16)
+    norm = (centered * r_ref[pl.ds(i, 1), :] * col(c_ref, NORM_OUT) + col(c_ref, NORM_OUT + 1)).astype(BF16)
+    upd = (dot_nn(wo_ref[...], norm) + col(c_ref, OUT_BIAS)).astype(BF16)
     return (z_ref[i].astype(F32) + gate_ref[i] * upd.astype(F32)).astype(BF16)
 
 
-def middle_kernel(o_ref, zin_ref, gin_ref, nout_ref, wo_ref, bo_ref, u_ref, mask_ref, nin_ref, w_ref, b_ref,
+def middle_kernel(o_ref, zin_ref, gin_ref, wo_ref, cp_ref, u_ref, mask_ref, w_ref, c_ref,
                   z_out, ab_ref, s_a, s_b, s_o, r_ref):
     n_i = zin_ref.shape[0]
     finish_stats(o_ref, s_o, r_ref)
 
     def body(i, carry):
-        z_mid = finish_row(i, zin_ref, gin_ref, nout_ref, wo_ref, bo_ref, s_o, r_ref)
+        z_mid = finish_row(i, zin_ref, gin_ref, wo_ref, cp_ref, s_o, r_ref)
         z_new = (z_mid.astype(F32) + u_ref[i].astype(F32)).astype(BF16)
         z_out[i] = z_new
-        project_row(i, z_new.astype(F32), mask_ref[pl.ds(i, 1), :], nin_ref, w_ref, b_ref, (s_a, s_b))
+        project_row(i, z_new.astype(F32), mask_ref[pl.ds(i, 1), :].astype(F32), w_ref, c_ref, (s_a, s_b))
         return carry
     lax.fori_loop(0, n_i, body, 0, unroll=ROW_UNROLL)
     emit_ab(ab_ref, (s_a, s_b))
 
 
-def end_kernel(o_ref, zin_ref, gin_ref, nout_ref, wo_ref, bo_ref, z_out, s_o, r_ref):
+def end_kernel(o_ref, zin_ref, gin_ref, wo_ref, c_ref, z_out, s_o, r_ref):
     n_i = zin_ref.shape[0]
     finish_stats(o_ref, s_o, r_ref)
 
     def body(i, carry):
-        z_new = finish_row(i, zin_ref, gin_ref, nout_ref, wo_ref, bo_ref, s_o, r_ref)
+        z_new = finish_row(i, zin_ref, gin_ref, wo_ref, c_ref, s_o, r_ref)
         z_out[i] = z_new.astype(F32).T.astype(BF16)
         return carry
     lax.fori_loop(0, n_i, body, 0, unroll=ROW_UNROLL)
@@ -470,11 +497,8 @@
 
 
 def tri_call(kind, n_dev, args):
-    kernels = {'start': start_kernel, 'middle': middle_kernel, 'end': end_kernel}
-    if kind == 'start':
-        n_i, n_z, cols = args[0].shape
-    else:
-        n_i, n_z, cols = args[1].shape
+    kernels = {'middle': middle_kernel, 'end': end_kernel}
+    n_i, n_z, cols = args[1].shape
     n_ch = n_z
 
     def blk(arr, which):
@@ -484,9 +508,8 @@
         return pl.BlockSpec(shape, lambda j: (0,) * len(shape))
 
     tiles = J_BLK // LANES
-    fin = ['j', 'j', 'j', 'w', 'w', 'w']
-    pro = ['j', 'j', 'w', 'w', 'w']
-    kinds = {'start': ['j'] + pro, 'middle': fin + pro, 'end': fin}[kind]
+    fin = ['j', 'j', 'j', 'w', 'w']
+    kinds = {'middle': fin + ['j', 'j', 'w', 'w'], 'end': fin}[kind]
     scr = pltpu.VMEM((tiles, n_ch * I_STRIDE, LANES), F32)
     stat = pltpu.VMEM((n_i, J_BLK), F32)
     if kind == 'end':
@@ -539,46 +562,34 @@
     msa_spec = P(None, ('batch', 'dap'), None)
     n_dev = mesh.shape['dap']
 
-    def column(vec):
-        return vec.astype(F32)[..., None]
-
     def device_fn(pair_act, pair_mask, msa_act, opm_norm, opm_w_in, opm_b_in, opm_w_out, opm_b_out, tri_norm_in, tri_w_ab, tri_b_ab, tri_w_gate, tri_b_gate, tri_norm_out, tri_w_out, tri_b_out):
         layers = opm_norm.shape[0]
+        assert layers == 2
         n_i, cols, n_z = pair_act.shape
         n_c = opm_w_in.shape[-1]
-        mask_f = pair_mask.astype(F32)
         n_m = msa_act.shape[-1]
-        w_bd = jnp.zeros((layers, n_m, layers, 2 * n_c), BF16)
-        for l in range(layers):
-            w_bd = w_bd.at[l, :, l].set(opm_w_in[l].reshape(n_m, 2 * n_c))
-        sides = msa_project(msa_act, opm_norm.astype(F32), w_bd.reshape(layers * n_m, layers * 2 * n_c),
-                                  opm_b_in.astype(F32).reshape(1, -1))
+        same = jnp.arange(layers)[:, None] == jnp.arange(layers)[None, :]
+        w_bd = jnp.where(same[:, None, :, None], opm_w_in.reshape(layers, n_m, 1, 2 * n_c), 0)
+        sides = msa_project(msa_act, opm_norm, w_bd.reshape(layers * n_m, layers * 2 * n_c).astype(BF16),
+                            opm_b_in.astype(F32).reshape(1, -1))
         left, right = sides[:layers], sides[layers:]
         opm_w = [opm_w_out[l].reshape(n_c, n_c, n_z).transpose(2, 1, 0).reshape(n_z, n_c * n_c) for l in range(layers)]
+        w_abs = [tri_w_ab[l].transpose(1, 2, 0).reshape(-1, n_z) for l in range(layers)]
+        params = [pack_columns([p[l].reshape(-1) for p in (opm_b_out, tri_norm_in, tri_b_ab, tri_b_gate, tri_norm_out, tri_b_out)])
+                  for l in range(layers)]
         gathered = ring_gather(right[0], n_dev, 'dap', 0)
-        updates = []
-        for l in range(layers):
-            rest = (left[l], gathered, opm_w[l], column(opm_b_out[l]))
-            if l + 1 < layers:
-                gathered, update = gather_with_opm(right[l + 1], n_dev, 'dap', l + 1, *rest)
-            else:
-                update = opm_update(*rest)
-            updates.append(update)
-        z_t = jnp.swapaxes(pair_act, 1, 2)
+        gathered, z_t, ab = gather_with_opm(right[1], n_dev, 'dap', 1, left[0], gathered, opm_w[0], params[0], pair_act, pair_mask,
+                                            w_abs[0])
+        update = opm_update(left[1], gathered, opm_w[1], params[1])
         fin = None
         for l in range(layers):
-            w_all = tri_w_ab[l].transpose(1, 2, 0).reshape(-1, n_z)
-            norm_in = column(tri_norm_in[l])
-            pro = (updates[l], mask_f, norm_in, w_all, column(tri_b_ab[l].reshape(-1)))
-            if l == 0:
-                z_t, ab = tri_call('start', n_dev, (z_t,) + pro)
-            else:
-                z_t, ab = tri_call('middle', n_dev, fin + pro)
+            if l:
+                z_t, ab = tri_call('middle', n_dev, fin + (update, pair_mask, w_abs[l], params[l]))
             ab = lax.all_to_all(ab.reshape(n_dev, -1, cols), 'dap', 0, 0, tiled=True).reshape(ab.shape)
             prod, z_g = lax.optimization_barrier((tri_product(ab), z_t))
-            gate = gate_call(z_g, norm_in, tri_w_gate[l].T, column(tri_b_gate[l]))
+            gate = gate_call(z_g, tri_w_gate[l].T, params[l])
             prod = lax.all_to_all(prod, 'dap', 0, 0, tiled=True)
-            fin = (prod.reshape(-1, n_i, cols), z_t, gate, column(tri_norm_out[l]), tri_w_out[l].T, column(tri_b_out[l]))
+            fin = (prod.reshape(-1, n_i, cols), z_t, gate, tri_w_out[l].T, params[l])
         return tri_call('end', n_dev, fin)
 
     return jax.shard_map(device_fn, mesh=mesh, in_specs=(pair_spec, mask_spec, msa_spec) + (P(),) * 13, out_specs=pair_spec, check_vma=False)

time: 422 us -> 409 us (0.969)
  Pallas kernels: 199 us -> 190 us
  local copies, waits for them, and re-layouts: 22.4 us -> 14.7 us
    pallas_call x3 -> x2, Pallas kernels: 37.6 us -> 24.9 us  [tri_call(): pl.pallas_call(kernels[kind], grid=(cols // J_BLK,), in_specs=[blk(a, k)...]
    convert_element_type x12 -> x4, local copies, waits for them, and re-layouts: 9.35 us -> 2.88 us  [pack_columns(): p.astype(F32)]
  transfers between devices with their start and end apart: 2 -> 2, of which waited for: 2 -> 2; matrix products, arithmetic and copies ran while one was open for 3% -> 1% of each run, Pallas kernels for 7% -> 8%
where the time goes in v5:
time: 409 us; the launch traced here: 408 us
  Pallas kernels  190 us (46%)
  blocking collectives  116 us (28%)
  waiting for transfers between devices  76.2 us (19%)
  local copies, waits for them, and re-layouts  14.7 us (4%)
  starting transfers between devices  11.4 us (3%)
    all_to_all x2, blocking collectives, device_fn(): lax.all_to_all(ab.reshape(n_dev, -1, cols), 'dap', 0, 0, tiled=True)  116 us
    all_to_all x2, waiting for transfers between devices, device_fn(): prod = lax.all_to_all(prod, 'dap', 0, 0, tiled=True)  76.2 us
    pallas_call x1, Pallas kernels, gather_with_opm(): pl.pallas_call(functools.partial(gather_opm_kernel, n, axis, 1.0 / seqs),...  57.6 us
    pallas_call x1, Pallas kernels, ring_gather(): pl.pallas_call(functools.partial(gather_kernel, n, axis), out_shape=jax.S...  54.5 us
    pallas_call x2, Pallas kernels, tri_call(): pl.pallas_call(kernels[kind], grid=(cols // J_BLK,), in_specs=[blk(a, k)...  24.9 us
    pallas_call x1, Pallas kernels, opm_update(): pl.pallas_call(functools.partial(opm_kernel, 1.0 / seqs, first, last), gr...  18.5 us
    pallas_call x2, Pallas kernels, gate_call(): pl.pallas_call(gate_kernel, grid=(cols // J_BLK,), in_specs=[row_spec, pl...  12.6 us
    pallas_call x2, Pallas kernels, tri_product(): pl.pallas_call(product_kernel, grid=(n_cl,), in_specs=[pl.BlockSpec((n_de...  11.4 us
  transfers between devices with their start and end apart: 2, of which 2 were waited for; matrix products, arithmetic and copies ran while one was open for 1% of the time, Pallas kernels for 8%

profile of v5, /device:TPU:103, one launch (start us, length us, event | category | flops | bytes accessed | tf_op | source)
XLA Modules:
  0.0 408.1 jit_solution(10235042744749243319)
XLA Ops:
  0.7 0.7 slice_bitcast_fusion.8
  1.4 0.7 slice_bitcast_fusion.5
  2.1 0.7 slice_bitcast_fusion.4
  2.9 1.1 broadcast_in_dim.37.c_ref.cp_ref
  4.0 0.9 copy.43
  5.2 0.8 copy.44.w_ref
  5.9 1.2 reshape.91.bias_ref
  7.2 10.1 %msa_project.1 = (bf16[512,512]{1,0:T(8,128)(2,1)}, bf16[512,512]{1,0:T(8,128)(2,1)}, bf16[32,16,512]{2,1,0:T(8,128)(2,1)}, bf16[32,16,512]{2,1,0:T(8,128)(2,1)}) custom-call(bf16[512,16,256]{2,1,0:T(8,128)(2,1)} %m_ref.1, bf16[2,2,256]{2,1,0:T(2,128)(2,1)} %norm_ref.1, bf16[512,128]{1,0:T(8,128)(2,1)} %copy.44.w_ref, f32[1,128]{1,0:T(1,128)} %reshape.91.bias_ref), custom_call_target="tpu_custom_call" | custom-call | flops 536870912 | bytes 6291456 | tf_op jit(solution)/shard_map/msa_project/pallas_call | solution.py:87
  17.3 54.5 %ring_gather.1.b_ref = bf16[32,32,16,512]{3,2,1,0:T(8,128)(2,1)} custom-call(bf16[32,16,512]{2,1,0:T(8,128)(2,1)} %get-tuple-element.20.src_ref), custom_call_target="tpu_custom_call" | custom-call | tf_op jit(solution)/shard_map/ring_gather/pallas_call | solution.py:282
  71.9 0.8 copy.47.w_ref
  72.9 0.8 copy.46
  73.7 57.6 %ring_gather_opm.1 = (bf16[32,32,16,512]{3,2,1,0:T(8,128)(2,1)}, bf16[16,128,512]{2,1,0:T(8,128)(2,1)}, bf16[32,2,4,16,512]{4,3,2,1,0:T(8,128)(2,1)}) custom-call(bf16[32,16,512]{2,1,0:T(8,128)(2,1)} %get-tuple-element.18.src_ref, bf16[512,512]{1,0:T(8,128)(2,1)} %get-tuple-element.19.a_ref, bf16[32,32,16,512]{3,2,1,0:T(8,128)(2,1)} %ring_gather.1.b_ref, ...), custom_call_target="tpu_custom_call" | custom-call | flops 34359738368 | bytes 16777216 | tf_op jit(solution)/shard_map/ring_gather_opm/pallas_call | solution.py:373
  131.3 59.1 %all_to_all.20 = bf16[32,128,512]{2,1,0:T(8,128)(2,1)} all-to-all(bf16[32,128,512]{2,1,0:T(8,128)(2,1)} %bitcast.69), channel_id=1, replica_groups=mesh['batch'=1,'dap'=32] {'dap'}, dimensions={0} | all-to-all | bytes 8388608 | tf_op jit(solution)/shard_map/all_to_all | solution.py:588
  190.4 5.7 %tri_product.2 = f32[32,4,16,512]{3,2,1,0:T(8,128)} custom-call(bf16[32,2,4,16,512]{4,3,2,1,0:T(8,128)(2,1)} %bitcast.66), custom_call_target="tpu_custom_call" | custom-call | flops 1073741824 | bytes 8388608 | tf_op jit(solution)/shard_map/tri_product/pallas_call | solution.py:547
  196.1 5.7 %all-to-all-start.1 = ((f32[32,4,16,512]{3,2,1,0:T(8,128)}), f32[32,4,16,512]{3,2,1,0:T(8,128)}, u32[]{:S(2)}, u32[]{:S(2)}) async-start(f32[32,4,16,512]{3,2,1,0:T(8,128)} %tri_product.2), calls=%async_computation.1 | async-start | bytes 8388608 | tf_op jit(solution)/shard_map/all_to_all | solution.py:591
  201.8 0.7 copy.62
  202.6 1.2 broadcast_in_dim.38.bias_ref.c_ref
  203.9 0.9 copy.53.w_ref
  204.7 0.8 copy.55
  205.5 0.7 copy.63
  206.2 18.5 %opm_update.1.u_ref = bf16[16,128,512]{2,1,0:T(8,128)(2,1)} custom-call(bf16[512,512]{1,0:T(8,128)(2,1)} %get-tuple-element.25.a_ref, bf16[32,32,16,512]{3,2,1,0:T(8,128)(2,1)} %get-tuple-element.26.b_ref, bf16[128,1024]{1,0:T(8,128)(2,1)} %copy.53.w_ref, f32[1408,1]{1,0:T(8,128)} %broadcast_in_dim.38.bias_ref.c_ref), custom_call_target="tpu_custom_call" | custom-call | flops 10737418240 | bytes 18874368 | tf_op jit(solution)/shard_map/opm_update/pallas_call | solution.py:144
  224.7 6.3 %tri_gate.2.gin_ref = f32[16,128,512]{2,1,0:T(8,128)} custom-call(bf16[16,128,512]{2,1,0:T(8,128)(2,1)} %get-tuple-element.24.z_ref.zin_ref, bf16[128,128]{1,0:T(8,128)(2,1)} %bitcast.77, f32[1408,1]{1,0:T(8,128)} %broadcast_in_dim.37.c_ref.cp_ref), custom_call_target="tpu_custom_call" | custom-call | flops 1610612736 | bytes 6291456 | tf_op jit(solution)/shard_map/tri_gate/pallas_call | solution.py:421
  231.0 27.4 %all-to-all-done.1 = f32[32,4,16,512]{3,2,1,0:T(8,128)} async-done(((f32[32,4,16,512]{3,2,1,0:T(8,128)}), f32[32,4,16,512]{3,2,1,0:T(8,128)}, u32[]{:S(2)}, u32[]{:S(2)}) %all-to-all-start.1) | async-done | bytes 4194336 | tf_op jit(solution)/shard_map/all_to_all | solution.py:591
  258.4 16.5 %tri_middle.1 = (bf16[16,128,512]{2,1,0:T(8,128)(2,1)}, bf16[32,2,4,16,512]{4,3,2,1,0:T(8,128)(2,1)}) custom-call(f32[128,16,512]{2,1,0:T(8,128)} %bitcast.15.o_ref, bf16[16,128,512]{2,1,0:T(8,128)(2,1)} %get-tuple-element.24.z_ref.zin_ref, f32[16,128,512]{2,1,0:T(8,128)} %tri_gate.2.gin_ref, bf16[128,128]{1,0:T(8,128)(2,1)} %bitcast.79, ...), custom_call_target="tpu_custom_call" | custom-call | flops 1610612736 | bytes 16777216 | tf_op jit(solution)/shard_map/tri_middle/pallas_call | solution.py:524
  274.9 56.7 %all_to_all.21 = bf16[32,128,512]{2,1,0:T(8,128)(2,1)} all-to-all(bf16[32,128,512]{2,1,0:T(8,128)(2,1)} %bitcast.68), channel_id=1, replica_groups=mesh['batch'=1,'dap'=32] {'dap'}, dimensions={0} | all-to-all | bytes 8388608 | tf_op jit(solution)/shard_map/all_to_all | solution.py:588
  331.6 5.7 %tri_product.3 = f32[32,4,16,512]{3,2,1,0:T(8,128)} custom-call(bf16[32,2,4,16,512]{4,3,2,1,0:T(8,128)(2,1)} %bitcast.67), custom_call_target="tpu_custom_call" | custom-call | flops 1073741824 | bytes 8388608 | tf_op jit(solution)/shard_map/tri_product/pallas_call | solution.py:547
  337.3 5.7 %all-to-all-start.3 = ((f32[32,4,16,512]{3,2,1,0:T(8,128)}), f32[32,4,16,512]{3,2,1,0:T(8,128)}, u32[]{:S(2)}, u32[]{:S(2)}) async-start(f32[32,4,16,512]{3,2,1,0:T(8,128)} %tri_product.3), calls=%async_computation.3 | async-start | bytes 8388608 | tf_op jit(solution)/shard_map/all_to_all | solution.py:591
  343.1 0.7 copy.64
  343.8 0.7 copy.65
  344.5 6.3 %tri_gate.3.gin_ref = f32[16,128,512]{2,1,0:T(8,128)} custom-call(bf16[16,128,512]{2,1,0:T(8,128)(2,1)} %get-tuple-element.30.z_ref.zin_ref, bf16[128,128]{1,0:T(8,128)(2,1)} %bitcast.78, f32[1408,1]{1,0:T(8,128)} %broadcast_in_dim.38.bias_ref.c_ref), custom_call_target="tpu_custom_call" | custom-call | flops 1610612736 | bytes 6291456 | tf_op jit(solution)/shard_map/tri_gate/pallas_call | solution.py:421
  350.8 48.8 %all-to-all-done.3 = f32[32,4,16,512]{3,2,1,0:T(8,128)} async-done(((f32[32,4,16,512]{3,2,1,0:T(8,128)}), f32[32,4,16,512]{3,2,1,0:T(8,128)}, u32[]{:S(2)}, u32[]{:S(2)}) %all-to-all-start.3) | async-done | bytes 4194336 | tf_op jit(solution)/shard_map/all_to_all | solution.py:591
  399.7 8.4 %tri_end.1 = bf16[16,512,128]{2,1,0:T(8,128)(2,1)} custom-call(f32[128,16,512]{2,1,0:T(8,128)} %bitcast.34.o_ref, bf16[16,128,512]{2,1,0:T(8,128)(2,1)} %get-tuple-element.30.z_ref.zin_ref, f32[16,128,512]{2,1,0:T(8,128)} %tri_gate.3.gin_ref, bf16[128,128]{1,0:T(8,128)(2,1)} %bitcast.80, f32[1408,1]{1,0:T(8,128)} %broadcast_in_dim.38.bias_ref.c_ref), custom_call_target="tpu_custom_call" | custom-call | flops 1610612736 | bytes 16777216 | tf_op jit(solution)/shard_map/tri_end/pallas_call | solution.py:524
  (20 shorter events, 1.3 us)
Async XLA Ops:
  17.3 54.5 %copy-start = (bf16[2,1024,128]{2,1,0:T(8,128)(2,1)S(1)}, bf16[2,1024,128]{2,1,0:T(8,128)(2,1)}, u32[]{:S(2)}) copy-start(bf16[2,1024,128]{2,1,0:T(8,128)(2,1)} %param.22) | copy-start | bytes 1572868
  17.3 55.5 %copy-start.1 = (bf16[2,128,4,128]{3,2,1,0:T(4,128)(2,1)S(1)}, bf16[2,128,4,128]{3,2,1,0:T(4,128)(2,1)}, u32[]{:S(2)}) copy-start(bf16[2,128,4,128]{3,2,1,0:T(4,128)(2,1)} %param.25) | copy-start | bytes 786436
  196.1 5.7 %copy-start.2 = (bf16[2,128,128]{2,1,0:T(8,128)(2,1)S(1)}, bf16[2,128,128]{2,1,0:T(8,128)(2,1)}, u32[]{:S(2)}) copy-start(bf16[2,128,128]{2,1,0:T(8,128)(2,1)} %param.27) | copy-start | bytes 196612
  196.1 9.4 %copy-start.3 = (bf16[2,128,128]{2,1,0:T(8,128)(2,1)S(1)}, bf16[2,128,128]{2,1,0:T(8,128)(2,1)}, u32[]{:S(2)}) copy-start(bf16[2,128,128]{2,1,0:T(8,128)(2,1)} %param.30) | copy-start | bytes 196612
  196.1 62.3 %all-to-all-start.1 = ((f32[32,4,16,512]{3,2,1,0:T(8,128)}), f32[32,4,16,512]{3,2,1,0:T(8,128)}, u32[]{:S(2)}, u32[]{:S(2)}) async-start(f32[32,4,16,512]{3,2,1,0:T(8,128)} %tri_product.2), calls=%async_computation.1 | async-start | bytes 8388608 | tf_op jit(solution)/shard_map/all_to_all | solution.py:591
  337.3 62.3 %all-to-all-start.3 = ((f32[32,4,16,512]{3,2,1,0:T(8,128)}), f32[32,4,16,512]{3,2,1,0:T(8,128)}, u32[]{:S(2)}, u32[]{:S(2)}) async-start(f32[32,4,16,512]{3,2,1,0:T(8,128)} %tri_product.3), calls=%async_computation.3 | async-start | bytes 8388608 | tf_op jit(solution)/shard_map/all_to_all | solution.py:591

commit v6 on v5

--- a/solution.py
+++ b/solution.py
@@ -64,7 +64,7 @@
         for s in range(group):
             y_ref[pl.ds(pl.multiple_of((base + s) * I_STRIDE, 8), n_i), :] = proj[s * n_i:(s + 1) * n_i]
         return carry
-    lax.fori_loop(0, s_blk // group, rows, 0, unroll=2)
+    lax.fori_loop(0, s_blk // group, rows, 0, unroll=4)
 
     def columns(i, carry):
         flip = y_ref[pl.ds(i, s_blk, stride=I_STRIDE), :].T
@@ -73,7 +73,7 @@
             a_refs[l][pl.ds(pl.multiple_of(i * n_c, n_c), n_c), :] = flip[top:top + n_c].astype(BF16)
             t_ref[l, pl.ds(i, n_c, stride=I_STRIDE), :] = flip[top + n_c:top + 2 * n_c]
         return carry
-    lax.fori_loop(0, n_i, columns, 0, unroll=4)
+    lax.fori_loop(0, n_i, columns, 0, unroll=8)
     for l in range(layers):
         for d in range(n_c):
             b_refs[l][d] = t_ref[l, d * I_STRIDE:d * I_STRIDE + n_i, :].astype(BF16)

time: 409 us -> 407 us (level)
  no operation moved by 1% of the time
where the time goes in v6:
time: 407 us
  Pallas kernels  188 us (46%)
  blocking collectives  116 us (29%)
  waiting for transfers between devices  76.2 us (19%)
  local copies, waits for them, and re-layouts  14.7 us (4%)
  starting transfers between devices  11.4 us (3%)
    all_to_all x2, blocking collectives, device_fn(): lax.all_to_all(ab.reshape(n_dev, -1, cols), 'dap', 0, 0, tiled=True)  116 us
    all_to_all x2, waiting for transfers between devices, device_fn(): prod = lax.all_to_all(prod, 'dap', 0, 0, tiled=True)  76.2 us
    pallas_call x1, Pallas kernels, gather_with_opm(): pl.pallas_call(functools.partial(gather_opm_kernel, n, axis, 1.0 / seqs),...  57.6 us
    pallas_call x1, Pallas kernels, ring_gather(): pl.pallas_call(functools.partial(gather_kernel, n, axis), out_shape=jax.S...  54.5 us
    pallas_call x2, Pallas kernels, tri_call(): pl.pallas_call(kernels[kind], grid=(cols // J_BLK,), in_specs=[blk(a, k)...  24.9 us
    pallas_call x1, Pallas kernels, opm_update(): pl.pallas_call(functools.partial(opm_kernel, 1.0 / seqs, first, last), gr...  18.5 us
    pallas_call x2, Pallas kernels, gate_call(): pl.pallas_call(gate_kernel, grid=(cols // J_BLK,), in_specs=[row_spec, pl...  12.6 us
    pallas_call x2, Pallas kernels, tri_product(): pl.pallas_call(product_kernel, grid=(n_cl,), in_specs=[pl.BlockSpec((n_de...  11.4 us
  transfers between devices with their start and end apart: 2, of which 2 were waited for; matrix products, arithmetic and copies ran while one was open for 1% of the time, Pallas kernels for 8%

profile of v6, /device:TPU:103, one launch (start us, length us, event | category | flops | bytes accessed | tf_op | source)
XLA Modules:
  0.0 406.7 jit_solution(6374978555448186924)
XLA Ops:
  0.7 0.7 slice_bitcast_fusion.8
  1.4 0.7 slice_bitcast_fusion.5
  2.1 0.7 slice_bitcast_fusion.4
  2.9 1.1 broadcast_in_dim.37.c_ref.cp_ref
  4.0 0.9 copy.43
  5.2 0.8 copy.44.w_ref
  5.9 1.2 reshape.91.bias_ref
  7.2 8.6 %msa_project.1 = (bf16[512,512]{1,0:T(8,128)(2,1)}, bf16[512,512]{1,0:T(8,128)(2,1)}, bf16[32,16,512]{2,1,0:T(8,128)(2,1)}, bf16[32,16,512]{2,1,0:T(8,128)(2,1)}) custom-call(bf16[512,16,256]{2,1,0:T(8,128)(2,1)} %m_ref.1, bf16[2,2,256]{2,1,0:T(2,128)(2,1)} %norm_ref.1, bf16[512,128]{1,0:T(8,128)(2,1)} %copy.44.w_ref, f32[1,128]{1,0:T(1,128)} %reshape.91.bias_ref), custom_call_target="tpu_custom_call" | custom-call | flops 536870912 | bytes 6291456 | tf_op jit(solution)/shard_map/msa_project/pallas_call | solution.py:87
  15.8 54.5 %ring_gather.1.b_ref = bf16[32,32,16,512]{3,2,1,0:T(8,128)(2,1)} custom-call(bf16[32,16,512]{2,1,0:T(8,128)(2,1)} %get-tuple-element.20.src_ref), custom_call_target="tpu_custom_call" | custom-call | tf_op jit(solution)/shard_map/ring_gather/pallas_call | solution.py:282
  70.4 0.8 copy.47.w_ref
  71.4 0.8 copy.46
  72.2 57.6 %ring_gather_opm.1 = (bf16[32,32,16,512]{3,2,1,0:T(8,128)(2,1)}, bf16[16,128,512]{2,1,0:T(8,128)(2,1)}, bf16[32,2,4,16,512]{4,3,2,1,0:T(8,128)(2,1)}) custom-call(bf16[32,16,512]{2,1,0:T(8,128)(2,1)} %get-tuple-element.18.src_ref, bf16[512,512]{1,0:T(8,128)(2,1)} %get-tuple-element.19.a_ref, bf16[32,32,16,512]{3,2,1,0:T(8,128)(2,1)} %ring_gather.1.b_ref, ...), custom_call_target="tpu_custom_call" | custom-call | flops 34359738368 | bytes 16777216 | tf_op jit(solution)/shard_map/ring_gather_opm/pallas_call | solution.py:373
  129.8 59.1 %all_to_all.20 = bf16[32,128,512]{2,1,0:T(8,128)(2,1)} all-to-all(bf16[32,128,512]{2,1,0:T(8,128)(2,1)} %bitcast.69), channel_id=1, replica_groups=mesh['batch'=1,'dap'=32] {'dap'}, dimensions={0} | all-to-all | bytes 8388608 | tf_op jit(solution)/shard_map/all_to_all | solution.py:588
  188.9 5.7 %tri_product.2 = f32[32,4,16,512]{3,2,1,0:T(8,128)} custom-call(bf16[32,2,4,16,512]{4,3,2,1,0:T(8,128)(2,1)} %bitcast.66), custom_call_target="tpu_custom_call" | custom-call | flops 1073741824 | bytes 8388608 | tf_op jit(solution)/shard_map/tri_product/pallas_call | solution.py:547
  194.6 5.7 %all-to-all-start.1 = ((f32[32,4,16,512]{3,2,1,0:T(8,128)}), f32[32,4,16,512]{3,2,1,0:T(8,128)}, u32[]{:S(2)}, u32[]{:S(2)}) async-start(f32[32,4,16,512]{3,2,1,0:T(8,128)} %tri_product.2), calls=%async_computation.1 | async-start | bytes 8388608 | tf_op jit(solution)/shard_map/all_to_all | solution.py:591
  200.3 0.7 copy.62
  201.1 1.2 broadcast_in_dim.38.bias_ref.c_ref
  202.4 0.9 copy.53.w_ref
  203.2 0.8 copy.55
  204.0 0.7 copy.63
  204.7 18.5 %opm_update.1.u_ref = bf16[16,128,512]{2,1,0:T(8,128)(2,1)} custom-call(bf16[512,512]{1,0:T(8,128)(2,1)} %get-tuple-element.25.a_ref, bf16[32,32,16,512]{3,2,1,0:T(8,128)(2,1)} %get-tuple-element.26.b_ref, bf16[128,1024]{1,0:T(8,128)(2,1)} %copy.53.w_ref, f32[1408,1]{1,0:T(8,128)} %broadcast_in_dim.38.bias_ref.c_ref), custom_call_target="tpu_custom_call" | custom-call | flops 10737418240 | bytes 18874368 | tf_op jit(solution)/shard_map/opm_update/pallas_call | solution.py:144
  223.2 6.3 %tri_gate.2.gin_ref = f32[16,128,512]{2,1,0:T(8,128)} custom-call(bf16[16,128,512]{2,1,0:T(8,128)(2,1)} %get-tuple-element.24.z_ref.zin_ref, bf16[128,128]{1,0:T(8,128)(2,1)} %bitcast.77, f32[1408,1]{1,0:T(8,128)} %broadcast_in_dim.37.c_ref.cp_ref), custom_call_target="tpu_custom_call" | custom-call | flops 1610612736 | bytes 6291456 | tf_op jit(solution)/shard_map/tri_gate/pallas_call | solution.py:421
  229.5 27.4 %all-to-all-done.1 = f32[32,4,16,512]{3,2,1,0:T(8,128)} async-done(((f32[32,4,16,512]{3,2,1,0:T(8,128)}), f32[32,4,16,512]{3,2,1,0:T(8,128)}, u32[]{:S(2)}, u32[]{:S(2)}) %all-to-all-start.1) | async-done | bytes 4194336 | tf_op jit(solution)/shard_map/all_to_all | solution.py:591
  256.9 16.5 %tri_middle.1 = (bf16[16,128,512]{2,1,0:T(8,128)(2,1)}, bf16[32,2,4,16,512]{4,3,2,1,0:T(8,128)(2,1)}) custom-call(f32[128,16,512]{2,1,0:T(8,128)} %bitcast.15.o_ref, bf16[16,128,512]{2,1,0:T(8,128)(2,1)} %get-tuple-element.24.z_ref.zin_ref, f32[16,128,512]{2,1,0:T(8,128)} %tri_gate.2.gin_ref, bf16[128,128]{1,0:T(8,128)(2,1)} %bitcast.79, ...), custom_call_target="tpu_custom_call" | custom-call | flops 1610612736 | bytes 16777216 | tf_op jit(solution)/shard_map/tri_middle/pallas_call | solution.py:524
  273.4 56.9 %all_to_all.21 = bf16[32,128,512]{2,1,0:T(8,128)(2,1)} all-to-all(bf16[32,128,512]{2,1,0:T(8,128)(2,1)} %bitcast.68), channel_id=1, replica_groups=mesh['batch'=1,'dap'=32] {'dap'}, dimensions={0} | all-to-all | bytes 8388608 | tf_op jit(solution)/shard_map/all_to_all | solution.py:588
  330.3 5.7 %tri_product.3 = f32[32,4,16,512]{3,2,1,0:T(8,128)} custom-call(bf16[32,2,4,16,512]{4,3,2,1,0:T(8,128)(2,1)} %bitcast.67), custom_call_target="tpu_custom_call" | custom-call | flops 1073741824 | bytes 8388608 | tf_op jit(solution)/shard_map/tri_product/pallas_call | solution.py:547
  336.0 5.7 %all-to-all-start.3 = ((f32[32,4,16,512]{3,2,1,0:T(8,128)}), f32[32,4,16,512]{3,2,1,0:T(8,128)}, u32[]{:S(2)}, u32[]{:S(2)}) async-start(f32[32,4,16,512]{3,2,1,0:T(8,128)} %tri_product.3), calls=%async_computation.3 | async-start | bytes 8388608 | tf_op jit(solution)/shard_map/all_to_all | solution.py:591
  341.7 0.7 copy.64
  342.4 0.7 copy.65
  343.2 6.3 %tri_gate.3.gin_ref = f32[16,128,512]{2,1,0:T(8,128)} custom-call(bf16[16,128,512]{2,1,0:T(8,128)(2,1)} %get-tuple-element.30.z_ref.zin_ref, bf16[128,128]{1,0:T(8,128)(2,1)} %bitcast.78, f32[1408,1]{1,0:T(8,128)} %broadcast_in_dim.38.bias_ref.c_ref), custom_call_target="tpu_custom_call" | custom-call | flops 1610612736 | bytes 6291456 | tf_op jit(solution)/shard_map/tri_gate/pallas_call | solution.py:421
  349.5 48.8 %all-to-all-done.3 = f32[32,4,16,512]{3,2,1,0:T(8,128)} async-done(((f32[32,4,16,512]{3,2,1,0:T(8,128)}), f32[32,4,16,512]{3,2,1,0:T(8,128)}, u32[]{:S(2)}, u32[]{:S(2)}) %all-to-all-start.3) | async-done | bytes 4194336 | tf_op jit(solution)/shard_map/all_to_all | solution.py:591
  398.3 8.4 %tri_end.1 = bf16[16,512,128]{2,1,0:T(8,128)(2,1)} custom-call(f32[128,16,512]{2,1,0:T(8,128)} %bitcast.34.o_ref, bf16[16,128,512]{2,1,0:T(8,128)(2,1)} %get-tuple-element.30.z_ref.zin_ref, f32[16,128,512]{2,1,0:T(8,128)} %tri_gate.3.gin_ref, bf16[128,128]{1,0:T(8,128)(2,1)} %bitcast.80, f32[1408,1]{1,0:T(8,128)} %broadcast_in_dim.38.bias_ref.c_ref), custom_call_target="tpu_custom_call" | custom-call | flops 1610612736 | bytes 16777216 | tf_op jit(solution)/shard_map/tri_end/pallas_call | solution.py:524
  (20 shorter events, 1.3 us)
Async XLA Ops:
  15.8 54.5 %copy-start = (bf16[2,1024,128]{2,1,0:T(8,128)(2,1)S(1)}, bf16[2,1024,128]{2,1,0:T(8,128)(2,1)}, u32[]{:S(2)}) copy-start(bf16[2,1024,128]{2,1,0:T(8,128)(2,1)} %param.22) | copy-start | bytes 1572868
  15.8 55.5 %copy-start.1 = (bf16[2,128,4,128]{3,2,1,0:T(4,128)(2,1)S(1)}, bf16[2,128,4,128]{3,2,1,0:T(4,128)(2,1)}, u32[]{:S(2)}) copy-start(bf16[2,128,4,128]{3,2,1,0:T(4,128)(2,1)} %param.25) | copy-start | bytes 786436
  194.6 5.7 %copy-start.2 = (bf16[2,128,128]{2,1,0:T(8,128)(2,1)S(1)}, bf16[2,128,128]{2,1,0:T(8,128)(2,1)}, u32[]{:S(2)}) copy-start(bf16[2,128,128]{2,1,0:T(8,128)(2,1)} %param.27) | copy-start | bytes 196612
  194.6 9.4 %copy-start.3 = (bf16[2,128,128]{2,1,0:T(8,128)(2,1)S(1)}, bf16[2,128,128]{2,1,0:T(8,128)(2,1)}, u32[]{:S(2)}) copy-start(bf16[2,128,128]{2,1,0:T(8,128)(2,1)} %param.30) | copy-start | bytes 196612
  194.6 62.3 %all-to-all-start.1 = ((f32[32,4,16,512]{3,2,1,0:T(8,128)}), f32[32,4,16,512]{3,2,1,0:T(8,128)}, u32[]{:S(2)}, u32[]{:S(2)}) async-start(f32[32,4,16,512]{3,2,1,0:T(8,128)} %tri_product.2), calls=%async_computation.1 | async-start | bytes 8388608 | tf_op jit(solution)/shard_map/all_to_all | solution.py:591
  336.0 62.3 %all-to-all-start.3 = ((f32[32,4,16,512]{3,2,1,0:T(8,128)}), f32[32,4,16,512]{3,2,1,0:T(8,128)}, u32[]{:S(2)}, u32[]{:S(2)}) async-start(f32[32,4,16,512]{3,2,1,0:T(8,128)} %tri_product.3), calls=%async_computation.3 | async-start | bytes 8388608 | tf_op jit(solution)/shard_map/all_to_all | solution.py:591
